TPU v7x, 32 devices: a whole 2x2x4 slice. The times are simulated.
32 devices in a mesh: dp: 4 (over y, x), mp: 8 (over z, core).
Axes of the slice: x: 2, y: 2, z: 4, core: 2. Of those that a mesh axis runs over, the one named last changes fastest.
Arguments:
- data_rows: bfloat16 [16384, 2048], P(('dp', 'mp')), may hold values from -32 to 32
- centroids: bfloat16 [12288, 2048], P('mp'), may hold values from -0.75 to 0.75
- block_mask: int32 [8, 128], P(None, ('dp', 'mp')), may hold values from 0 to 1, as said below
- lower_bound: float32 [8, 16384], P(None, ('dp', 'mp')), may hold values from 0 to 4
Outputs:
- new_centroids: float32 [12288, 2048], P(('mp', 'dp'))
- centroid_shift: float32 [12288], P(('mp', 'dp'))
- log_norm: float32 [16384], P(('dp', 'mp'))
- new_lower: float32 [8, 16384], P(None, ('dp', 'mp'))
Inputs may be any that keep to these rules, and one draw needn't show every extreme that they name: `block_mask`: within the 4 blocks of one device (aligned runs along the last dimension), at most 1 are 1 for each shard; for some shard every device has exactly 1.
All inputs are finite; a program needn't handle non-finite values.
Results may differ from a plain program's by a relative error of at most 0.0011.
Values may be sent and summed in bfloat16 or wider, within the bound.
No kernel may reach another device: no remote copies, remote signals or barrier semaphores. Data moves between devices by JAX's collectives and lax.ppermute only.
A program may use at most 128 MiB of HBM per device.

v0:
```python
import math

import jax
import jax.numpy as jnp
from jax import lax
from jax.experimental import pallas as pl
from jax.experimental.pallas import tpu as pltpu
from jax.sharding import PartitionSpec as P


BLOCK = 128
LANES = 128
F32 = jnp.float32
BF16 = jnp.bfloat16
NEVER = 1e30
ANY = pl.BlockSpec(memory_space=pl.ANY)
SMEM = pl.BlockSpec(memory_space=pltpu.SMEM)
VMEM = pl.BlockSpec(memory_space=pltpu.VMEM)


def hbm(*arrays):
    return [pltpu.with_memory_space_constraint(v, pltpu.HBM) for v in arrays]


def vmem(*arrays):
    return [pltpu.with_memory_space_constraint(v, pltpu.VMEM) for v in arrays]


def swap(value, axis, size, offset):
    return lax.ppermute(value, axis, [(i, i ^ offset) for i in range(size)])


def call(body, out_shape, in_specs, out_specs, scratch=(), vmem=4):
    return pl.pallas_call(
        body,
        out_shape=out_shape,
        in_specs=in_specs,
        out_specs=out_specs,
        scratch_shapes=list(scratch),
        compiler_params=pltpu.CompilerParams(vmem_limit_bytes=vmem << 20),
    )


def take_slots(ids, mask_t, data_rows, pieces, with_codes):
    block_count, n_mp = mask_t.shape

    def body(ids_ref, mask_ref, rows_ref, *refs):
        outs, sems = refs[:-1], refs[-1]

        def code_of(k):
            shard = ids_ref[0] ^ k
            code = mask_ref[0, shard]
            for b in range(1, block_count):
                code = code + (b + 1) * mask_ref[b, shard]
            return code

        copies = []
        for i, (k, first, count) in enumerate(pieces):
            start = jnp.maximum(code_of(k) - 1, 0) * BLOCK
            src = rows_ref.at[pl.ds(pl.multiple_of(start, BLOCK), BLOCK), pl.ds(first, count)]
            copies.append(pltpu.make_async_copy(src, outs[i], sems.at[i]))
            copies[-1].start()
        if with_codes:
            for k in range(n_mp):
                outs[-1][k : k + 1, :] = jnp.full((1, LANES), code_of(k), jnp.int32).astype(F32)
        for copy in copies:
            copy.wait()

    shapes = [pltpu.VMEM((BLOCK, count), data_rows.dtype) for _, _, count in pieces]
    if with_codes:
        shapes.append(jax.ShapeDtypeStruct((n_mp, LANES), F32))
    return call(
        body, shapes, [SMEM, SMEM, ANY], [VMEM] * len(shapes), [pltpu.SemaphoreType.DMA((len(pieces),))], 8
    )(ids, mask_t, *hbm(data_rows))


def load_centroids(centroids, n_parts):
    width, feat = centroids.shape
    part = width // n_parts

    def body(in_ref, out_ref, norm_ref):
        values = in_ref[...]
        out_ref[...] = values
        norm_ref[...] = jnp.sum(jnp.square(values.astype(F32)), axis=1, keepdims=True)

    return pl.pallas_call(
        body,
        out_shape=[pltpu.VMEM((width, feat), centroids.dtype), jax.ShapeDtypeStruct((width, 1), F32)],
        grid=(n_parts,),
        in_specs=[pl.BlockSpec((part, feat), lambda i: (i, 0))],
        out_specs=[pl.BlockSpec((part, feat), lambda i: (i, 0)), pl.BlockSpec((part, 1), lambda i: (i, 0))],
        name="load_centroids",
        compiler_params=pltpu.CompilerParams(vmem_limit_bytes=10 << 20),
    )(*hbm(centroids))


def product(cents_ref, rows_ref):
    return lax.dot_general(
        cents_ref[...], rows_ref[...], (((1,), (1,)), ((), ())), preferred_element_type=F32
    )


def keep(row_refs, pieces, out_ref):
    for ref, (place, first, count) in zip(row_refs, pieces):
        out_ref[place * BLOCK : (place + 1) * BLOCK, first : first + count] = ref[...]


def own_scores(ids, centroids, cent_norm, rows, pieces, state, at, n_slots, n_parts, sharpness):
    width, feat = centroids.shape
    part = width // n_parts
    n_rows = n_slots * BLOCK
    fresh = isinstance(state[0], jax.ShapeDtypeStruct)
    n_in = len(rows)

    def body(ids_ref, cents_ref, norm_ref, *refs):
        row_refs = refs[:n_in]
        rows_out, score_out, lse_out, top_ref, mass_ref = refs[len(refs) - 5 :]
        step = pl.program_id(0)

        @pl.when(step == 0)
        def _():
            keep(row_refs, pieces, rows_out)
            top_ref[...] = jnp.full(top_ref.shape, -NEVER, F32)
            mass_ref[...] = jnp.zeros(mass_ref.shape, F32)

        score = sharpness * (2.0 * product(cents_ref, rows_out) - norm_ref[...])

        @pl.when(step == ids_ref[1])
        def _():
            score_out[...] = score

        old_top = top_ref[...]
        top = jnp.maximum(old_top, jnp.max(score, axis=0, keepdims=True))
        mass = mass_ref[...] * jnp.exp(old_top - top) + jnp.sum(jnp.exp(score - top), axis=0, keepdims=True)
        top_ref[...] = top
        mass_ref[...] = mass
        lse = top + jnp.log(mass)
        for i in range(n_slots):
            lse_out[i] = lse[:, i * BLOCK : (i + 1) * BLOCK]

    grid_spec = pltpu.PrefetchScalarGridSpec(
        num_scalar_prefetch=1,
        grid=(n_parts,),
        in_specs=[
            pl.BlockSpec((part, feat), lambda i, ids: (i, 0)),
            pl.BlockSpec((part, 1), lambda i, ids: (i, 0)),
        ]
        + [pl.BlockSpec(r.shape, lambda i, ids: (0, 0)) for r in rows]
        + ([] if fresh else [ANY] * 3),
        out_specs=[
            pl.BlockSpec((n_rows, feat), lambda i, ids: (at, 0)),
            pl.BlockSpec((part, n_rows), lambda i, ids: (0, at)),
            pl.BlockSpec((n_slots, 1, BLOCK), lambda i, ids: (at, 0, 0)),
        ],
        scratch_shapes=[pltpu.VMEM((1, n_rows), F32)] * 2,
    )
    return pl.pallas_call(
        body,
        out_shape=[pltpu.VMEM(v.shape, v.dtype) for v in state],
        grid_spec=grid_spec,
        input_output_aliases={} if fresh else {3 + n_in + i: i for i in range(3)},
        name="own_scores",
        compiler_params=pltpu.CompilerParams(vmem_limit_bytes=10 << 20),
    )(ids, *vmem(centroids), cent_norm, *rows, *([] if fresh else state))


def side_scores(ids, centroids, cent_norm, sides, pieces, state, at, n_slots, half, sharpness):
    feat = centroids.shape[1]
    n_rows = n_slots * BLOCK
    fresh = isinstance(state[0], jax.ShapeDtypeStruct)
    n_in = len(sides[0])

    def body(ids_ref, cents_ref, norm_ref, *refs):
        x_refs, y_refs = refs[:n_in], refs[n_in : 2 * n_in]
        x_rows, y_rows, x_out, y_out = refs[len(refs) - 4 :]
        step = pl.program_id(0)

        def score(rows_ref):
            return sharpness * (2.0 * product(cents_ref, rows_ref) - norm_ref[...])

        @pl.when(step == 0)
        def _():
            keep(x_refs, pieces, x_rows)
            keep(y_refs, pieces, y_rows)

        @pl.when(step != 3)
        def _():
            x_out[...] = score(x_rows)

        @pl.when(step != 2)
        def _():
            y_out[...] = score(y_rows)

    def block(i, ids):
        mine = ids[1]
        other = jnp.where(i == 2, 2 * (mine ^ 2) + 1, 2 * (mine ^ 1))
        return (jnp.where(i < 2, 2 * mine + i, other), 0)

    grid_spec = pltpu.PrefetchScalarGridSpec(
        num_scalar_prefetch=1,
        grid=(4,),
        in_specs=[pl.BlockSpec((half, feat), block), pl.BlockSpec((half, 1), block)]
        + [pl.BlockSpec(r.shape, lambda i, ids: (0, 0)) for r in sides[0] + sides[1]]
        + ([] if fresh else [ANY] * 4),
        out_specs=[
            pl.BlockSpec((n_rows, feat), lambda i, ids: (at, 0)),
            pl.BlockSpec((n_rows, feat), lambda i, ids: (at, 0)),
            pl.BlockSpec((half, n_rows), lambda i, ids: (jnp.minimum(i, 2), at)),
            pl.BlockSpec((half, n_rows), lambda i, ids: (jnp.where(i == 3, 2, jnp.minimum(i, 1)), at)),
        ],
    )
    return pl.pallas_call(
        body,
        out_shape=[pltpu.VMEM(v.shape, v.dtype) for v in state],
        grid_spec=grid_spec,
        input_output_aliases={} if fresh else {3 + 2 * n_in + i: i for i in range(4)},
        name="side_scores",
        compiler_params=pltpu.CompilerParams(vmem_limit_bytes=12 << 20),
    )(ids, *vmem(centroids), cent_norm, *sides[0], *sides[1], *([] if fresh else state))


def log_total(kept):
    peak = jnp.maximum(jnp.max(kept, axis=0, keepdims=True), 0.0)
    mass = jnp.sum(jnp.exp(kept - peak), axis=0, keepdims=True)
    return peak + jnp.log(jnp.exp(-peak) + mass)


def combine(notes, block_count):
    n_mp = len(notes)

    def body(*refs):
        note_refs, (slot_ref, row_ref) = refs[:n_mp], refs[n_mp:]
        for k in range(n_mp):
            lse = jnp.concatenate([note_refs[k ^ j][j : j + 1, :] for j in range(n_mp)], axis=0)
            code = note_refs[k][n_mp : 2 * n_mp, :]
            mine = code[k : k + 1, :]
            total = log_total(jnp.where((code == mine) & (code > 0.0), lse, -NEVER))
            slot_ref[k : k + 1, :] = jnp.where(mine > 0.0, total, NEVER)
            if k == 0:
                for b in range(block_count):
                    row_ref[b : b + 1, :] = log_total(jnp.where(code == float(b + 1), lse, -NEVER))

    return call(
        body,
        [jax.ShapeDtypeStruct((n_mp, LANES), F32), jax.ShapeDtypeStruct((block_count, LANES), F32)],
        [VMEM] * n_mp,
        [VMEM, VMEM],
    )(*notes)


def weights_of(score_ref, norm_ref, into, column, total):
    for k in range(norm_ref.shape[0]):
        tile = jnp.exp(score_ref[:, k * BLOCK : (k + 1) * BLOCK] - norm_ref[k : k + 1, :])
        total = tile if total is None else total + tile
        into[:, column + k * BLOCK : column + (k + 1) * BLOCK] = tile.astype(BF16)
    return total


def sent_sums(side_rows, side_score, norms, half, first, columns, tile):
    n_rows = side_rows[0].shape[0]
    steps = columns // tile

    def body(x_ref, y_ref, xs_ref, ys_ref, xn_ref, yn_ref, x_out, y_out, w_buf, c_buf):
        step = pl.program_id(0)

        @pl.when(step == 0)
        def _():
            for i, (s_ref, n_ref) in enumerate(((xs_ref, xn_ref), (ys_ref, yn_ref))):
                total = weights_of(s_ref, n_ref, w_buf.at[i], 0, None)
                c_buf[i] = jnp.broadcast_to(jnp.sum(total, axis=1, keepdims=True), c_buf.shape[1:])

        for i, (r_ref, out) in enumerate(((x_ref, x_out), (y_ref, y_out))):
            counts = c_buf[i]

            @pl.when(step < steps)
            def _():
                part = jnp.dot(w_buf[i], r_ref[...], preferred_element_type=F32)
                out[...] = part * (2.0**10 / jnp.maximum(counts[:, 0:1], 2.0**-20))

            @pl.when(step == steps)
            def _():
                hi = counts.astype(BF16).astype(F32)
                mid = (counts - hi).astype(BF16).astype(F32)
                low = (counts - hi - mid).astype(BF16).astype(F32)
                lane = lax.broadcasted_iota(jnp.int32, counts.shape, 1)
                terms = jnp.where(lane == 0, hi, jnp.where(lane == 1, mid, jnp.where(lane == 2, low, 0.0)))
                out[:, :LANES] = terms

    base = first // tile
    rows_spec = pl.BlockSpec((n_rows, tile), lambda i: (0, base + jnp.minimum(i, steps - 1)))
    score_spec = pl.BlockSpec((half, n_rows), lambda i: (2, 0))
    norm_spec = pl.BlockSpec(norms[0].shape, lambda i: (0, 0))
    out_spec = pl.BlockSpec((half, tile), lambda i: (0, i))
    with_counts = first == 0
    width = columns + LANES if with_counts else columns
    return pl.pallas_call(
        body,
        out_shape=[jax.ShapeDtypeStruct((half, width), F32)] * 2,
        grid=(steps + 1 if with_counts else steps,),
        in_specs=[rows_spec] * 2 + [score_spec] * 2 + [norm_spec] * 2,
        out_specs=[out_spec] * 2,
        scratch_shapes=[pltpu.VMEM((2, half, n_rows), BF16), pltpu.VMEM((2, half, LANES), F32)],
        name="sent_sums",
        compiler_params=pltpu.CompilerParams(vmem_limit_bytes=16 << 20),
    )(*vmem(*side_rows, *side_score), *norms)


def own_sums(rows, scores, norms, width, tile):
    n_rows, feat = rows[0].shape

    def body(a_ref, b_ref, c_ref, as_ref, bs_ref, cs_ref, an_ref, bn_ref, cn_ref, out_ref, count_ref, w_buf):
        @pl.when(pl.program_id(0) == 0)
        def _():
            total = None
            for i, (s_ref, n_ref) in enumerate(((as_ref, an_ref), (bs_ref, bn_ref), (cs_ref, cn_ref))):
                total = weights_of(s_ref, n_ref, w_buf, i * n_rows, total)
            count_ref[...] = jnp.sum(total, axis=1, keepdims=True)

        acc = jnp.dot(w_buf[:, :n_rows], a_ref[...], preferred_element_type=F32)
        acc += jnp.dot(w_buf[:, n_rows : 2 * n_rows], b_ref[...], preferred_element_type=F32)
        acc += jnp.dot(w_buf[:, 2 * n_rows :], c_ref[...], preferred_element_type=F32)
        out_ref[...] = acc

    return pl.pallas_call(
        body,
        out_shape=[pltpu.VMEM((width, feat), F32), jax.ShapeDtypeStruct((width, 1), F32)],
        grid=(feat // tile,),
        in_specs=[pl.BlockSpec((n_rows, tile), lambda i: (0, i))] * 3
        + [pl.BlockSpec((width, n_rows), lambda i: (0, 0))] * 3
        + [pl.BlockSpec(norms[0].shape, lambda i: (0, 0))] * 3,
        out_specs=[
            pl.BlockSpec((width, tile), lambda i: (0, i)),
            pl.BlockSpec((width, 1), lambda i: (0, 0)),
        ],
        scratch_shapes=[pltpu.VMEM((width, 3 * n_rows), BF16)],
        name="own_sums",
        compiler_params=pltpu.CompilerParams(vmem_limit_bytes=24 << 20),
    )(*vmem(*rows, *scores), *norms)


def update(ids, own, counts, parts, centroids, first, state, n_devices):
    width, feat = own.shape
    half = width // 2
    columns = feat // 2
    lead = first == 0
    rows = half // 2
    steps = half // rows

    def body(ids_ref, own_ref, count_ref, a_ref, b_ref, old_ref, *refs):
        step = pl.program_id(0)

        def finish(part_ref):
            if lead:
                new_ref, sent_ref, square_ref = refs
                tail = part_ref[:, columns:]
                lane = lax.broadcasted_iota(jnp.int32, tail.shape, 1)
                sent = jnp.sum(jnp.where(lane < 3, tail, 0.0), axis=1, keepdims=True)
                sent_ref[...] = sent
            else:
                sent_in, square_in, _, new_ref, move_ref, peak_ref = refs
                sent = sent_in[...]
            back = part_ref[:, :columns] * (jnp.maximum(sent, 2.0**-20) * 2.0**-10)
            before = old_ref[...].astype(F32)
            after = (own_ref[...] + back + before) / (count_ref[...] + sent + 1.0)
            new_ref[...] = after
            square = jnp.sum(jnp.square(after - before), axis=1, keepdims=True)
            if lead:
                square_ref[...] = square
            else:
                move = jnp.sqrt(square + square_in[...] + 1.0)
                move_ref[...] = move
                top = jnp.broadcast_to(jnp.max(move, axis=0, keepdims=True), peak_ref.shape)
                peak_ref[...] = jnp.where(step == 0, top, jnp.maximum(top, peak_ref[...]))

        @pl.when(step < steps)
        def _():
            finish(a_ref)

        @pl.when(step >= steps)
        def _():
            finish(b_ref)

    at = 0 if lead else 1
    column = pl.BlockSpec((rows, 1), lambda i, ids: (i, 0))
    part_width = parts[0].shape[1]
    in_specs = [
        pl.BlockSpec((rows, columns), lambda i, ids: (i, at)),
        column,
        pl.BlockSpec((rows, part_width), lambda i, ids: (jnp.minimum(i, steps - 1), 0)),
        pl.BlockSpec((rows, part_width), lambda i, ids: (jnp.maximum(i - steps, 0), 0)),
        pl.BlockSpec((rows, columns), lambda i, ids: (ids[1] * (2 * steps) + i, at)),
    ]
    new_spec = pl.BlockSpec((rows, columns), lambda i, ids: (i, at))
    new_shape = jax.ShapeDtypeStruct((width, feat), F32)
    thin = jax.ShapeDtypeStruct((width, 1), F32)
    if lead:
        out_shape, out_specs, extra, aliases = [new_shape, thin, thin], [new_spec, column, column], [], {}
    else:
        new, sent, square = state
        extra = [sent, square, new]
        in_specs += [column, column, ANY]
        out_shape = [new_shape, thin, jax.ShapeDtypeStruct((n_devices, LANES), F32)]
        out_specs = [new_spec, column, pl.BlockSpec((n_devices, LANES), lambda i, ids: (0, 0))]
        aliases = {8: 0}
    return pl.pallas_call(
        body,
        out_shape=out_shape,
        grid_spec=pltpu.PrefetchScalarGridSpec(
            num_scalar_prefetch=1, grid=(2 * steps,), in_specs=in_specs, out_specs=out_specs
        ),
        input_output_aliases=aliases,
        name="update",
        compiler_params=pltpu.CompilerParams(vmem_limit_bytes=8 << 20),
    )(ids, *vmem(own), counts, *parts, *vmem(centroids), *extra)


def z_order(n_mp):
    half = n_mp // 2
    return [half] + [k for k in range(2, n_mp) if k != half]


def own_groups(n_mp):
    return [(k, k + 1) for k in range(0, n_mp, 2)]


def on_square(data_rows, centroids, block_mask, lower_bound):
    feat = data_rows.shape[1]
    width = centroids.shape[0]
    block_count = data_rows.shape[0] // BLOCK
    n_mp = lax.axis_size("mp")
    n_dp = lax.axis_size("dp")
    own_width = width // n_dp
    half = own_width // 2
    my_mp = lax.axis_index("mp").astype(jnp.int32)
    my_dp = lax.axis_index("dp").astype(jnp.int32)
    sharpness = 4.0 / math.sqrt(feat)
    ids = jnp.stack([my_mp, my_dp])
    mask_t = block_mask.T

    last = n_mp - 1
    cuts = {k: [(k, 0, feat)] for k in range(n_mp)}
    cuts[last] = [(last, 0, feat // 2), (last, feat // 2, feat // 2)]
    early = [p for k in z_order(n_mp)[:3] for p in cuts[k]]
    late = cuts[0] + [p for k in z_order(n_mp)[3:] for p in cuts[k]] + cuts[1]
    got = dict(zip(early, take_slots(ids, mask_t, data_rows, early, False)))
    *rest, codes = take_slots(ids, mask_t, data_rows, late, True)
    got.update(zip(late, rest))
    for piece in early + late[1:]:
        got[piece] = swap(got[piece], "mp", n_mp, piece[0])

    side = {}
    for k in range(n_mp):
        for piece in cuts[k]:
            for bit in (1, 2):
                side[bit, piece] = swap(got[piece], "dp", n_dp, bit)

    cents, cent_norm = load_centroids(centroids, 2 * n_dp)

    n_rows = n_mp * BLOCK
    own = [
        jax.ShapeDtypeStruct((n_rows, feat), BF16),
        jax.ShapeDtypeStruct((own_width, n_rows), F32),
        jax.ShapeDtypeStruct((n_mp, 1, BLOCK), F32),
    ]
    sides = [jax.ShapeDtypeStruct((n_rows, feat), BF16)] * 2
    sides += [jax.ShapeDtypeStruct((3 * half, n_rows), F32)] * 2
    for group in own_groups(n_mp):
        held = [p for k in group for p in cuts[k]]
        placed = [(p[0] - group[0], p[1], p[2]) for p in held]
        own = own_scores(
            ids, cents, cent_norm, [got[p] for p in held], placed, own, group[0] // len(group), len(group),
            n_dp, sharpness,
        )
    for i in range(n_mp // 2):
        held = cuts[2 * i] + cuts[2 * i + 1]
        placed = [(p[0] - 2 * i, p[1], p[2]) for p in held]
        pair = [[side[bit, p] for p in held] for bit in (1, 2)]
        sides = side_scores(ids, cents, cent_norm, pair, placed, sides, i, 2, half, sharpness)

    note = jnp.concatenate([own[2][:, 0, :], codes])
    notes = [note]
    for k in range(1, n_mp):
        notes.append(swap(note, "mp", n_mp, k))
    slot_norm, row_norm = combine(notes, block_count)
    log_norm = row_norm.reshape(-1)
    side_norm = []
    for bit in (1, 2):
        side_norm.append(swap(slot_norm, "dp", n_dp, bit))

    received = []
    for part in range(2):
        first = part * (feat // 2)
        sent = sent_sums(sides[:2], sides[2:], side_norm, half, first, feat // 2, feat // 4)
        for_y, for_x = [v.astype(jnp.float16) for v in sent]
        received.append([swap(for_x, "dp", n_dp, 1), swap(for_y, "dp", n_dp, 2)])
    total, counts = own_sums(
        [own[0], sides[0], sides[1]],
        [own[1], sides[2], sides[3]],
        [slot_norm] + side_norm,
        own_width,
        feat // 4,
    )
    state = None
    for part in range(2):
        parts = [v.astype(F32) for v in received[part]]
        state = update(ids, total, counts, parts, cents, part * (feat // 2), state, n_dp * n_mp)
    updated, movement, peak = state
    shard_peaks = lax.all_to_all(peak, ("dp", "mp"), split_axis=0, concat_axis=0, tiled=True)
    shard_peak = jnp.max(shard_peaks.reshape(n_dp, n_mp, LANES), axis=(0, 2))
    new_lower = lower_bound - shard_peak[:, None]
    return (updated, movement[:, 0], log_norm, new_lower)


def on_device(data_rows, centroids, block_mask, lower_bound):
    feat = data_rows.shape[1]
    width = centroids.shape[0]
    block_count = data_rows.shape[0] // BLOCK
    n_mp = lax.axis_size("mp")
    n_dp = lax.axis_size("dp")
    own_width = width // n_dp
    my_mp = lax.axis_index("mp")
    my_dp = lax.axis_index("dp")
    sharpness = 4.0 / math.sqrt(feat)

    labels = jnp.arange(1, block_count + 1, dtype=jnp.int32)
    codes = jnp.sum(block_mask * labels[None, :], axis=1)

    def outgoing(k):
        code = lax.dynamic_index_in_dim(codes, my_mp ^ k, 0, keepdims=False)
        start = jnp.maximum(code - 1, 0) * BLOCK
        return lax.dynamic_slice(data_rows, (start, 0), (BLOCK, feat))

    order = list(range(2, n_mp)) + [1]
    got = {0: outgoing(0)}
    for k in order:
        got[k] = swap(outgoing(k), "mp", n_mp, k)

    cent_norm = jnp.sum(jnp.square(centroids.astype(jnp.float32)), axis=1)

    scores, lses = {}, {}
    groups = [(k, k + 1) for k in range(0, n_mp, 2)]
    for group in groups:
        rows = jnp.concatenate([got[k] for k in group], axis=0)
        product = lax.dot_general(
            centroids, rows, (((1,), (1,)), ((), ())), preferred_element_type=jnp.float32
        )
        score = sharpness * (2.0 * product - cent_norm[:, None])
        top = jnp.max(score, axis=0)
        lse = top + jnp.log(jnp.sum(jnp.exp(score - top[None, :]), axis=0))
        scores[group] = score
        for i, k in enumerate(group):
            lses[k] = lse[i * BLOCK : (i + 1) * BLOCK]

    note = jnp.concatenate(
        [
            jnp.stack([lses[k] for k in range(n_mp)]),
            jnp.pad(codes.astype(jnp.float32), (0, BLOCK - n_mp))[None, :],
        ]
    )
    notes = lax.all_to_all(
        jnp.broadcast_to(note[None], (n_mp,) + note.shape), "mp", split_axis=0, concat_axis=0, tiled=True
    )
    shard_ids = jnp.arange(n_mp, dtype=jnp.int32)
    lse_of = notes[:, :n_mp, :]
    all_code = notes[:, n_mp, :n_mp].astype(jnp.int32)
    all_lse = lse_of[shard_ids[None, :], shard_ids[None, :] ^ shard_ids[:, None]]
    tops = jnp.where((all_code > 0)[:, :, None], all_lse, -1e30)

    def normalizer(same, lse):
        kept = jnp.where(same[:, :, None], lse, -1e30)
        peak = jnp.maximum(jnp.max(kept, axis=1), 0.0)
        mass = jnp.sum(jnp.exp(kept - peak[:, None, :]), axis=1)
        return peak + jnp.log(jnp.exp(-peak) + mass)

    my_lse = lax.dynamic_index_in_dim(tops, my_mp, 0, keepdims=False)
    row_norm = normalizer(codes[None, :] == labels[:, None], jnp.broadcast_to(my_lse[None], (block_count,) + my_lse.shape))
    log_norm = row_norm.reshape(-1)

    slot_code = lax.dynamic_index_in_dim(all_code, my_mp, 1, keepdims=False)
    slot_norm = normalizer((all_code == slot_code[:, None]) & (all_code > 0), tops)

    weights, counts = [], 0.0
    for group in groups:
        src = [my_mp ^ k for k in group]
        norm = jnp.concatenate([slot_norm[m] for m in src])
        valid = jnp.concatenate([jnp.broadcast_to(slot_code[m] > 0, (BLOCK,)) for m in src])
        weight = jnp.where(valid[None, :], jnp.exp(scores[group] - norm[None, :]), 0.0)
        counts = counts + jnp.sum(weight, axis=1)
        weights.append(weight.astype(jnp.bfloat16))
    weight_half = jnp.concatenate(weights, axis=1)
    rows = jnp.concatenate([got[k] for k in range(n_mp)], axis=0)

    def quarter(j):
        return (my_dp ^ j) * own_width

    def partial(j, half):
        w = lax.dynamic_slice(weight_half, (quarter(j), 0), (own_width, weight_half.shape[1]))
        x = lax.slice_in_dim(rows, half * (feat // 2), (half + 1) * (feat // 2), axis=1)
        return lax.dot_general(w, x, (((1,), (0,)), ((), ())), preferred_element_type=jnp.float32)

    count_of = {0: counts}
    for j in range(1, n_dp):
        count_of[j] = swap(counts, "dp", n_dp, j)

    def sub(vec, j):
        return lax.dynamic_slice(vec, (quarter(j),), (own_width,))

    def scale(members, j):
        total = sum(sub(count_of[i], j) for i in members)
        return jnp.maximum(total, 2.0**-20)[:, None] * 2.0**-10

    bits = [1 << b for b in range(n_dp.bit_length() - 1)]
    plan = [bits, bits[::-1]]
    current = [{}, {}]
    for j in reversed(range(n_dp)):
        for half in range(2):
            jj = j if half == 0 or n_dp != 4 else {3: 3, 1: 2, 2: 1, 0: 0}[j]
            current[half][jj] = None
    todo = [[j for j in reversed(range(n_dp))] for _ in range(2)]
    for half in range(2):
        for j in todo[half]:
            current[half][j] = partial(j, half)
    members = [{0}, {0}]
    for step in range(len(bits)):
        for half in range(2):
            bit = plan[half][step]
            cur = current[half]
            mine = members[half]
            theirs = {i ^ bit for i in mine}
            kept = {}
            for j in sorted(cur, reverse=True):
                if not j & bit:
                    continue
                sent = (cur[j] / scale(mine, j)).astype(jnp.float16)
                back = swap(sent, "dp", n_dp, bit)
                kept[j ^ bit] = cur[j ^ bit] + back.astype(jnp.float32) * scale(theirs, j ^ bit)
            current[half] = kept
            members[half] = mine | theirs
    part_sums = jnp.concatenate([current[0][0], current[1][0]], axis=1)
    part_counts = sum(sub(count_of[j], 0) for j in range(n_dp))

    old_cents = lax.dynamic_slice_in_dim(centroids, my_dp * own_width, own_width, 0).astype(jnp.float32)
    updated = (part_sums + old_cents) / (part_counts[:, None] + 1.0)
    movement = jnp.sqrt(jnp.sum(jnp.square(updated - old_cents), axis=1) + 1.0)
    peak = jnp.broadcast_to(jnp.max(movement), (n_dp * n_mp, 1))
    shard_peaks = lax.all_to_all(peak, ("dp", "mp"), split_axis=0, concat_axis=0, tiled=True)
    shard_peak = jnp.max(shard_peaks.reshape(n_dp, n_mp), axis=0)
    new_lower = lower_bound - shard_peak[:, None]
    return (updated, movement, log_norm, new_lower)


def solution(mesh):
    placed = (P(("dp", "mp"), None), P("mp", None), P(None, ("dp", "mp")), P(None, ("dp", "mp")))
    square = mesh.shape["dp"] == 4

    def body(*args):
        return on_square(*args) if square else on_device(*args)

    return jax.shard_map(
        body,
        mesh=mesh,
        in_specs=placed,
        out_specs=(P(("mp", "dp"), None), P(("mp", "dp")), P(("dp", "mp")), P(None, ("dp", "mp"))),
        check_vma=False,
    )
```

profile of v0, /device:TPU:0, one launch (start us, length us, event | category | flops | bytes accessed | tf_op | source)
XLA Modules:
  0.0 257.7 jit_solution(9586388203879280071)
XLA Ops:
  1.4 2.4 shard_map.75
  4.3 2.0 shard_map.76
  6.4 3.2 %collective-permute-start.5 = (bf16[128,2048]{1,0:T(8,128)(2,1)S(1)}, bf16[128,2048]{1,0:T(8,128)(2,1)S(1)}, u32[]{:S(2)}, u32[]{:S(2)}) collective-permute-start(bf16[128,2048]{1,0:T(8,128)(2,1)S(1)} %get-tuple-element.65), channel_id=1, source_target_pairs={{0,2},{1,3},{2,0},{3,1},{4,6},{5,7},{6,4},{7,5},{8,10},{9,11},{10,... | collective-permute-start | bytes 1572872 | tf_op jit(solution)/shard_map/ppermute | solution.py:30
  9.5 3.4 %collective-permute-start.1 = (bf16[128,1024]{1,0:T(8,128)(2,1)S(1)}, bf16[128,1024]{1,0:T(8,128)(2,1)S(1)}, u32[]{:S(2)}, u32[]{:S(2)}) collective-permute-start(bf16[128,1024]{1,0:T(8,128)(2,1)S(1)} %get-tuple-element.61), channel_id=1, source_target_pairs={{0,7},{1,6},{2,5},{3,4},{4,3},{5,2},{6,1},{7,0},{8,15},{9,14},{10,... | collective-permute-start | bytes 786440 | tf_op jit(solution)/shard_map/ppermute | solution.py:30
  13.1 27.1 %collective-permute-done.1.refs_1_ = bf16[128,1024]{1,0:T(8,128)(2,1)S(1)} collective-permute-done((bf16[128,1024]{1,0:T(8,128)(2,1)S(1)}, bf16[128,1024]{1,0:T(8,128)(2,1)S(1)}, u32[]{:S(2)}, u32[]{:S(2)}) %collective-permute-start.1) | collective-permute-done | bytes 262176 | tf_op jit(solution)/shard_map/ppermute | solution.py:30
  40.2 5.7 %collective-permute-done.2.refs_2_ = bf16[128,1024]{1,0:T(8,128)(2,1)S(1)} collective-permute-done((bf16[128,1024]{1,0:T(8,128)(2,1)S(1)}, bf16[128,1024]{1,0:T(8,128)(2,1)S(1)}, u32[]{:S(2)}, u32[]{:S(2)}) %collective-permute-start.2) | collective-permute-done | bytes 262176 | tf_op jit(solution)/shard_map/ppermute | solution.py:30
  50.4 40.9 %collective-permute-done.4.refs_1_ = bf16[128,2048]{1,0:T(8,128)(2,1)S(1)} collective-permute-done((bf16[128,2048]{1,0:T(8,128)(2,1)S(1)}, bf16[128,2048]{1,0:T(8,128)(2,1)S(1)}, u32[]{:S(2)}, u32[]{:S(2)}) %collective-permute-start.4) | collective-permute-done | bytes 524320 | tf_op jit(solution)/shard_map/ppermute | solution.py:30
  92.8 9.9 %collective-permute-done.3.refs_0_ = bf16[128,2048]{1,0:T(8,128)(2,1)S(1)} collective-permute-done((bf16[128,2048]{1,0:T(8,128)(2,1)S(1)}, bf16[128,2048]{1,0:T(8,128)(2,1)S(1)}, u32[]{:S(2)}, u32[]{:S(2)}) %collective-permute-start.3) | collective-permute-done | bytes 524320 | tf_op jit(solution)/shard_map/ppermute | solution.py:30
  108.2 6.0 %load_centroids.1 = (bf16[1536,2048]{1,0:T(8,128)(2,1)S(1)}, f32[1536,1]{1,0:T(8,128)S(1)}) custom-call(bf16[1536,2048]{1,0:T(8,128)(2,1)} %in_ref.1), custom_call_target="tpu_custom_call" | custom-call | tf_op jit(solution)/shard_map/load_centroids/pallas_call | solution.py:86
  114.2 3.7 %own_scores.4 = (bf16[1024,2048]{1,0:T(8,128)(2,1)S(1)}, f32[384,1024]{1,0:T(8,128)S(1)}, f32[8,1,128]{2,1,0:T(1,128)S(1)}) custom-call(s32[2]{0:T(128)S(1)} %pad_add_fusion.ids_ref, bf16[1536,2048]{1,0:T(8,128)(2,1)S(1)} %get-tuple-element.58.cents_ref.old_ref, f32[1536,1]{1,0:T(8,128)S(1)} %get-tuple-element.59.norm_ref, ...), custom_call_target="tpu_custom_call" | custom-call | tf_op jit(solution)/shard_map/own_scores/pallas_call | solution.py:157
  117.9 3.7 %own_scores.5 = (bf16[1024,2048]{1,0:T(8,128)(2,1)S(1)}, f32[384,1024]{1,0:T(8,128)S(1)}, f32[8,1,128]{2,1,0:T(1,128)S(1)}) custom-call(s32[2]{0:T(128)S(1)} %pad_add_fusion.ids_ref, bf16[1536,2048]{1,0:T(8,128)(2,1)S(1)} %get-tuple-element.58.cents_ref.old_ref, ...), custom_call_target="tpu_custom_call", output_to_operand_aliasing={{0}: (5, {}), {1}: (6, {}), {2}: (7, {})} | custom-call | tf_op jit(solution)/shard_map/own_scores/pallas_call | solution.py:157
  121.6 3.7 %own_scores.6 = (bf16[1024,2048]{1,0:T(8,128)(2,1)S(1)}, f32[384,1024]{1,0:T(8,128)S(1)}, f32[8,1,128]{2,1,0:T(1,128)S(1)}) custom-call(s32[2]{0:T(128)S(1)} %pad_add_fusion.ids_ref, bf16[1536,2048]{1,0:T(8,128)(2,1)S(1)} %get-tuple-element.58.cents_ref.old_ref, ...), custom_call_target="tpu_custom_call", output_to_operand_aliasing={{0}: (5, {}), {1}: (6, {}), {2}: (7, {})} | custom-call | tf_op jit(solution)/shard_map/own_scores/pallas_call | solution.py:157
  125.3 3.7 %own_scores.7 = (bf16[1024,2048]{1,0:T(8,128)(2,1)S(1)}, f32[384,1024]{1,0:T(8,128)S(1)}, f32[8,1,128]{2,1,0:T(1,128)S(1)}) custom-call(s32[2]{0:T(128)S(1)} %pad_add_fusion.ids_ref, bf16[1536,2048]{1,0:T(8,128)(2,1)S(1)} %get-tuple-element.58.cents_ref.old_ref, ...), custom_call_target="tpu_custom_call", output_to_operand_aliasing={{0}: (6, {}), {1}: (7, {}), {2}: (8, {})} | custom-call | tf_op jit(solution)/shard_map/own_scores/pallas_call | solution.py:157
  129.1 11.4 %collective-permute-start.27 = (f32[16,128]{1,0:T(8,128)S(1)}, f32[16,128]{1,0:T(8,128)S(1)}, u32[]{:S(2)}, u32[]{:S(2)}) collective-permute-start(f32[16,128]{1,0:T(8,128)S(1)} %pad_maximum_fusion.refs_0_), channel_id=1, source_target_pairs={{0,2},{1,3},{2,0},{3,1},{4,6},{5,7},{6,4},{7,5},{8,10},{9,11},{10,... | collective-permute-start | bytes 24584 | tf_op jit(solution)/shard_map/ppermute | solution.py:30
  144.2 2.5 collective-permute-done.29.refs_4_
  149.1 3.0 %collective-permute-done.31.refs_6_ = f32[16,128]{1,0:T(8,128)S(1)} collective-permute-done((f32[16,128]{1,0:T(8,128)S(1)}, f32[16,128]{1,0:T(8,128)S(1)}, u32[]{:S(2)}, u32[]{:S(2)}) %collective-permute-start.31) | collective-permute-done | bytes 8224 | tf_op jit(solution)/shard_map/ppermute | solution.py:30
  157.2 9.8 %collective-permute-done.19.refs_1_ = bf16[128,2048]{1,0:T(8,128)(2,1)S(1)} collective-permute-done((bf16[128,2048]{1,0:T(8,128)(2,1)S(1)}, bf16[128,2048]{1,0:T(8,128)(2,1)S(1)}, u32[]{:S(2)}, u32[]{:S(2)}) %collective-permute-start.19) | collective-permute-done | bytes 524320 | tf_op jit(solution)/shard_map/ppermute | solution.py:30
  169.0 10.0 %collective-permute-done.21.refs_3_ = bf16[128,2048]{1,0:T(8,128)(2,1)S(1)} collective-permute-done((bf16[128,2048]{1,0:T(8,128)(2,1)S(1)}, bf16[128,2048]{1,0:T(8,128)(2,1)S(1)}, u32[]{:S(2)}, u32[]{:S(2)}) %collective-permute-start.21) | collective-permute-done | bytes 524320 | tf_op jit(solution)/shard_map/ppermute | solution.py:30
  181.2 9.1 %collective-permute-done.17.refs_3_ = bf16[128,2048]{1,0:T(8,128)(2,1)S(1)} collective-permute-done((bf16[128,2048]{1,0:T(8,128)(2,1)S(1)}, bf16[128,2048]{1,0:T(8,128)(2,1)S(1)}, u32[]{:S(2)}, u32[]{:S(2)}) %collective-permute-start.17) | collective-permute-done | bytes 524320 | tf_op jit(solution)/shard_map/ppermute | solution.py:30
  192.9 8.6 %collective-permute-done.16.refs_2_ = bf16[128,2048]{1,0:T(8,128)(2,1)S(1)} collective-permute-done((bf16[128,2048]{1,0:T(8,128)(2,1)S(1)}, bf16[128,2048]{1,0:T(8,128)(2,1)S(1)}, u32[]{:S(2)}, u32[]{:S(2)}) %collective-permute-start.16) | collective-permute-done | bytes 524320 | tf_op jit(solution)/shard_map/ppermute | solution.py:30
  202.7 4.0 %side_scores.4 = (bf16[1024,2048]{1,0:T(8,128)(2,1)S(1)}, bf16[1024,2048]{1,0:T(8,128)(2,1)S(1)}, f32[576,1024]{1,0:T(8,128)S(1)}, f32[576,1024]{1,0:T(8,128)S(1)}) custom-call(s32[2]{0:T(128)S(1)} %pad_add_fusion.ids_ref, bf16[1536,2048]{1,0:T(8,128)(2,1)S(1)} %get-tuple-element.58.cents_ref.old_ref, f32[1536,1]{1,0:T(8,128)S(1)} %get-tuple-element.59.norm_ref, ...), custom_call_target="tpu_custom_call" | custom-call | tf_op jit(solution)/shard_map/side_scores/pallas_call | solution.py:212
  206.7 4.0 %side_scores.5 = (bf16[1024,2048]{1,0:T(8,128)(2,1)S(1)}, bf16[1024,2048]{1,0:T(8,128)(2,1)S(1)}, f32[576,1024]{1,0:T(8,128)S(1)}, f32[576,1024]{1,0:T(8,128)S(1)}) custom-call(s32[2]{0:T(128)S(1)} %pad_add_fusion.ids_ref, ...), custom_call_target="tpu_custom_call", output_to_operand_aliasing={{0}: (7, {}), {1}: (8, {}), {2}: (9, {}), {3}: (10, {})} | custom-call | tf_op jit(solution)/shard_map/side_scores/pallas_call | solution.py:212
  210.7 4.0 %side_scores.6 = (bf16[1024,2048]{1,0:T(8,128)(2,1)S(1)}, bf16[1024,2048]{1,0:T(8,128)(2,1)S(1)}, f32[576,1024]{1,0:T(8,128)S(1)}, f32[576,1024]{1,0:T(8,128)S(1)}) custom-call(s32[2]{0:T(128)S(1)} %pad_add_fusion.ids_ref, ...), custom_call_target="tpu_custom_call", output_to_operand_aliasing={{0}: (7, {}), {1}: (8, {}), {2}: (9, {}), {3}: (10, {})} | custom-call | tf_op jit(solution)/shard_map/side_scores/pallas_call | solution.py:212
  214.7 4.0 %side_scores.7 = (bf16[1024,2048]{1,0:T(8,128)(2,1)S(1)}, bf16[1024,2048]{1,0:T(8,128)(2,1)S(1)}, f32[576,1024]{1,0:T(8,128)S(1)}, f32[576,1024]{1,0:T(8,128)S(1)}) custom-call(s32[2]{0:T(128)S(1)} %pad_add_fusion.ids_ref, ...), custom_call_target="tpu_custom_call", output_to_operand_aliasing={{0}: (9, {}), {1}: (10, {}), {2}: (11, {}), {3}: (12, {})} | custom-call | tf_op jit(solution)/shard_map/side_scores/pallas_call | solution.py:212
  218.8 2.7 %sent_sums.3 = (f32[192,1152]{1,0:T(8,128)S(1)}, f32[192,1152]{1,0:T(8,128)S(1)}) custom-call(bf16[1024,2048]{1,0:T(8,128)(2,1)S(1)} %get-tuple-element.91.b_ref.x_ref, bf16[1024,2048]{1,0:T(8,128)(2,1)S(1)} %get-tuple-element.92.c_ref.y_ref, f32[576,1024]{1,0:T(8,128)S(1)} %get-tuple-element.94.bs_ref.xs_ref, ...), custom_call_target="tpu_custom_call" | custom-call | tf_op jit(solution)/shard_map/sent_sums/pallas_call | solution.py:296
  223.7 2.4 sent_sums.2
  228.4 7.9 %own_sums.1 = (f32[384,2048]{1,0:T(8,128)S(1)}, f32[384,1]{1,0:T(8,128)S(1)}) custom-call(bf16[1024,2048]{1,0:T(8,128)(2,1)S(1)} %get-tuple-element.78.a_ref, bf16[1024,2048]{1,0:T(8,128)(2,1)S(1)} %get-tuple-element.91.b_ref.x_ref, bf16[1024,2048]{1,0:T(8,128)(2,1)S(1)} %get-tuple-element.92.c_ref.y_ref, f32[384,1024]{1,0:T(8,128)S(1)} %get-tuple-element.93.as_ref, ...), custom_call_target="tpu_custom_call" | custom-call | tf_op jit(solution)/shard_map/own_sums/pallas_call | solution.py:324
  236.4 3.0 %collective-permute-done.35 = f16[192,1024]{1,0:T(8,128)(2,1)S(1)} collective-permute-done((f16[192,1024]{1,0:T(8,128)(2,1)S(1)}, f16[192,1024]{1,0:T(8,128)(2,1)S(1)}, u32[]{:S(2)}, u32[]{:S(2)}) %collective-permute-start.35) | collective-permute-done | bytes 393248 | tf_op jit(solution)/shard_map/ppermute | solution.py:30
  239.7 3.2 %update.2 = (f32[384,2048]{1,0:T(8,128)}, f32[384,1]{1,0:T(8,128)S(1)}, f32[384,1]{1,0:T(8,128)S(1)}) custom-call(s32[2]{0:T(128)S(1)} %pad_add_fusion.ids_ref, f32[384,2048]{1,0:T(8,128)S(1)} %get-tuple-element.99.own_ref, f32[384,1]{1,0:T(8,128)S(1)} %get-tuple-element.100.count_ref, f32[192,1152]{1,0:T(8,128)S(1)} %convert_element_type.29.a_ref, ...), custom_call_target="tpu_custom_call" | custom-call | tf_op jit(solution)/shard_map/update/pallas_call | solution.py:405
  242.9 3.4 %update.3 = (f32[384,2048]{1,0:T(8,128)}, f32[384,1]{1,0:T(8,128)S(1)}, f32[32,128]{1,0:T(8,128)}) custom-call(s32[2]{0:T(128)S(1)} %pad_add_fusion.ids_ref, f32[384,2048]{1,0:T(8,128)S(1)} %get-tuple-element.99.own_ref, f32[384,1]{1,0:T(8,128)S(1)} %get-tuple-element.100.count_ref, ...), custom_call_target="tpu_custom_call", output_to_operand_aliasing={{0}: (8, {})} | custom-call | tf_op jit(solution)/shard_map/update/pallas_call | solution.py:405
  246.3 3.3 %all-to-all-start = ((f32[32,1,128]{2,1,0:T(1,128)}), f32[32,1,128]{2,1,0:T(1,128)S(1)}, u32[]{:S(2)}, u32[]{:S(2)}) async-start(f32[32,1,128]{2,1,0:T(1,128)} %bitcast.6), calls=%async_computation | async-start | bytes 32768 | tf_op jit(solution)/shard_map/all_to_all | solution.py:508
  250.3 6.4 %all-to-all-done = f32[32,1,128]{2,1,0:T(1,128)S(1)} async-done(((f32[32,1,128]{2,1,0:T(1,128)}), f32[32,1,128]{2,1,0:T(1,128)S(1)}, u32[]{:S(2)}, u32[]{:S(2)}) %all-to-all-start) | async-done | bytes 16416 | tf_op jit(solution)/shard_map/all_to_all | solution.py:508
  (84 shorter events, 38.9 us)
Async XLA Ops:
  3.8 42.1 %collective-permute-start.7 = (bf16[128,2048]{1,0:T(8,128)(2,1)S(1)}, bf16[128,2048]{1,0:T(8,128)(2,1)S(1)}, u32[]{:S(2)}, u32[]{:S(2)}) collective-permute-start(bf16[128,2048]{1,0:T(8,128)(2,1)S(1)} %get-tuple-element.68), channel_id=1, source_target_pairs={{0,1},{1,0},{2,3},{3,2},{4,5},{5,4},{6,7},{7,6},{8,9},{9,8},{10,11... | collective-permute-start | bytes 1572872 | tf_op jit(solution)/shard_map/ppermute | solution.py:30
  6.4 41.0 %collective-permute-start.5 = (bf16[128,2048]{1,0:T(8,128)(2,1)S(1)}, bf16[128,2048]{1,0:T(8,128)(2,1)S(1)}, u32[]{:S(2)}, u32[]{:S(2)}) collective-permute-start(bf16[128,2048]{1,0:T(8,128)(2,1)S(1)} %get-tuple-element.65), channel_id=1, source_target_pairs={{0,2},{1,3},{2,0},{3,1},{4,6},{5,7},{6,4},{7,5},{8,10},{9,11},{10,... | collective-permute-start | bytes 1572872 | tf_op jit(solution)/shard_map/ppermute | solution.py:30
  9.5 39.6 %collective-permute-start.6 = (bf16[128,2048]{1,0:T(8,128)(2,1)S(1)}, bf16[128,2048]{1,0:T(8,128)(2,1)S(1)}, u32[]{:S(2)}, u32[]{:S(2)}) collective-permute-start(bf16[128,2048]{1,0:T(8,128)(2,1)S(1)} %get-tuple-element.66), channel_id=1, source_target_pairs={{0,3},{1,2},{2,1},{3,0},{4,7},{5,6},{6,5},{7,4},{8,11},{9,10},{10,... | collective-permute-start | bytes 1572872 | tf_op jit(solution)/shard_map/ppermute | solution.py:30
  9.5 30.7 %collective-permute-start.1 = (bf16[128,1024]{1,0:T(8,128)(2,1)S(1)}, bf16[128,1024]{1,0:T(8,128)(2,1)S(1)}, u32[]{:S(2)}, u32[]{:S(2)}) collective-permute-start(bf16[128,1024]{1,0:T(8,128)(2,1)S(1)} %get-tuple-element.61), channel_id=1, source_target_pairs={{0,7},{1,6},{2,5},{3,4},{4,3},{5,2},{6,1},{7,0},{8,15},{9,14},{10,... | collective-permute-start | bytes 786440 | tf_op jit(solution)/shard_map/ppermute | solution.py:30
  12.9 33.0 %collective-permute-start.2 = (bf16[128,1024]{1,0:T(8,128)(2,1)S(1)}, bf16[128,1024]{1,0:T(8,128)(2,1)S(1)}, u32[]{:S(2)}, u32[]{:S(2)}) collective-permute-start(bf16[128,1024]{1,0:T(8,128)(2,1)S(1)} %get-tuple-element.62), channel_id=1, source_target_pairs={{0,7},{1,6},{2,5},{3,4},{4,3},{5,2},{6,1},{7,0},{8,15},{9,14},{10,... | collective-permute-start | bytes 786440 | tf_op jit(solution)/shard_map/ppermute | solution.py:30
  40.2 51.1 %collective-permute-start.4 = (bf16[128,2048]{1,0:T(8,128)(2,1)S(1)}, bf16[128,2048]{1,0:T(8,128)(2,1)S(1)}, u32[]{:S(2)}, u32[]{:S(2)}) collective-permute-start(bf16[128,2048]{1,0:T(8,128)(2,1)S(1)} %get-tuple-element.64), channel_id=1, source_target_pairs={{0,5},{1,4},{2,7},{3,6},{4,1},{5,0},{6,3},{7,2},{8,13},{9,12},{10,... | collective-permute-start | bytes 1572872 | tf_op jit(solution)/shard_map/ppermute | solution.py:30
  45.9 56.8 %collective-permute-start.3 = (bf16[128,2048]{1,0:T(8,128)(2,1)S(1)}, bf16[128,2048]{1,0:T(8,128)(2,1)S(1)}, u32[]{:S(2)}, u32[]{:S(2)}) collective-permute-start(bf16[128,2048]{1,0:T(8,128)(2,1)S(1)} %get-tuple-element.63), channel_id=1, source_target_pairs={{0,4},{1,5},{2,6},{3,7},{4,0},{5,1},{6,2},{7,3},{8,12},{9,13},{10,... | collective-permute-start | bytes 1572872 | tf_op jit(solution)/shard_map/ppermute | solution.py:30
  45.9 58.3 %collective-permute-start = (bf16[128,2048]{1,0:T(8,128)(2,1)S(1)}, bf16[128,2048]{1,0:T(8,128)(2,1)S(1)}, u32[]{:S(2)}, u32[]{:S(2)}) collective-permute-start(bf16[128,2048]{1,0:T(8,128)(2,1)S(1)} %get-tuple-element.60), channel_id=1, source_target_pairs={{0,6},{1,7},{2,4},{3,5},{4,2},{5,3},{6,0},{7,1},{8,14},{9,15},{10,... | collective-permute-start | bytes 1572872 | tf_op jit(solution)/shard_map/ppermute | solution.py:30
  47.4 58.4 %collective-permute-start.22 = (bf16[128,2048]{1,0:T(8,128)(2,1)S(1)}, bf16[128,2048]{1,0:T(8,128)(2,1)S(1)}, u32[]{:S(2)}, u32[]{:S(2)}) collective-permute-start(bf16[128,2048]{1,0:T(8,128)(2,1)S(1)} %get-tuple-element.67.refs_0_), channel_id=1, source_target_pairs={{0,8},{8,0},{16,24},{24,16},{1,9},{9,1},{17,25},{25,17},{2,10},{10... | collective-permute-start | bytes 1572872 | tf_op jit(solution)/shard_map/ppermute | solution.py:30
  49.1 57.1 %collective-permute-start.24 = (bf16[128,2048]{1,0:T(8,128)(2,1)S(1)}, bf16[128,2048]{1,0:T(8,128)(2,1)S(1)}, u32[]{:S(2)}, u32[]{:S(2)}) collective-permute-start(bf16[128,2048]{1,0:T(8,128)(2,1)S(1)} %get-tuple-element.67.refs_0_), channel_id=1, source_target_pairs={{0,16},{8,24},{16,0},{24,8},{1,17},{9,25},{17,1},{25,9},{2,18},{10... | collective-permute-start | bytes 1572872 | tf_op jit(solution)/shard_map/ppermute | solution.py:30
  91.3 16.5 %collective-permute-start.10 = (bf16[128,1024]{1,0:T(8,128)(2,1)S(1)}, bf16[128,1024]{1,0:T(8,128)(2,1)S(1)}, u32[]{:S(2)}, u32[]{:S(2)}) collective-permute-start(bf16[128,1024]{1,0:T(8,128)(2,1)S(1)} %collective-permute-done.2.refs_2_), channel_id=1, source_target_pairs={{0,8},{8,0},{16,24},{24,16},{1,9},{9,1},{17,25},{25,17},{2,10},{10... | collective-permute-start | bytes 786440 | tf_op jit(solution)/shard_map/ppermute | solution.py:30
  102.7 51.5 %collective-permute-start.23 = (bf16[128,2048]{1,0:T(8,128)(2,1)S(1)}, bf16[128,2048]{1,0:T(8,128)(2,1)S(1)}, u32[]{:S(2)}, u32[]{:S(2)}) collective-permute-start(bf16[128,2048]{1,0:T(8,128)(2,1)S(1)} %collective-permute-done.7.refs_1_), channel_id=1, source_target_pairs={{0,8},{8,0},{16,24},{24,16},{1,9},{9,1},{17,25},{25,17},{2,10},{10... | collective-permute-start | bytes 1572872 | tf_op jit(solution)/shard_map/ppermute | solution.py:30
  104.2 50.8 %collective-permute-start.25 = (bf16[128,2048]{1,0:T(8,128)(2,1)S(1)}, bf16[128,2048]{1,0:T(8,128)(2,1)S(1)}, u32[]{:S(2)}, u32[]{:S(2)}) collective-permute-start(bf16[128,2048]{1,0:T(8,128)(2,1)S(1)} %collective-permute-done.7.refs_1_), channel_id=1, source_target_pairs={{0,16},{8,24},{16,0},{24,8},{1,17},{9,25},{17,1},{25,9},{2,18},{10... | collective-permute-start | bytes 1572872 | tf_op jit(solution)/shard_map/ppermute | solution.py:30
  105.8 23.2 %collective-permute-start.12 = (bf16[128,1024]{1,0:T(8,128)(2,1)S(1)}, bf16[128,1024]{1,0:T(8,128)(2,1)S(1)}, u32[]{:S(2)}, u32[]{:S(2)}) collective-permute-start(bf16[128,1024]{1,0:T(8,128)(2,1)S(1)} %collective-permute-done.1.refs_1_), channel_id=1, source_target_pairs={{0,16},{8,24},{16,0},{24,8},{1,17},{9,25},{17,1},{25,9},{2,18},{10... | collective-permute-start | bytes 786440 | tf_op jit(solution)/shard_map/ppermute | solution.py:30
  106.3 22.8 %collective-permute-start.13 = (bf16[128,1024]{1,0:T(8,128)(2,1)S(1)}, bf16[128,1024]{1,0:T(8,128)(2,1)S(1)}, u32[]{:S(2)}, u32[]{:S(2)}) collective-permute-start(bf16[128,1024]{1,0:T(8,128)(2,1)S(1)} %collective-permute-done.2.refs_2_), channel_id=1, source_target_pairs={{0,16},{8,24},{16,0},{24,8},{1,17},{9,25},{17,1},{25,9},{2,18},{10... | collective-permute-start | bytes 786440 | tf_op jit(solution)/shard_map/ppermute | solution.py:30
  107.9 48.3 %collective-permute-start.18 = (bf16[128,2048]{1,0:T(8,128)(2,1)S(1)}, bf16[128,2048]{1,0:T(8,128)(2,1)S(1)}, u32[]{:S(2)}, u32[]{:S(2)}) collective-permute-start(bf16[128,2048]{1,0:T(8,128)(2,1)S(1)} %collective-permute-done.5.refs_0_), channel_id=1, source_target_pairs={{0,8},{8,0},{16,24},{24,16},{1,9},{9,1},{17,25},{25,17},{2,10},{10... | collective-permute-start | bytes 1572872 | tf_op jit(solution)/shard_map/ppermute | solution.py:30
  129.1 13.0 %collective-permute-start.27 = (f32[16,128]{1,0:T(8,128)S(1)}, f32[16,128]{1,0:T(8,128)S(1)}, u32[]{:S(2)}, u32[]{:S(2)}) collective-permute-start(f32[16,128]{1,0:T(8,128)S(1)} %pad_maximum_fusion.refs_0_), channel_id=1, source_target_pairs={{0,2},{1,3},{2,0},{3,1},{4,6},{5,7},{6,4},{7,5},{8,10},{9,11},{10,... | collective-permute-start | bytes 24584 | tf_op jit(solution)/shard_map/ppermute | solution.py:30
  152.1 14.8 %collective-permute-start.19 = (bf16[128,2048]{1,0:T(8,128)(2,1)S(1)}, bf16[128,2048]{1,0:T(8,128)(2,1)S(1)}, u32[]{:S(2)}, u32[]{:S(2)}) collective-permute-start(bf16[128,2048]{1,0:T(8,128)(2,1)S(1)} %collective-permute-done.6.refs_1_), channel_id=1, source_target_pairs={{0,8},{8,0},{16,24},{24,16},{1,9},{9,1},{17,25},{25,17},{2,10},{10... | collective-permute-start | bytes 1572872 | tf_op jit(solution)/shard_map/ppermute | solution.py:30
  153.0 14.8 %collective-permute-start.20 = (bf16[128,2048]{1,0:T(8,128)(2,1)S(1)}, bf16[128,2048]{1,0:T(8,128)(2,1)S(1)}, u32[]{:S(2)}, u32[]{:S(2)}) collective-permute-start(bf16[128,2048]{1,0:T(8,128)(2,1)S(1)} %collective-permute-done.5.refs_0_), channel_id=1, source_target_pairs={{0,16},{8,24},{16,0},{24,8},{1,17},{9,25},{17,1},{25,9},{2,18},{10... | collective-permute-start | bytes 1572872 | tf_op jit(solution)/shard_map/ppermute | solution.py:30
  154.2 24.8 %collective-permute-start.21 = (bf16[128,2048]{1,0:T(8,128)(2,1)S(1)}, bf16[128,2048]{1,0:T(8,128)(2,1)S(1)}, u32[]{:S(2)}, u32[]{:S(2)}) collective-permute-start(bf16[128,2048]{1,0:T(8,128)(2,1)S(1)} %collective-permute-done.6.refs_1_), channel_id=1, source_target_pairs={{0,16},{8,24},{16,0},{24,8},{1,17},{9,25},{17,1},{25,9},{2,18},{10... | collective-permute-start | bytes 1572872 | tf_op jit(solution)/shard_map/ppermute | solution.py:30
  155.1 25.2 %collective-permute-start.15 = (bf16[128,2048]{1,0:T(8,128)(2,1)S(1)}, bf16[128,2048]{1,0:T(8,128)(2,1)S(1)}, u32[]{:S(2)}, u32[]{:S(2)}) collective-permute-start(bf16[128,2048]{1,0:T(8,128)(2,1)S(1)} %collective-permute-done.4.refs_1_), channel_id=1, source_target_pairs={{0,8},{8,0},{16,24},{24,16},{1,9},{9,1},{17,25},{25,17},{2,10},{10... | collective-permute-start | bytes 1572872 | tf_op jit(solution)/shard_map/ppermute | solution.py:30
  156.2 34.1 %collective-permute-start.17 = (bf16[128,2048]{1,0:T(8,128)(2,1)S(1)}, bf16[128,2048]{1,0:T(8,128)(2,1)S(1)}, u32[]{:S(2)}, u32[]{:S(2)}) collective-permute-start(bf16[128,2048]{1,0:T(8,128)(2,1)S(1)} %collective-permute-done.4.refs_1_), channel_id=1, source_target_pairs={{0,16},{8,24},{16,0},{24,8},{1,17},{9,25},{17,1},{25,9},{2,18},{10... | collective-permute-start | bytes 1572872 | tf_op jit(solution)/shard_map/ppermute | solution.py:30
  166.9 25.1 %collective-permute-start.14 = (bf16[128,2048]{1,0:T(8,128)(2,1)S(1)}, bf16[128,2048]{1,0:T(8,128)(2,1)S(1)}, u32[]{:S(2)}, u32[]{:S(2)}) collective-permute-start(bf16[128,2048]{1,0:T(8,128)(2,1)S(1)} %collective-permute-done.3.refs_0_), channel_id=1, source_target_pairs={{0,8},{8,0},{16,24},{24,16},{1,9},{9,1},{17,25},{25,17},{2,10},{10... | collective-permute-start | bytes 1572872 | tf_op jit(solution)/shard_map/ppermute | solution.py:30
  167.8 33.7 %collective-permute-start.16 = (bf16[128,2048]{1,0:T(8,128)(2,1)S(1)}, bf16[128,2048]{1,0:T(8,128)(2,1)S(1)}, u32[]{:S(2)}, u32[]{:S(2)}) collective-permute-start(bf16[128,2048]{1,0:T(8,128)(2,1)S(1)} %collective-permute-done.3.refs_0_), channel_id=1, source_target_pairs={{0,16},{8,24},{16,0},{24,8},{1,17},{9,25},{17,1},{25,9},{2,18},{10... | collective-permute-start | bytes 1572872 | tf_op jit(solution)/shard_map/ppermute | solution.py:30
  179.1 35.7 %collective-permute-start.11 = (bf16[128,2048]{1,0:T(8,128)(2,1)S(1)}, bf16[128,2048]{1,0:T(8,128)(2,1)S(1)}, u32[]{:S(2)}, u32[]{:S(2)}) collective-permute-start(bf16[128,2048]{1,0:T(8,128)(2,1)S(1)} %collective-permute-done.refs_0_), channel_id=1, source_target_pairs={{0,16},{8,24},{16,0},{24,8},{1,17},{9,25},{17,1},{25,9},{2,18},{10... | collective-permute-start | bytes 1572872 | tf_op jit(solution)/shard_map/ppermute | solution.py:30
  180.3 34.5 %collective-permute-start.8 = (bf16[128,2048]{1,0:T(8,128)(2,1)S(1)}, bf16[128,2048]{1,0:T(8,128)(2,1)S(1)}, u32[]{:S(2)}, u32[]{:S(2)}) collective-permute-start(bf16[128,2048]{1,0:T(8,128)(2,1)S(1)} %collective-permute-done.refs_0_), channel_id=1, source_target_pairs={{0,8},{8,0},{16,24},{24,16},{1,9},{9,1},{17,25},{25,17},{2,10},{10... | collective-permute-start | bytes 1572872 | tf_op jit(solution)/shard_map/ppermute | solution.py:30
  190.3 24.4 %collective-permute-start.9 = (bf16[128,1024]{1,0:T(8,128)(2,1)S(1)}, bf16[128,1024]{1,0:T(8,128)(2,1)S(1)}, u32[]{:S(2)}, u32[]{:S(2)}) collective-permute-start(bf16[128,1024]{1,0:T(8,128)(2,1)S(1)} %collective-permute-done.1.refs_1_), channel_id=1, source_target_pairs={{0,8},{8,0},{16,24},{24,16},{1,9},{9,1},{17,25},{25,17},{2,10},{10... | collective-permute-start | bytes 786440 | tf_op jit(solution)/shard_map/ppermute | solution.py:30
  192.0 26.7 %collective-permute-start.33 = (f32[8,128]{1,0:T(8,128)S(1)}, f32[8,128]{1,0:T(8,128)S(1)}, u32[]{:S(2)}, u32[]{:S(2)}) collective-permute-start(f32[8,128]{1,0:T(8,128)S(1)} %get-tuple-element.98.an_ref), channel_id=1, source_target_pairs={{0,8},{8,0},{16,24},{24,16},{1,9},{9,1},{17,25},{25,17},{2,10},{10... | collective-permute-start | bytes 12296 | tf_op jit(solution)/shard_map/ppermute | solution.py:30
  201.5 17.2 %collective-permute-start.34 = (f32[8,128]{1,0:T(8,128)S(1)}, f32[8,128]{1,0:T(8,128)S(1)}, u32[]{:S(2)}, u32[]{:S(2)}) collective-permute-start(f32[8,128]{1,0:T(8,128)S(1)} %get-tuple-element.98.an_ref), channel_id=1, source_target_pairs={{0,16},{8,24},{16,0},{24,8},{1,17},{9,25},{17,1},{25,9},{2,18},{10... | collective-permute-start | bytes 12296 | tf_op jit(solution)/shard_map/ppermute | solution.py:30
  221.6 18.0 %collective-permute-start.37 = (f16[192,1152]{1,0:T(8,128)(2,1)S(1)}, f16[192,1152]{1,0:T(8,128)(2,1)S(1)}, u32[]{:S(2)}, u32[]{:S(2)}) collective-permute-start(f16[192,1152]{1,0:T(8,128)(2,1)S(1)} %convert_element_type.28), channel_id=1, source_target_pairs={{0,8},{8,0},{16,24},{24,16},{1,9},{9,1},{17,25},{25,17},{2,10},{10... | collective-permute-start | bytes 1327112 | tf_op jit(solution)/shard_map/ppermute | solution.py:30
  222.6 17.0 %collective-permute-start.38 = (f16[192,1152]{1,0:T(8,128)(2,1)S(1)}, f16[192,1152]{1,0:T(8,128)(2,1)S(1)}, u32[]{:S(2)}, u32[]{:S(2)}) collective-permute-start(f16[192,1152]{1,0:T(8,128)(2,1)S(1)} %convert_element_type.30), channel_id=1, source_target_pairs={{0,16},{8,24},{16,0},{24,8},{1,17},{9,25},{17,1},{25,9},{2,18},{10... | collective-permute-start | bytes 1327112 | tf_op jit(solution)/shard_map/ppermute | solution.py:30
  226.1 13.2 %collective-permute-start.35 = (f16[192,1024]{1,0:T(8,128)(2,1)S(1)}, f16[192,1024]{1,0:T(8,128)(2,1)S(1)}, u32[]{:S(2)}, u32[]{:S(2)}) collective-permute-start(f16[192,1024]{1,0:T(8,128)(2,1)S(1)} %convert_element_type.24), channel_id=1, source_target_pairs={{0,8},{8,0},{16,24},{24,16},{1,9},{9,1},{17,25},{25,17},{2,10},{10... | collective-permute-start | bytes 1179656 | tf_op jit(solution)/shard_map/ppermute | solution.py:30
  (10 other events, 71.6 us)
where the time goes:
time: 258 us
  waiting for transfers between devices  138 us (53%)
  Pallas kernels  61.3 us (24%)
  starting transfers between devices  54.8 us (21%)
    ppermute x39, waiting for transfers between devices, swap(): return lax.ppermute(value, axis, [(i, i ^ offset) for i in range(size)])  131 us
    ppermute x39, starting transfers between devices, swap(): return lax.ppermute(value, axis, [(i, i ^ offset) for i in range(size)])  51.5 us
    pallas_call x4, Pallas kernels, side_scores(): pl.pallas_call(body, out_shape=[pltpu.VMEM(v.shape, v.dtype) for v in sta...  15.9 us
    pallas_call x4, Pallas kernels, own_scores(): pl.pallas_call(body, out_shape=[pltpu.VMEM(v.shape, v.dtype) for v in sta...  14.8 us
    pallas_call x1, Pallas kernels, own_sums(): pl.pallas_call(body, out_shape=[pltpu.VMEM((width, feat), F32), jax.Shape...  7.92 us
    pallas_call x2, Pallas kernels, update(): pl.pallas_call(body, out_shape=out_shape, grid_spec=pltpu.PrefetchScalarG...  6.55 us
    all_to_all x1, waiting for transfers between devices, on_square(): lax.all_to_all(peak, ('dp', 'mp'), split_axis=0, concat_axis=0, tiled=True)  6.37 us
    pallas_call x1, Pallas kernels, load_centroids(): pl.pallas_call(body, out_shape=[pltpu.VMEM((width, feat), centroids.dtype...  5.97 us
  transfers between devices with their start and end apart: 40, of which 16 were waited for; matrix products, arithmetic and copies ran while one was open for 0% of the time, Pallas kernels for 19%

commit v1 on v0

--- a/solution.py
+++ b/solution.py
@@ -41,7 +41,7 @@
     )
 
 
-def take_slots(ids, mask_t, data_rows, pieces, with_codes):
+def take_slots(ids, mask_t, data_rows, pieces, coded):
     block_count, n_mp = mask_t.shape
 
     def body(ids_ref, mask_ref, rows_ref, *refs):
@@ -60,14 +60,13 @@
             src = rows_ref.at[pl.ds(pl.multiple_of(start, BLOCK), BLOCK), pl.ds(first, count)]
             copies.append(pltpu.make_async_copy(src, outs[i], sems.at[i]))
             copies[-1].start()
-        if with_codes:
-            for k in range(n_mp):
-                outs[-1][k : k + 1, :] = jnp.full((1, LANES), code_of(k), jnp.int32).astype(F32)
+        for i, k in enumerate(coded):
+            outs[-1][i : i + 1, :] = jnp.full((1, LANES), code_of(k), jnp.int32).astype(F32)
         for copy in copies:
             copy.wait()
 
     shapes = [pltpu.VMEM((BLOCK, count), data_rows.dtype) for _, _, count in pieces]
-    if with_codes:
+    if coded:
         shapes.append(jax.ShapeDtypeStruct((n_mp, LANES), F32))
     return call(
         body, shapes, [SMEM, SMEM, ANY], [VMEM] * len(shapes), [pltpu.SemaphoreType.DMA((len(pieces),))], 8
@@ -164,6 +163,98 @@
     )(ids, *vmem(centroids), cent_norm, *rows, *([] if fresh else state))
 
 
+def first_product(centroids, rows, n_parts):
+    width = centroids.shape[0]
+    columns = rows.shape[1]
+    part = width // n_parts
+
+    def body(cents_ref, rows_ref, out_ref):
+        out_ref[...] = product(cents_ref, rows_ref)
+
+    return pl.pallas_call(
+        body,
+        out_shape=pltpu.VMEM((width, BLOCK), F32),
+        grid=(n_parts,),
+        in_specs=[
+            pl.BlockSpec((part, columns), lambda i: (i, 0)),
+            pl.BlockSpec((BLOCK, columns), lambda i: (0, 0)),
+        ],
+        out_specs=pl.BlockSpec((part, BLOCK), lambda i: (i, 0)),
+        name="first_product",
+        compiler_params=pltpu.CompilerParams(vmem_limit_bytes=8 << 20),
+    )(*vmem(centroids), rows)
+
+
+def last_scores(ids, centroids, cent_norm, rows, ahead, codes, state, n_parts, sharpness):
+    width, feat = centroids.shape
+    part = width // n_parts
+    wide = 2 * part
+    mid = feat // 2
+    n_mp = codes.shape[0]
+    last = n_mp - 1
+
+    def body(ids_ref, cents_ref, norm_ref, a_ref, b_ref, ahead_ref, code_ref, lse_ref, *refs):
+        rows_out, score_out, note_ref, top_ref, mass_ref = refs[len(refs) - 5 :]
+        step = pl.program_id(0)
+
+        @pl.when(step == 0)
+        def _():
+            rows_out[:, :mid] = a_ref[...]
+            rows_out[:, mid:] = b_ref[...]
+            top_ref[...] = jnp.full(top_ref.shape, -NEVER, F32)
+            mass_ref[...] = jnp.zeros(mass_ref.shape, F32)
+            for k in range(last):
+                note_ref[k : k + 1, :] = lse_ref[k]
+            note_ref[n_mp:, :] = code_ref[...]
+
+        score = sharpness * (2.0 * (ahead_ref[...] + product(cents_ref, b_ref)) - norm_ref[...])
+
+        @pl.when(step == ids_ref[1] // 2)
+        def _():
+            score_out[...] = jnp.where(ids_ref[1] % 2 == 0, score[:part], score[part:])
+
+        old_top = top_ref[...]
+        top = jnp.maximum(old_top, jnp.max(score, axis=0, keepdims=True))
+        mass = mass_ref[...] * jnp.exp(old_top - top) + jnp.sum(jnp.exp(score - top), axis=0, keepdims=True)
+        top_ref[...] = top
+        mass_ref[...] = mass
+        note_ref[last : last + 1, :] = top + jnp.log(mass)
+
+    def whole(shape):
+        return pl.BlockSpec(shape, lambda i, ids: (0,) * len(shape))
+
+    grid_spec = pltpu.PrefetchScalarGridSpec(
+        num_scalar_prefetch=1,
+        grid=(n_parts // 2,),
+        in_specs=[
+            pl.BlockSpec((wide, mid), lambda i, ids: (i, 1)),
+            pl.BlockSpec((wide, 1), lambda i, ids: (i, 0)),
+            whole((BLOCK, mid)),
+            whole((BLOCK, mid)),
+            pl.BlockSpec((wide, BLOCK), lambda i, ids: (i, 0)),
+            whole(codes.shape),
+            whole(state[2].shape),
+            ANY,
+            ANY,
+        ],
+        out_specs=[
+            pl.BlockSpec((BLOCK, feat), lambda i, ids: (last, 0)),
+            pl.BlockSpec((part, BLOCK), lambda i, ids: (0, last)),
+            whole((2 * n_mp, LANES)),
+        ],
+        scratch_shapes=[pltpu.VMEM((1, BLOCK), F32)] * 2,
+    )
+    return pl.pallas_call(
+        body,
+        out_shape=[pltpu.VMEM(v.shape, v.dtype) for v in state[:2]]
+        + [jax.ShapeDtypeStruct((2 * n_mp, LANES), F32)],
+        grid_spec=grid_spec,
+        input_output_aliases={8: 0, 9: 1},
+        name="last_scores",
+        compiler_params=pltpu.CompilerParams(vmem_limit_bytes=10 << 20),
+    )(ids, *vmem(centroids), cent_norm, *rows, ahead, codes, state[2], *state[:2])
+
+
 def side_scores(ids, centroids, cent_norm, sides, pieces, state, at, n_slots, half, sharpness):
     feat = centroids.shape[1]
     n_rows = n_slots * BLOCK
@@ -219,23 +310,68 @@
     )(ids, *vmem(centroids), cent_norm, *sides[0], *sides[1], *([] if fresh else state))
 
 
+def one_side_scores(ids, centroids, cent_norm, rows, pieces, state, at, n_slots, half, sharpness, bit):
+    feat = centroids.shape[1]
+    n_rows = n_slots * BLOCK
+    n_in = len(rows)
+
+    def body(ids_ref, cents_ref, norm_ref, *refs):
+        rows_out, score_out = refs[len(refs) - 2 :]
+
+        @pl.when(pl.program_id(0) == 0)
+        def _():
+            keep(refs[:n_in], pieces, rows_out)
+
+        score_out[...] = sharpness * (2.0 * product(cents_ref, rows_out) - norm_ref[...])
+
+    def block(i, ids):
+        mine = ids[1]
+        other = 2 * (mine ^ 2) + 1 if bit == 1 else 2 * (mine ^ 1)
+        return (jnp.where(i < 2, 2 * mine + i, other), 0)
+
+    grid_spec = pltpu.PrefetchScalarGridSpec(
+        num_scalar_prefetch=1,
+        grid=(3,),
+        in_specs=[pl.BlockSpec((half, feat), block), pl.BlockSpec((half, 1), block)]
+        + [pl.BlockSpec(r.shape, lambda i, ids: (0, 0)) for r in rows]
+        + [ANY] * 2,
+        out_specs=[
+            pl.BlockSpec((n_rows, feat), lambda i, ids: (at, 0)),
+            pl.BlockSpec((half, n_rows), lambda i, ids: (i, at)),
+        ],
+    )
+    return pl.pallas_call(
+        body,
+        out_shape=[pltpu.VMEM(v.shape, v.dtype) for v in state],
+        grid_spec=grid_spec,
+        input_output_aliases={3 + n_in + i: i for i in range(2)},
+        name="one_side_scores",
+        compiler_params=pltpu.CompilerParams(vmem_limit_bytes=12 << 20),
+    )(ids, *vmem(centroids), cent_norm, *rows, *state)
+
+
 def log_total(kept):
     peak = jnp.maximum(jnp.max(kept, axis=0, keepdims=True), 0.0)
     mass = jnp.sum(jnp.exp(kept - peak), axis=0, keepdims=True)
     return peak + jnp.log(jnp.exp(-peak) + mass)
 
 
-def combine(notes, block_count):
-    n_mp = len(notes)
+def combine(notes, seq, block_count):
+    n_mp = 2 * len(notes)
 
     def body(*refs):
-        note_refs, (slot_ref, row_ref) = refs[:n_mp], refs[n_mp:]
-        for k in range(n_mp):
-            lse = jnp.concatenate([note_refs[k ^ j][j : j + 1, :] for j in range(n_mp)], axis=0)
-            code = note_refs[k][n_mp : 2 * n_mp, :]
-            mine = code[k : k + 1, :]
+        note_refs, (slot_ref, row_ref) = refs[: len(notes)], refs[len(notes) :]
+
+        def rows(j, first, count):
+            start = 2 * n_mp * (j % 2) + first
+            return note_refs[j // 2][start : start + count, :]
+
+        for i, k in enumerate(seq):
+            lse = jnp.concatenate([rows(k ^ j, at, 1) for at, j in enumerate(seq)], axis=0)
+            code = rows(k, n_mp, n_mp)
+            mine = code[i : i + 1, :]
             total = log_total(jnp.where((code == mine) & (code > 0.0), lse, -NEVER))
-            slot_ref[k : k + 1, :] = jnp.where(mine > 0.0, total, NEVER)
+            slot_ref[i : i + 1, :] = jnp.where(mine > 0.0, total, NEVER)
             if k == 0:
                 for b in range(block_count):
                     row_ref[b : b + 1, :] = log_total(jnp.where(code == float(b + 1), lse, -NEVER))
@@ -243,7 +379,7 @@
     return call(
         body,
         [jax.ShapeDtypeStruct((n_mp, LANES), F32), jax.ShapeDtypeStruct((block_count, LANES), F32)],
-        [VMEM] * n_mp,
+        [VMEM] * len(notes),
         [VMEM, VMEM],
     )(*notes)
 
@@ -256,7 +392,7 @@
     return total
 
 
-def sent_sums(side_rows, side_score, norms, half, first, columns, tile):
+def sent_sums(side_rows, side_score, norms, half, first, columns, tile, with_counts):
     n_rows = side_rows[0].shape[0]
     steps = columns // tile
 
@@ -291,7 +427,6 @@
     score_spec = pl.BlockSpec((half, n_rows), lambda i: (2, 0))
     norm_spec = pl.BlockSpec(norms[0].shape, lambda i: (0, 0))
     out_spec = pl.BlockSpec((half, tile), lambda i: (0, i))
-    with_counts = first == 0
     width = columns + LANES if with_counts else columns
     return pl.pallas_call(
         body,
@@ -305,122 +440,153 @@
     )(*vmem(*side_rows, *side_score), *norms)
 
 
-def own_sums(rows, scores, norms, width, tile):
+def own_sums(ids, rows, scores, norms, parts, centroids, width, tile, done):
     n_rows, feat = rows[0].shape
-
-    def body(a_ref, b_ref, c_ref, as_ref, bs_ref, cs_ref, an_ref, bn_ref, cn_ref, out_ref, count_ref, w_buf):
+    half = width // 2
+
+    def body(ids_ref, *refs):
+        row_refs, score_refs, norm_refs = refs[:3], refs[3:6], refs[6:9]
+        part_refs, tail_refs, old_ref = refs[9:11], refs[11:13], refs[13]
+        out_ref, count_ref, new_ref, sent_ref, square_ref, w_buf = refs[14:]
+
         @pl.when(pl.program_id(0) == 0)
         def _():
             total = None
-            for i, (s_ref, n_ref) in enumerate(((as_ref, an_ref), (bs_ref, bn_ref), (cs_ref, cn_ref))):
-                total = weights_of(s_ref, n_ref, w_buf, i * n_rows, total)
+            for i in range(3):
+                total = weights_of(score_refs[i], norm_refs[i], w_buf, i * n_rows, total)
             count_ref[...] = jnp.sum(total, axis=1, keepdims=True)
 
-        acc = jnp.dot(w_buf[:, :n_rows], a_ref[...], preferred_element_type=F32)
-        acc += jnp.dot(w_buf[:, n_rows : 2 * n_rows], b_ref[...], preferred_element_type=F32)
-        acc += jnp.dot(w_buf[:, 2 * n_rows :], c_ref[...], preferred_element_type=F32)
+        acc = jnp.dot(w_buf[:, :n_rows], row_refs[0][...], preferred_element_type=F32)
+        acc += jnp.dot(w_buf[:, n_rows : 2 * n_rows], row_refs[1][...], preferred_element_type=F32)
+        acc += jnp.dot(w_buf[:, 2 * n_rows :], row_refs[2][...], preferred_element_type=F32)
         out_ref[...] = acc
 
-    return pl.pallas_call(
-        body,
-        out_shape=[pltpu.VMEM((width, feat), F32), jax.ShapeDtypeStruct((width, 1), F32)],
-        grid=(feat // tile,),
-        in_specs=[pl.BlockSpec((n_rows, tile), lambda i: (0, i))] * 3
-        + [pl.BlockSpec((width, n_rows), lambda i: (0, 0))] * 3
-        + [pl.BlockSpec(norms[0].shape, lambda i: (0, 0))] * 3,
-        out_specs=[
-            pl.BlockSpec((width, tile), lambda i: (0, i)),
-            pl.BlockSpec((width, 1), lambda i: (0, 0)),
+        @pl.when(pl.program_id(0) == done)
+        def _():
+            for i in range(2):
+                span = slice(i * half, (i + 1) * half)
+                lane = lax.broadcasted_iota(jnp.int32, (half, LANES), 1)
+                sent = jnp.sum(jnp.where(lane < 3, tail_refs[i][...], 0.0), axis=1, keepdims=True)
+                back = part_refs[i][...] * (jnp.maximum(sent, 2.0**-20) * 2.0**-10)
+                before = old_ref[span, :].astype(F32)
+                after = (out_ref[span, :] + back + before) / (count_ref[span, :] + sent + 1.0)
+                new_ref[span, :] = after
+                sent_ref[span, :] = sent
+                square_ref[span, :] = jnp.sum(jnp.square(after - before), axis=1, keepdims=True)
+
+    def whole(shape):
+        return pl.BlockSpec(shape, lambda i, ids: (0,) * len(shape))
+
+    thin = jax.ShapeDtypeStruct((width, 1), F32)
+    return pl.pallas_call(
+        body,
+        out_shape=[
+            pltpu.VMEM((width, feat), F32),
+            thin,
+            jax.ShapeDtypeStruct((width, feat), F32),
+            thin,
+            thin,
         ],
-        scratch_shapes=[pltpu.VMEM((width, 3 * n_rows), BF16)],
+        grid_spec=pltpu.PrefetchScalarGridSpec(
+            num_scalar_prefetch=1,
+            grid=(feat // tile,),
+            in_specs=[pl.BlockSpec((n_rows, tile), lambda i, ids: (0, i))] * 3
+            + [whole((width, n_rows))] * 3
+            + [whole(norms[0].shape)] * 3
+            + [whole((half, tile))] * 2
+            + [pl.BlockSpec((half, LANES), lambda i, ids: (0, tile // LANES))] * 2
+            + [pl.BlockSpec((width, tile), lambda i, ids: (ids[1], done))],
+            out_specs=[
+                pl.BlockSpec((width, tile), lambda i, ids: (0, i)),
+                whole((width, 1)),
+                pl.BlockSpec((width, tile), lambda i, ids: (0, done)),
+                whole((width, 1)),
+                whole((width, 1)),
+            ],
+            scratch_shapes=[pltpu.VMEM((width, 3 * n_rows), BF16)],
+        ),
         name="own_sums",
         compiler_params=pltpu.CompilerParams(vmem_limit_bytes=24 << 20),
-    )(*vmem(*rows, *scores), *norms)
-
-
-def update(ids, own, counts, parts, centroids, first, state, n_devices):
+    )(ids, *vmem(*rows, *scores), *norms, *parts, *parts, *vmem(centroids))
+
+
+def update(ids, own, counts, parts, centroids, first, columns, state, final, n_devices):
     width, feat = own.shape
     half = width // 2
-    columns = feat // 2
-    lead = first == 0
-    rows = half // 2
-    steps = half // rows
-
-    def body(ids_ref, own_ref, count_ref, a_ref, b_ref, old_ref, *refs):
-        step = pl.program_id(0)
+    at = first // columns
+
+    def body(ids_ref, own_ref, count_ref, a_ref, b_ref, old_ref, sent_in, square_in, _, new_ref, *refs):
+        i = pl.program_id(0)
 
         def finish(part_ref):
-            if lead:
-                new_ref, sent_ref, square_ref = refs
-                tail = part_ref[:, columns:]
-                lane = lax.broadcasted_iota(jnp.int32, tail.shape, 1)
-                sent = jnp.sum(jnp.where(lane < 3, tail, 0.0), axis=1, keepdims=True)
-                sent_ref[...] = sent
-            else:
-                sent_in, square_in, _, new_ref, move_ref, peak_ref = refs
-                sent = sent_in[...]
-            back = part_ref[:, :columns] * (jnp.maximum(sent, 2.0**-20) * 2.0**-10)
+            sent = sent_in[...]
+            back = part_ref[...] * (jnp.maximum(sent, 2.0**-20) * 2.0**-10)
             before = old_ref[...].astype(F32)
             after = (own_ref[...] + back + before) / (count_ref[...] + sent + 1.0)
             new_ref[...] = after
-            square = jnp.sum(jnp.square(after - before), axis=1, keepdims=True)
-            if lead:
-                square_ref[...] = square
-            else:
-                move = jnp.sqrt(square + square_in[...] + 1.0)
-                move_ref[...] = move
-                top = jnp.broadcast_to(jnp.max(move, axis=0, keepdims=True), peak_ref.shape)
-                peak_ref[...] = jnp.where(step == 0, top, jnp.maximum(top, peak_ref[...]))
-
-        @pl.when(step < steps)
+            total = square_in[...] + jnp.sum(jnp.square(after - before), axis=1, keepdims=True)
+            if not final:
+                refs[0][...] = total
+                return
+            move_ref, peak_ref = refs
+            move = jnp.sqrt(total + 1.0)
+            move_ref[...] = move
+            top = jnp.broadcast_to(jnp.max(move, axis=0, keepdims=True), peak_ref.shape)
+            peak_ref[...] = jnp.where(i == 0, top, jnp.maximum(top, peak_ref[...]))
+
+        @pl.when(i == 0)
         def _():
             finish(a_ref)
 
-        @pl.when(step >= steps)
+        @pl.when(i == 1)
         def _():
             finish(b_ref)
 
-    at = 0 if lead else 1
-    column = pl.BlockSpec((rows, 1), lambda i, ids: (i, 0))
-    part_width = parts[0].shape[1]
-    in_specs = [
-        pl.BlockSpec((rows, columns), lambda i, ids: (i, at)),
-        column,
-        pl.BlockSpec((rows, part_width), lambda i, ids: (jnp.minimum(i, steps - 1), 0)),
-        pl.BlockSpec((rows, part_width), lambda i, ids: (jnp.maximum(i - steps, 0), 0)),
-        pl.BlockSpec((rows, columns), lambda i, ids: (ids[1] * (2 * steps) + i, at)),
-    ]
-    new_spec = pl.BlockSpec((rows, columns), lambda i, ids: (i, at))
-    new_shape = jax.ShapeDtypeStruct((width, feat), F32)
+    column = pl.BlockSpec((half, 1), lambda i, ids: (i, 0))
+    block = pl.BlockSpec((half, columns), lambda i, ids: (i, at))
     thin = jax.ShapeDtypeStruct((width, 1), F32)
-    if lead:
-        out_shape, out_specs, extra, aliases = [new_shape, thin, thin], [new_spec, column, column], [], {}
-    else:
-        new, sent, square = state
-        extra = [sent, square, new]
-        in_specs += [column, column, ANY]
-        out_shape = [new_shape, thin, jax.ShapeDtypeStruct((n_devices, LANES), F32)]
-        out_specs = [new_spec, column, pl.BlockSpec((n_devices, LANES), lambda i, ids: (0, 0))]
-        aliases = {8: 0}
+    new, sent, square = state
+    out_shape = [jax.ShapeDtypeStruct((width, feat), F32), thin]
+    out_specs = [block, column]
+    if final:
+        out_shape.append(jax.ShapeDtypeStruct((n_devices, LANES), F32))
+        out_specs.append(pl.BlockSpec((n_devices, LANES), lambda i, ids: (0, 0)))
     return pl.pallas_call(
         body,
         out_shape=out_shape,
         grid_spec=pltpu.PrefetchScalarGridSpec(
-            num_scalar_prefetch=1, grid=(2 * steps,), in_specs=in_specs, out_specs=out_specs
+            num_scalar_prefetch=1,
+            grid=(2,),
+            in_specs=[
+                block,
+                column,
+                pl.BlockSpec((half, columns), lambda i, ids: (0, 0)),
+                pl.BlockSpec((half, columns), lambda i, ids: (0, 0)),
+                pl.BlockSpec((half, columns), lambda i, ids: (2 * ids[1] + i, at)),
+                column,
+                column,
+                ANY,
+            ],
+            out_specs=out_specs,
         ),
-        input_output_aliases=aliases,
+        input_output_aliases={8: 0},
         name="update",
-        compiler_params=pltpu.CompilerParams(vmem_limit_bytes=8 << 20),
-    )(ids, *vmem(own), counts, *parts, *vmem(centroids), *extra)
-
-
-def z_order(n_mp):
-    half = n_mp // 2
-    return [half] + [k for k in range(2, n_mp) if k != half]
+        compiler_params=pltpu.CompilerParams(vmem_limit_bytes=10 << 20),
+    )(ids, *vmem(own), counts, *parts, *vmem(centroids), sent, square, new)
+
+
+def sequence(n_mp):
+    return [0, 1, 6, 2, 3, 7, 4, 5] if n_mp == 8 else list(range(n_mp))
+
+
+def pieces_of(n_mp, feat):
+    mid = feat // 2
+    seq = sequence(n_mp)
+    return [[(k, 0, feat)] if at < n_mp - 3 else [(k, 0, mid), (k, mid, mid)] for at, k in enumerate(seq)]
 
 
 def own_groups(n_mp):
-    return [(k, k + 1) for k in range(0, n_mp, 2)]
+    return [(k, k + 1) for k in range(0, n_mp - 2, 2)] + [(n_mp - 2,)]
 
 
 def on_square(data_rows, centroids, block_mask, lower_bound):
@@ -437,19 +603,19 @@
     ids = jnp.stack([my_mp, my_dp])
     mask_t = block_mask.T
 
-    last = n_mp - 1
-    cuts = {k: [(k, 0, feat)] for k in range(n_mp)}
-    cuts[last] = [(last, 0, feat // 2), (last, feat // 2, feat // 2)]
-    early = [p for k in z_order(n_mp)[:3] for p in cuts[k]]
-    late = cuts[0] + [p for k in z_order(n_mp)[3:] for p in cuts[k]] + cuts[1]
-    got = dict(zip(early, take_slots(ids, mask_t, data_rows, early, False)))
-    *rest, codes = take_slots(ids, mask_t, data_rows, late, True)
+    seq = sequence(n_mp)
+    last = seq[-1]
+    cuts = {cut[0][0]: cut for cut in pieces_of(n_mp, feat)}
+    early = [p for k in seq[2:5] for p in cuts[k]]
+    late = cuts[0] + [p for k in seq[5:] for p in cuts[k]] + cuts[1]
+    got = dict(zip(early, take_slots(ids, mask_t, data_rows, early, [])))
+    *rest, codes = take_slots(ids, mask_t, data_rows, late, seq)
     got.update(zip(late, rest))
     for piece in early + late[1:]:
         got[piece] = swap(got[piece], "mp", n_mp, piece[0])
 
     side = {}
-    for k in range(n_mp):
+    for k in seq:
         for piece in cuts[k]:
             for bit in (1, 2):
                 side[bit, piece] = swap(got[piece], "dp", n_dp, bit)
@@ -464,47 +630,64 @@
     ]
     sides = [jax.ShapeDtypeStruct((n_rows, feat), BF16)] * 2
     sides += [jax.ShapeDtypeStruct((3 * half, n_rows), F32)] * 2
+    ahead = first_product(cents, got[cuts[last][0]], n_dp)
     for group in own_groups(n_mp):
-        held = [p for k in group for p in cuts[k]]
-        placed = [(p[0] - group[0], p[1], p[2]) for p in held]
+        held = [p for at in group for p in cuts[seq[at]]]
+        placed = [(seq.index(p[0]) - group[0], p[1], p[2]) for p in held]
         own = own_scores(
             ids, cents, cent_norm, [got[p] for p in held], placed, own, group[0] // len(group), len(group),
             n_dp, sharpness,
         )
     for i in range(n_mp // 2):
-        held = cuts[2 * i] + cuts[2 * i + 1]
-        placed = [(p[0] - 2 * i, p[1], p[2]) for p in held]
+        held = cuts[seq[2 * i]] + cuts[seq[2 * i + 1]]
+        placed = [(seq.index(p[0]) - 2 * i, p[1], p[2]) for p in held]
         pair = [[side[bit, p] for p in held] for bit in (1, 2)]
-        sides = side_scores(ids, cents, cent_norm, pair, placed, sides, i, 2, half, sharpness)
-
-    note = jnp.concatenate([own[2][:, 0, :], codes])
-    notes = [note]
-    for k in range(1, n_mp):
-        notes.append(swap(note, "mp", n_mp, k))
-    slot_norm, row_norm = combine(notes, block_count)
+        if i < n_mp // 2 - 1:
+            sides = list(side_scores(ids, cents, cent_norm, pair, placed, sides, i, 2, half, sharpness))
+            continue
+        for bit in (1, 2):
+            sides[bit - 1 :: 2] = one_side_scores(
+                ids, cents, cent_norm, pair[bit - 1], placed, sides[bit - 1 :: 2], i, 2, half, sharpness, bit
+            )
+
+    *own, note = last_scores(ids, cents, cent_norm, [got[p] for p in cuts[last]], ahead, codes, own, n_dp, sharpness)
+    beside = swap(note, "mp", n_mp, 1)
+    both = jnp.concatenate([note, beside])
+    notes = [both]
+    for k in range(2, n_mp, 2):
+        notes.append(swap(both, "mp", n_mp, k))
+    slot_norm, row_norm = combine(notes, seq, block_count)
     log_norm = row_norm.reshape(-1)
     side_norm = []
     for bit in (1, 2):
         side_norm.append(swap(slot_norm, "dp", n_dp, bit))
 
+    tile = feat // 4
+    spans = [(3 * tile, tile), (0, 2 * tile), (2 * tile, tile)]
     received = []
-    for part in range(2):
-        first = part * (feat // 2)
-        sent = sent_sums(sides[:2], sides[2:], side_norm, half, first, feat // 2, feat // 4)
+    for i, (first, columns) in enumerate(spans):
+        sent = sent_sums(sides[:2], sides[2:], side_norm, half, first, columns, tile, i == 0)
         for_y, for_x = [v.astype(jnp.float16) for v in sent]
-        received.append([swap(for_x, "dp", n_dp, 1), swap(for_y, "dp", n_dp, 2)])
-    total, counts = own_sums(
+        pair = []
+        for bit, message in ((1, for_x), (2, for_y)):
+            pair.append(swap(message, "dp", n_dp, bit).astype(F32))
+        received.append(pair)
+    total, counts, updated, sent, square = own_sums(
+        ids,
         [own[0], sides[0], sides[1]],
         [own[1], sides[2], sides[3]],
         [slot_norm] + side_norm,
+        received[0],
+        cents,
         own_width,
-        feat // 4,
-    )
-    state = None
-    for part in range(2):
-        parts = [v.astype(F32) for v in received[part]]
-        state = update(ids, total, counts, parts, cents, part * (feat // 2), state, n_dp * n_mp)
-    updated, movement, peak = state
+        tile,
+        spans[0][0] // tile,
+    )
+    for i, (first, columns) in list(enumerate(spans))[1:]:
+        updated, square, *peak = update(
+            ids, total, counts, received[i], cents, first, columns, [updated, sent, square], i == 2, n_dp * n_mp
+        )
+    movement, peak = square, peak[0]
     shard_peaks = lax.all_to_all(peak, ("dp", "mp"), split_axis=0, concat_axis=0, tiled=True)
     shard_peak = jnp.max(shard_peaks.reshape(n_dp, n_mp, LANES), axis=(0, 2))
     new_lower = lower_bound - shard_peak[:, None]

time: 258 us -> 274 us (1.062)
  starting transfers between devices: 54.8 us -> 85.9 us
  waiting for transfers between devices: 138 us -> 118 us
  Pallas kernels: 61.3 us -> 65.3 us
    ppermute x39 -> x44, starting transfers between devices: 51.5 us -> 83.2 us  [swap(): return lax.ppermute(value, axis, [(i, i ^ offset) for i in range(size)])]
    ppermute x39 -> x44, waiting for transfers between devices: 131 us -> 112 us  [swap(): return lax.ppermute(value, axis, [(i, i ^ offset) for i in range(size)])]
    pallas_call x1 -> x5, Pallas kernels: 7.92 us -> 18.5 us  [the longest x1 10 us: own_sums(): pl.pallas_call(body, out_shape=[pltpu.VMEM((width, feat), F32), thin, jax...]
    pallas_call x4 -> x3, Pallas kernels: 15.9 us -> 11.9 us  [side_scores(): pl.pallas_call(body, out_shape=[pltpu.VMEM(v.shape, v.dtype) for v in sta...]
  transfers between devices with their start and end apart: 40 -> 45, of which waited for: 16 -> 19; matrix products, arithmetic and copies ran while one was open for 0% -> 0% of each run, Pallas kernels for 19% -> 21%
where the time goes in v1:
time: 274 us; the launch traced here: 273 us
  waiting for transfers between devices  118 us (43%)
  starting transfers between devices  85.9 us (31%)
  Pallas kernels  65.3 us (24%)
    ppermute x44, waiting for transfers between devices, swap(): return lax.ppermute(value, axis, [(i, i ^ offset) for i in range(size)])  112 us
    ppermute x44, starting transfers between devices, swap(): return lax.ppermute(value, axis, [(i, i ^ offset) for i in range(size)])  83.2 us
    pallas_call x4, Pallas kernels, own_scores(): pl.pallas_call(body, out_shape=[pltpu.VMEM(v.shape, v.dtype) for v in sta...  14.3 us
    pallas_call x3, Pallas kernels, side_scores(): pl.pallas_call(body, out_shape=[pltpu.VMEM(v.shape, v.dtype) for v in sta...  11.9 us
    pallas_call x1, Pallas kernels, own_sums(): pl.pallas_call(body, out_shape=[pltpu.VMEM((width, feat), F32), thin, jax...  10 us
    all_to_all x1, waiting for transfers between devices, on_square(): lax.all_to_all(peak, ('dp', 'mp'), split_axis=0, concat_axis=0, tiled=True)  6.37 us
    pallas_call x1, Pallas kernels, load_centroids(): pl.pallas_call(body, out_shape=[pltpu.VMEM((width, feat), centroids.dtype...  5.96 us
  transfers between devices with their start and end apart: 45, of which 19 were waited for; matrix products, arithmetic and copies ran while one was open for 0% of the time, Pallas kernels for 21%

profile of v1, /device:TPU:0, one launch (start us, length us, event | category | flops | bytes accessed | tf_op | source)
XLA Modules:
  0.0 273.4 jit_solution(18051753375234331548)
XLA Ops:
  3.7 4.9 %collective-permute-start.5 = (bf16[128,1024]{1,0:T(8,128)(2,1)S(1)}, bf16[128,1024]{1,0:T(8,128)(2,1)S(1)}, u32[]{:S(2)}, u32[]{:S(2)}) collective-permute-start(bf16[128,1024]{1,0:T(8,128)(2,1)S(1)} %get-tuple-element.75), channel_id=1, source_target_pairs={{0,7},{1,6},{2,5},{3,4},{4,3},{5,2},{6,1},{7,0},{8,15},{9,14},{10,... | collective-permute-start | bytes 786440 | tf_op jit(solution)/shard_map/ppermute | solution.py:30
  12.0 3.3 %collective-permute-done.5.refs_1_ = bf16[128,1024]{1,0:T(8,128)(2,1)S(1)} collective-permute-done((bf16[128,1024]{1,0:T(8,128)(2,1)S(1)}, bf16[128,1024]{1,0:T(8,128)(2,1)S(1)}, u32[]{:S(2)}, u32[]{:S(2)}) %collective-permute-start.5) | collective-permute-done | bytes 262176 | tf_op jit(solution)/shard_map/ppermute | solution.py:30
  15.4 23.7 %collective-permute-start = (bf16[128,1024]{1,0:T(8,128)(2,1)S(1)}, bf16[128,1024]{1,0:T(8,128)(2,1)S(1)}, u32[]{:S(2)}, u32[]{:S(2)}) collective-permute-start(bf16[128,1024]{1,0:T(8,128)(2,1)S(1)} %get-tuple-element.69), channel_id=1, source_target_pairs={{0,5},{1,4},{2,7},{3,6},{4,1},{5,0},{6,3},{7,2},{8,13},{9,12},{10,... | collective-permute-start | bytes 786440 | tf_op jit(solution)/shard_map/ppermute | solution.py:30
  39.1 10.9 %collective-permute-start.1 = (bf16[128,1024]{1,0:T(8,128)(2,1)S(1)}, bf16[128,1024]{1,0:T(8,128)(2,1)S(1)}, u32[]{:S(2)}, u32[]{:S(2)}) collective-permute-start(bf16[128,1024]{1,0:T(8,128)(2,1)S(1)} %get-tuple-element.70), channel_id=1, source_target_pairs={{0,5},{1,4},{2,7},{3,6},{4,1},{5,0},{6,3},{7,2},{8,13},{9,12},{10,... | collective-permute-start | bytes 786440 | tf_op jit(solution)/shard_map/ppermute | solution.py:30
  52.2 8.2 %collective-permute-done.2.refs_0_ = bf16[128,1024]{1,0:T(8,128)(2,1)S(1)} collective-permute-done((bf16[128,1024]{1,0:T(8,128)(2,1)S(1)}, bf16[128,1024]{1,0:T(8,128)(2,1)S(1)}, u32[]{:S(2)}, u32[]{:S(2)}) %collective-permute-start.2) | collective-permute-done | bytes 262176 | tf_op jit(solution)/shard_map/ppermute | solution.py:30
  60.3 2.5 collective-permute-start.7
  62.8 14.4 %collective-permute-done.3.refs_1_ = bf16[128,1024]{1,0:T(8,128)(2,1)S(1)} collective-permute-done((bf16[128,1024]{1,0:T(8,128)(2,1)S(1)}, bf16[128,1024]{1,0:T(8,128)(2,1)S(1)}, u32[]{:S(2)}, u32[]{:S(2)}) %collective-permute-start.3) | collective-permute-done | bytes 262176 | tf_op jit(solution)/shard_map/ppermute | solution.py:30
  77.2 5.6 %collective-permute-done.rows_ref.a_ref = bf16[128,1024]{1,0:T(8,128)(2,1)S(1)} collective-permute-done((bf16[128,1024]{1,0:T(8,128)(2,1)S(1)}, bf16[128,1024]{1,0:T(8,128)(2,1)S(1)}, u32[]{:S(2)}, u32[]{:S(2)}) %collective-permute-start) | collective-permute-done | bytes 262176 | tf_op jit(solution)/shard_map/ppermute | solution.py:30
  82.8 5.6 %collective-permute-done.1.b_ref = bf16[128,1024]{1,0:T(8,128)(2,1)S(1)} collective-permute-done((bf16[128,1024]{1,0:T(8,128)(2,1)S(1)}, bf16[128,1024]{1,0:T(8,128)(2,1)S(1)}, u32[]{:S(2)}, u32[]{:S(2)}) %collective-permute-start.1) | collective-permute-done | bytes 262176 | tf_op jit(solution)/shard_map/ppermute | solution.py:30
  91.7 8.0 %collective-permute-done.8.refs_1_ = bf16[128,2048]{1,0:T(8,128)(2,1)S(1)} collective-permute-done((bf16[128,2048]{1,0:T(8,128)(2,1)S(1)}, bf16[128,2048]{1,0:T(8,128)(2,1)S(1)}, u32[]{:S(2)}, u32[]{:S(2)}) %collective-permute-start.8) | collective-permute-done | bytes 524320 | tf_op jit(solution)/shard_map/ppermute | solution.py:30
  101.0 9.8 %collective-permute-done.4.refs_0_ = bf16[128,2048]{1,0:T(8,128)(2,1)S(1)} collective-permute-done((bf16[128,2048]{1,0:T(8,128)(2,1)S(1)}, bf16[128,2048]{1,0:T(8,128)(2,1)S(1)}, u32[]{:S(2)}, u32[]{:S(2)}) %collective-permute-start.4) | collective-permute-done | bytes 524320 | tf_op jit(solution)/shard_map/ppermute | solution.py:30
  116.1 3.8 %collective-permute-done.18.refs_4_ = bf16[128,1024]{1,0:T(8,128)(2,1)S(1)} collective-permute-done((bf16[128,1024]{1,0:T(8,128)(2,1)S(1)}, bf16[128,1024]{1,0:T(8,128)(2,1)S(1)}, u32[]{:S(2)}, u32[]{:S(2)}) %collective-permute-start.18) | collective-permute-done | bytes 262176 | tf_op jit(solution)/shard_map/ppermute | solution.py:30
  121.2 4.3 %collective-permute-done.19.refs_5_ = bf16[128,1024]{1,0:T(8,128)(2,1)S(1)} collective-permute-done((bf16[128,1024]{1,0:T(8,128)(2,1)S(1)}, bf16[128,1024]{1,0:T(8,128)(2,1)S(1)}, u32[]{:S(2)}, u32[]{:S(2)}) %collective-permute-start.19) | collective-permute-done | bytes 262176 | tf_op jit(solution)/shard_map/ppermute | solution.py:30
  126.9 4.3 %collective-permute-done.30.refs_2_ = bf16[128,1024]{1,0:T(8,128)(2,1)S(1)} collective-permute-done((bf16[128,1024]{1,0:T(8,128)(2,1)S(1)}, bf16[128,1024]{1,0:T(8,128)(2,1)S(1)}, u32[]{:S(2)}, u32[]{:S(2)}) %collective-permute-start.30) | collective-permute-done | bytes 262176 | tf_op jit(solution)/shard_map/ppermute | solution.py:30
  132.5 6.0 %load_centroids.1 = (bf16[1536,2048]{1,0:T(8,128)(2,1)S(1)}, f32[1536,1]{1,0:T(8,128)S(1)}) custom-call(bf16[1536,2048]{1,0:T(8,128)(2,1)} %in_ref.1), custom_call_target="tpu_custom_call" | custom-call | tf_op jit(solution)/shard_map/load_centroids/pallas_call | solution.py:85
  140.1 3.7 %own_scores.4 = (bf16[1024,2048]{1,0:T(8,128)(2,1)S(1)}, f32[384,1024]{1,0:T(8,128)S(1)}, f32[8,1,128]{2,1,0:T(1,128)S(1)}) custom-call(s32[2]{0:T(128)S(1)} %pad_add_fusion.ids_ref, bf16[1536,2048]{1,0:T(8,128)(2,1)S(1)} %get-tuple-element.67.cents_ref.refs_13_.old_ref, f32[1536,1]{1,0:T(8,128)S(1)} %get-tuple-element.68.norm_ref, ...), custom_call_target="tpu_custom_call" | custom-call | tf_op jit(solution)/shard_map/own_scores/pallas_call | solution.py:156
  143.8 3.7 %own_scores.5 = (bf16[1024,2048]{1,0:T(8,128)(2,1)S(1)}, f32[384,1024]{1,0:T(8,128)S(1)}, f32[8,1,128]{2,1,0:T(1,128)S(1)}) custom-call(s32[2]{0:T(128)S(1)} %pad_add_fusion.ids_ref, bf16[1536,2048]{1,0:T(8,128)(2,1)S(1)} %get-tuple-element.67.cents_ref.refs_13_.old_ref, ...), custom_call_target="tpu_custom_call", output_to_operand_aliasing={{0}: (5, {}), {1}: (6, {}), {2}: (7, {})} | custom-call | tf_op jit(solution)/shard_map/own_scores/pallas_call | solution.py:156
  147.5 3.7 %own_scores.6 = (bf16[1024,2048]{1,0:T(8,128)(2,1)S(1)}, f32[384,1024]{1,0:T(8,128)S(1)}, f32[8,1,128]{2,1,0:T(1,128)S(1)}) custom-call(s32[2]{0:T(128)S(1)} %pad_add_fusion.ids_ref, bf16[1536,2048]{1,0:T(8,128)(2,1)S(1)} %get-tuple-element.67.cents_ref.refs_13_.old_ref, ...), custom_call_target="tpu_custom_call", output_to_operand_aliasing={{0}: (6, {}), {1}: (7, {}), {2}: (8, {})} | custom-call | tf_op jit(solution)/shard_map/own_scores/pallas_call | solution.py:156
  151.2 3.3 %own_scores.7 = (bf16[1024,2048]{1,0:T(8,128)(2,1)S(1)}, f32[384,1024]{1,0:T(8,128)S(1)}, f32[8,1,128]{2,1,0:T(1,128)S(1)}) custom-call(s32[2]{0:T(128)S(1)} %pad_add_fusion.ids_ref, bf16[1536,2048]{1,0:T(8,128)(2,1)S(1)} %get-tuple-element.67.cents_ref.refs_13_.old_ref, ...), custom_call_target="tpu_custom_call", output_to_operand_aliasing={{0}: (5, {}), {1}: (6, {}), {2}: (7, {})} | custom-call | tf_op jit(solution)/shard_map/own_scores/pallas_call | solution.py:156
  159.0 2.9 %collective-permute-start.34 = (f32[32,128]{1,0:T(8,128)S(1)}, f32[32,128]{1,0:T(8,128)S(1)}, u32[]{:S(2)}, u32[]{:S(2)}) collective-permute-start(f32[32,128]{1,0:T(8,128)S(1)} %constant_dynamic-update-slice_fusion.refs_0_), channel_id=1, source_target_pairs={{0,4},{1,5},{2,6},{3,7},{4,0},{5,1},{6,2},{7,3},{8,12},{9,13},{10,... | collective-permute-start | bytes 49160 | tf_op jit(solution)/shard_map/ppermute | solution.py:30
  174.3 10.2 %collective-permute-done.21.refs_1_ = bf16[128,2048]{1,0:T(8,128)(2,1)S(1)} collective-permute-done((bf16[128,2048]{1,0:T(8,128)(2,1)S(1)}, bf16[128,2048]{1,0:T(8,128)(2,1)S(1)}, u32[]{:S(2)}, u32[]{:S(2)}) %collective-permute-start.21) | collective-permute-done | bytes 524320 | tf_op jit(solution)/shard_map/ppermute | solution.py:30
  186.5 7.9 %collective-permute-done.23.refs_3_ = bf16[128,2048]{1,0:T(8,128)(2,1)S(1)} collective-permute-done((bf16[128,2048]{1,0:T(8,128)(2,1)S(1)}, bf16[128,2048]{1,0:T(8,128)(2,1)S(1)}, u32[]{:S(2)}, u32[]{:S(2)}) %collective-permute-start.23) | collective-permute-done | bytes 524320 | tf_op jit(solution)/shard_map/ppermute | solution.py:30
  197.0 7.9 %collective-permute-done.17.refs_3_ = bf16[128,2048]{1,0:T(8,128)(2,1)S(1)} collective-permute-done((bf16[128,2048]{1,0:T(8,128)(2,1)S(1)}, bf16[128,2048]{1,0:T(8,128)(2,1)S(1)}, u32[]{:S(2)}, u32[]{:S(2)}) %collective-permute-start.17) | collective-permute-done | bytes 524320 | tf_op jit(solution)/shard_map/ppermute | solution.py:30
  206.4 4.0 %side_scores.3 = (bf16[1024,2048]{1,0:T(8,128)(2,1)S(1)}, bf16[1024,2048]{1,0:T(8,128)(2,1)S(1)}, f32[576,1024]{1,0:T(8,128)S(1)}, f32[576,1024]{1,0:T(8,128)S(1)}) custom-call(s32[2]{0:T(128)S(1)} %pad_add_fusion.ids_ref, bf16[1536,2048]{1,0:T(8,128)(2,1)S(1)} %get-tuple-element.67.cents_ref.refs_13_.old_ref, f32[1536,1]{1,0:T(8,128)S(1)} %get-tuple-element.68.norm_ref, ...), custom_call_target="tpu_custom_call" | custom-call | tf_op jit(solution)/shard_map/side_scores/pallas_call | solution.py:303
  210.4 4.0 %side_scores.4 = (bf16[1024,2048]{1,0:T(8,128)(2,1)S(1)}, bf16[1024,2048]{1,0:T(8,128)(2,1)S(1)}, f32[576,1024]{1,0:T(8,128)S(1)}, f32[576,1024]{1,0:T(8,128)S(1)}) custom-call(s32[2]{0:T(128)S(1)} %pad_add_fusion.ids_ref, ...), custom_call_target="tpu_custom_call", output_to_operand_aliasing={{0}: (7, {}), {1}: (8, {}), {2}: (9, {}), {3}: (10, {})} | custom-call | tf_op jit(solution)/shard_map/side_scores/pallas_call | solution.py:303
  214.4 4.0 %side_scores.5 = (bf16[1024,2048]{1,0:T(8,128)(2,1)S(1)}, bf16[1024,2048]{1,0:T(8,128)(2,1)S(1)}, f32[576,1024]{1,0:T(8,128)S(1)}, f32[576,1024]{1,0:T(8,128)S(1)}) custom-call(s32[2]{0:T(128)S(1)} %pad_add_fusion.ids_ref, ...), custom_call_target="tpu_custom_call", output_to_operand_aliasing={{0}: (9, {}), {1}: (10, {}), {2}: (11, {}), {3}: (12, {})} | custom-call | tf_op jit(solution)/shard_map/side_scores/pallas_call | solution.py:303
  224.3 2.4 sent_sums.5
  234.0 13.7 %collective-permute-done.41 = f16[192,512]{1,0:T(8,128)(2,1)S(1)} collective-permute-done((f16[192,512]{1,0:T(8,128)(2,1)S(1)}, f16[192,512]{1,0:T(8,128)(2,1)S(1)}, u32[]{:S(2)}, u32[]{:S(2)}) %collective-permute-start.41) | collective-permute-done | bytes 196640 | tf_op jit(solution)/shard_map/ppermute | solution.py:30
  247.8 10.0 %own_sums.1 = (f32[384,2048]{1,0:T(8,128)S(1)}, f32[384,1]{1,0:T(8,128)S(1)}, f32[384,2048]{1,0:T(8,128)}, f32[384,1]{1,0:T(8,128)S(1)}, f32[384,1]{1,0:T(8,128)S(1)}) custom-call(s32[2]{0:T(128)S(1)} %pad_add_fusion.ids_ref, bf16[1024,2048]{1,0:T(8,128)(2,1)S(1)} %get-tuple-element.93.refs_0_, bf16[1024,2048]{1,0:T(8,128)(2,1)S(1)} %get-tuple-element.104.x_ref.refs_1_, ...), custom_call_target="tpu_custom_call" | custom-call | tf_op jit(solution)/shard_map/own_sums/pallas_call | solution.py:481
  258.0 2.4 update.2
  262.6 2.7 all-to-all-start
  266.0 6.4 %all-to-all-done = f32[32,1,128]{2,1,0:T(1,128)S(1)} async-done(((f32[32,1,128]{2,1,0:T(1,128)}), f32[32,1,128]{2,1,0:T(1,128)S(1)}, u32[]{:S(2)}, u32[]{:S(2)}) %all-to-all-start) | async-done | bytes 16416 | tf_op jit(solution)/shard_map/all_to_all | solution.py:691
  (103 shorter events, 64.4 us)
Async XLA Ops:
  8.6 30.5 %collective-permute-start.6 = (bf16[128,1024]{1,0:T(8,128)(2,1)S(1)}, bf16[128,1024]{1,0:T(8,128)(2,1)S(1)}, u32[]{:S(2)}, u32[]{:S(2)}) collective-permute-start(bf16[128,1024]{1,0:T(8,128)(2,1)S(1)} %get-tuple-element.76), channel_id=1, source_target_pairs={{0,7},{1,6},{2,5},{3,4},{4,3},{5,2},{6,1},{7,0},{8,15},{9,14},{10,... | collective-permute-start | bytes 786440 | tf_op jit(solution)/shard_map/ppermute | solution.py:30
  8.7 81.0 %collective-permute-start.9 = (bf16[128,2048]{1,0:T(8,128)(2,1)S(1)}, bf16[128,2048]{1,0:T(8,128)(2,1)S(1)}, u32[]{:S(2)}, u32[]{:S(2)}) collective-permute-start(bf16[128,2048]{1,0:T(8,128)(2,1)S(1)} %get-tuple-element.80), channel_id=1, source_target_pairs={{0,1},{1,0},{2,3},{3,2},{4,5},{5,4},{6,7},{7,6},{8,9},{9,8},{10,11... | collective-permute-start | bytes 1572872 | tf_op jit(solution)/shard_map/ppermute | solution.py:30
  9.1 51.2 %collective-permute-start.2 = (bf16[128,1024]{1,0:T(8,128)(2,1)S(1)}, bf16[128,1024]{1,0:T(8,128)(2,1)S(1)}, u32[]{:S(2)}, u32[]{:S(2)}) collective-permute-start(bf16[128,1024]{1,0:T(8,128)(2,1)S(1)} %get-tuple-element.72), channel_id=1, source_target_pairs={{0,4},{1,5},{2,6},{3,7},{4,0},{5,1},{6,2},{7,3},{8,12},{9,13},{10,... | collective-permute-start | bytes 786440 | tf_op jit(solution)/shard_map/ppermute | solution.py:30
  9.9 67.3 %collective-permute-start.3 = (bf16[128,1024]{1,0:T(8,128)(2,1)S(1)}, bf16[128,1024]{1,0:T(8,128)(2,1)S(1)}, u32[]{:S(2)}, u32[]{:S(2)}) collective-permute-start(bf16[128,1024]{1,0:T(8,128)(2,1)S(1)} %get-tuple-element.73), channel_id=1, source_target_pairs={{0,4},{1,5},{2,6},{3,7},{4,0},{5,1},{6,2},{7,3},{8,12},{9,13},{10,... | collective-permute-start | bytes 786440 | tf_op jit(solution)/shard_map/ppermute | solution.py:30
  15.4 67.4 %collective-permute-start = (bf16[128,1024]{1,0:T(8,128)(2,1)S(1)}, bf16[128,1024]{1,0:T(8,128)(2,1)S(1)}, u32[]{:S(2)}, u32[]{:S(2)}) collective-permute-start(bf16[128,1024]{1,0:T(8,128)(2,1)S(1)} %get-tuple-element.69), channel_id=1, source_target_pairs={{0,5},{1,4},{2,7},{3,6},{4,1},{5,0},{6,3},{7,2},{8,13},{9,12},{10,... | collective-permute-start | bytes 786440 | tf_op jit(solution)/shard_map/ppermute | solution.py:30
  39.1 49.3 %collective-permute-start.1 = (bf16[128,1024]{1,0:T(8,128)(2,1)S(1)}, bf16[128,1024]{1,0:T(8,128)(2,1)S(1)}, u32[]{:S(2)}, u32[]{:S(2)}) collective-permute-start(bf16[128,1024]{1,0:T(8,128)(2,1)S(1)} %get-tuple-element.70), channel_id=1, source_target_pairs={{0,5},{1,4},{2,7},{3,6},{4,1},{5,0},{6,3},{7,2},{8,13},{9,12},{10,... | collective-permute-start | bytes 786440 | tf_op jit(solution)/shard_map/ppermute | solution.py:30
  60.3 30.9 %collective-permute-start.7 = (bf16[128,2048]{1,0:T(8,128)(2,1)S(1)}, bf16[128,2048]{1,0:T(8,128)(2,1)S(1)}, u32[]{:S(2)}, u32[]{:S(2)}) collective-permute-start(bf16[128,2048]{1,0:T(8,128)(2,1)S(1)} %get-tuple-element.77), channel_id=1, source_target_pairs={{0,6},{1,7},{2,4},{3,5},{4,2},{5,3},{6,0},{7,1},{8,14},{9,15},{10,... | collective-permute-start | bytes 1572872 | tf_op jit(solution)/shard_map/ppermute | solution.py:30
  77.2 22.5 %collective-permute-start.8 = (bf16[128,2048]{1,0:T(8,128)(2,1)S(1)}, bf16[128,2048]{1,0:T(8,128)(2,1)S(1)}, u32[]{:S(2)}, u32[]{:S(2)}) collective-permute-start(bf16[128,2048]{1,0:T(8,128)(2,1)S(1)} %get-tuple-element.78), channel_id=1, source_target_pairs={{0,2},{1,3},{2,0},{3,1},{4,6},{5,7},{6,4},{7,5},{8,10},{9,11},{10,... | collective-permute-start | bytes 1572872 | tf_op jit(solution)/shard_map/ppermute | solution.py:30
  82.8 27.9 %collective-permute-start.4 = (bf16[128,2048]{1,0:T(8,128)(2,1)S(1)}, bf16[128,2048]{1,0:T(8,128)(2,1)S(1)}, u32[]{:S(2)}, u32[]{:S(2)}) collective-permute-start(bf16[128,2048]{1,0:T(8,128)(2,1)S(1)} %get-tuple-element.74), channel_id=1, source_target_pairs={{0,3},{1,2},{2,1},{3,0},{4,7},{5,6},{6,5},{7,4},{8,11},{9,10},{10,... | collective-permute-start | bytes 1572872 | tf_op jit(solution)/shard_map/ppermute | solution.py:30
  88.4 23.6 %collective-permute-start.24 = (bf16[128,2048]{1,0:T(8,128)(2,1)S(1)}, bf16[128,2048]{1,0:T(8,128)(2,1)S(1)}, u32[]{:S(2)}, u32[]{:S(2)}) collective-permute-start(bf16[128,2048]{1,0:T(8,128)(2,1)S(1)} %get-tuple-element.79.refs_0_), channel_id=1, source_target_pairs={{0,8},{8,0},{16,24},{24,16},{1,9},{9,1},{17,25},{25,17},{2,10},{10... | collective-permute-start | bytes 1572872 | tf_op jit(solution)/shard_map/ppermute | solution.py:30
  89.7 23.1 %collective-permute-start.26 = (bf16[128,2048]{1,0:T(8,128)(2,1)S(1)}, bf16[128,2048]{1,0:T(8,128)(2,1)S(1)}, u32[]{:S(2)}, u32[]{:S(2)}) collective-permute-start(bf16[128,2048]{1,0:T(8,128)(2,1)S(1)} %get-tuple-element.79.refs_0_), channel_id=1, source_target_pairs={{0,16},{8,24},{16,0},{24,8},{1,17},{9,25},{17,1},{25,9},{2,18},{10... | collective-permute-start | bytes 1572872 | tf_op jit(solution)/shard_map/ppermute | solution.py:30
  91.2 22.9 %collective-permute-start.15 = (bf16[128,1024]{1,0:T(8,128)(2,1)S(1)}, bf16[128,1024]{1,0:T(8,128)(2,1)S(1)}, u32[]{:S(2)}, u32[]{:S(2)}) collective-permute-start(bf16[128,1024]{1,0:T(8,128)(2,1)S(1)} %collective-permute-done.5.refs_1_), channel_id=1, source_target_pairs={{0,8},{8,0},{16,24},{24,16},{1,9},{9,1},{17,25},{25,17},{2,10},{10... | collective-permute-start | bytes 786440 | tf_op jit(solution)/shard_map/ppermute | solution.py:30
  112.8 18.4 %collective-permute-start.30 = (bf16[128,1024]{1,0:T(8,128)(2,1)S(1)}, bf16[128,1024]{1,0:T(8,128)(2,1)S(1)}, u32[]{:S(2)}, u32[]{:S(2)}) collective-permute-start(bf16[128,1024]{1,0:T(8,128)(2,1)S(1)} %collective-permute-done.rows_ref.a_ref), channel_id=1, source_target_pairs={{0,16},{8,24},{16,0},{24,8},{1,17},{9,25},{17,1},{25,9},{2,18},{10... | collective-permute-start | bytes 786440 | tf_op jit(solution)/shard_map/ppermute | solution.py:30
  114.1 42.7 %collective-permute-start.28 = (bf16[128,1024]{1,0:T(8,128)(2,1)S(1)}, bf16[128,1024]{1,0:T(8,128)(2,1)S(1)}, u32[]{:S(2)}, u32[]{:S(2)}) collective-permute-start(bf16[128,1024]{1,0:T(8,128)(2,1)S(1)} %collective-permute-done.2.refs_0_), channel_id=1, source_target_pairs={{0,16},{8,24},{16,0},{24,8},{1,17},{9,25},{17,1},{25,9},{2,18},{10... | collective-permute-start | bytes 786440 | tf_op jit(solution)/shard_map/ppermute | solution.py:30
  114.8 42.1 %collective-permute-start.29 = (bf16[128,1024]{1,0:T(8,128)(2,1)S(1)}, bf16[128,1024]{1,0:T(8,128)(2,1)S(1)}, u32[]{:S(2)}, u32[]{:S(2)}) collective-permute-start(bf16[128,1024]{1,0:T(8,128)(2,1)S(1)} %collective-permute-done.3.refs_1_), channel_id=1, source_target_pairs={{0,16},{8,24},{16,0},{24,8},{1,17},{9,25},{17,1},{25,9},{2,18},{10... | collective-permute-start | bytes 786440 | tf_op jit(solution)/shard_map/ppermute | solution.py:30
  119.9 49.5 %collective-permute-start.25 = (bf16[128,2048]{1,0:T(8,128)(2,1)S(1)}, bf16[128,2048]{1,0:T(8,128)(2,1)S(1)}, u32[]{:S(2)}, u32[]{:S(2)}) collective-permute-start(bf16[128,2048]{1,0:T(8,128)(2,1)S(1)} %collective-permute-done.9.refs_1_), channel_id=1, source_target_pairs={{0,8},{8,0},{16,24},{24,16},{1,9},{9,1},{17,25},{25,17},{2,10},{10... | collective-permute-start | bytes 1572872 | tf_op jit(solution)/shard_map/ppermute | solution.py:30
  125.6 33.5 %collective-permute-start.31 = (bf16[128,1024]{1,0:T(8,128)(2,1)S(1)}, bf16[128,1024]{1,0:T(8,128)(2,1)S(1)}, u32[]{:S(2)}, u32[]{:S(2)}) collective-permute-start(bf16[128,1024]{1,0:T(8,128)(2,1)S(1)} %collective-permute-done.1.b_ref), channel_id=1, source_target_pairs={{0,16},{8,24},{16,0},{24,8},{1,17},{9,25},{17,1},{25,9},{2,18},{10... | collective-permute-start | bytes 786440 | tf_op jit(solution)/shard_map/ppermute | solution.py:30
  131.2 27.8 %collective-permute-start.12 = (bf16[128,1024]{1,0:T(8,128)(2,1)S(1)}, bf16[128,1024]{1,0:T(8,128)(2,1)S(1)}, u32[]{:S(2)}, u32[]{:S(2)}) collective-permute-start(bf16[128,1024]{1,0:T(8,128)(2,1)S(1)} %collective-permute-done.rows_ref.a_ref), channel_id=1, source_target_pairs={{0,8},{8,0},{16,24},{24,16},{1,9},{9,1},{17,25},{25,17},{2,10},{10... | collective-permute-start | bytes 786440 | tf_op jit(solution)/shard_map/ppermute | solution.py:30
  165.2 19.3 %collective-permute-start.21 = (bf16[128,2048]{1,0:T(8,128)(2,1)S(1)}, bf16[128,2048]{1,0:T(8,128)(2,1)S(1)}, u32[]{:S(2)}, u32[]{:S(2)}) collective-permute-start(bf16[128,2048]{1,0:T(8,128)(2,1)S(1)} %collective-permute-done.8.refs_1_), channel_id=1, source_target_pairs={{0,8},{8,0},{16,24},{24,16},{1,9},{9,1},{17,25},{25,17},{2,10},{10... | collective-permute-start | bytes 1572872 | tf_op jit(solution)/shard_map/ppermute | solution.py:30
  168.3 16.7 %collective-permute-start.22 = (bf16[128,2048]{1,0:T(8,128)(2,1)S(1)}, bf16[128,2048]{1,0:T(8,128)(2,1)S(1)}, u32[]{:S(2)}, u32[]{:S(2)}) collective-permute-start(bf16[128,2048]{1,0:T(8,128)(2,1)S(1)} %collective-permute-done.7.refs_0_), channel_id=1, source_target_pairs={{0,16},{8,24},{16,0},{24,8},{1,17},{9,25},{17,1},{25,9},{2,18},{10... | collective-permute-start | bytes 1572872 | tf_op jit(solution)/shard_map/ppermute | solution.py:30
  169.4 24.9 %collective-permute-start.23 = (bf16[128,2048]{1,0:T(8,128)(2,1)S(1)}, bf16[128,2048]{1,0:T(8,128)(2,1)S(1)}, u32[]{:S(2)}, u32[]{:S(2)}) collective-permute-start(bf16[128,2048]{1,0:T(8,128)(2,1)S(1)} %collective-permute-done.8.refs_1_), channel_id=1, source_target_pairs={{0,16},{8,24},{16,0},{24,8},{1,17},{9,25},{17,1},{25,9},{2,18},{10... | collective-permute-start | bytes 1572872 | tf_op jit(solution)/shard_map/ppermute | solution.py:30
  171.8 24.7 %collective-permute-start.14 = (bf16[128,2048]{1,0:T(8,128)(2,1)S(1)}, bf16[128,2048]{1,0:T(8,128)(2,1)S(1)}, u32[]{:S(2)}, u32[]{:S(2)}) collective-permute-start(bf16[128,2048]{1,0:T(8,128)(2,1)S(1)} %collective-permute-done.4.refs_0_), channel_id=1, source_target_pairs={{0,8},{8,0},{16,24},{24,16},{1,9},{9,1},{17,25},{25,17},{2,10},{10... | collective-permute-start | bytes 1572872 | tf_op jit(solution)/shard_map/ppermute | solution.py:30
  173.2 31.7 %collective-permute-start.17 = (bf16[128,2048]{1,0:T(8,128)(2,1)S(1)}, bf16[128,2048]{1,0:T(8,128)(2,1)S(1)}, u32[]{:S(2)}, u32[]{:S(2)}) collective-permute-start(bf16[128,2048]{1,0:T(8,128)(2,1)S(1)} %collective-permute-done.4.refs_0_), channel_id=1, source_target_pairs={{0,16},{8,24},{16,0},{24,8},{1,17},{9,25},{17,1},{25,9},{2,18},{10... | collective-permute-start | bytes 1572872 | tf_op jit(solution)/shard_map/ppermute | solution.py:30
  184.5 36.1 %collective-permute-start.10 = (bf16[128,1024]{1,0:T(8,128)(2,1)S(1)}, bf16[128,1024]{1,0:T(8,128)(2,1)S(1)}, u32[]{:S(2)}, u32[]{:S(2)}) collective-permute-start(bf16[128,1024]{1,0:T(8,128)(2,1)S(1)} %collective-permute-done.2.refs_0_), channel_id=1, source_target_pairs={{0,8},{8,0},{16,24},{24,16},{1,9},{9,1},{17,25},{25,17},{2,10},{10... | collective-permute-start | bytes 786440 | tf_op jit(solution)/shard_map/ppermute | solution.py:30
  185.0 35.6 %collective-permute-start.11 = (bf16[128,1024]{1,0:T(8,128)(2,1)S(1)}, bf16[128,1024]{1,0:T(8,128)(2,1)S(1)}, u32[]{:S(2)}, u32[]{:S(2)}) collective-permute-start(bf16[128,1024]{1,0:T(8,128)(2,1)S(1)} %collective-permute-done.3.refs_1_), channel_id=1, source_target_pairs={{0,8},{8,0},{16,24},{24,16},{1,9},{9,1},{17,25},{25,17},{2,10},{10... | collective-permute-start | bytes 786440 | tf_op jit(solution)/shard_map/ppermute | solution.py:30
  194.4 26.2 %collective-permute-start.13 = (bf16[128,1024]{1,0:T(8,128)(2,1)S(1)}, bf16[128,1024]{1,0:T(8,128)(2,1)S(1)}, u32[]{:S(2)}, u32[]{:S(2)}) collective-permute-start(bf16[128,1024]{1,0:T(8,128)(2,1)S(1)} %collective-permute-done.1.b_ref), channel_id=1, source_target_pairs={{0,8},{8,0},{16,24},{24,16},{1,9},{9,1},{17,25},{25,17},{2,10},{10... | collective-permute-start | bytes 786440 | tf_op jit(solution)/shard_map/ppermute | solution.py:30
  196.5 26.4 %collective-permute-start.36 = (f32[8,128]{1,0:T(8,128)S(1)}, f32[8,128]{1,0:T(8,128)S(1)}, u32[]{:S(2)}, u32[]{:S(2)}) collective-permute-start(f32[8,128]{1,0:T(8,128)S(1)} %get-tuple-element.112.refs_6_), channel_id=1, source_target_pairs={{0,8},{8,0},{16,24},{24,16},{1,9},{9,1},{17,25},{25,17},{2,10},{10... | collective-permute-start | bytes 12296 | tf_op jit(solution)/shard_map/ppermute | solution.py:30
  204.9 17.9 %collective-permute-start.37 = (f32[8,128]{1,0:T(8,128)S(1)}, f32[8,128]{1,0:T(8,128)S(1)}, u32[]{:S(2)}, u32[]{:S(2)}) collective-permute-start(f32[8,128]{1,0:T(8,128)S(1)} %get-tuple-element.112.refs_6_), channel_id=1, source_target_pairs={{0,16},{8,24},{16,0},{24,8},{1,17},{9,25},{17,1},{25,9},{2,18},{10... | collective-permute-start | bytes 12296 | tf_op jit(solution)/shard_map/ppermute | solution.py:30
  226.8 31.1 %collective-permute-start.42 = (f16[192,1024]{1,0:T(8,128)(2,1)S(1)}, f16[192,1024]{1,0:T(8,128)(2,1)S(1)}, u32[]{:S(2)}, u32[]{:S(2)}) collective-permute-start(f16[192,1024]{1,0:T(8,128)(2,1)S(1)} %convert_element_type.44), channel_id=1, source_target_pairs={{0,8},{8,0},{16,24},{24,16},{1,9},{9,1},{17,25},{25,17},{2,10},{10... | collective-permute-start | bytes 1179656 | tf_op jit(solution)/shard_map/ppermute | solution.py:30
  228.4 29.6 %collective-permute-start.43 = (f16[192,1024]{1,0:T(8,128)(2,1)S(1)}, f16[192,1024]{1,0:T(8,128)(2,1)S(1)}, u32[]{:S(2)}, u32[]{:S(2)}) collective-permute-start(f16[192,1024]{1,0:T(8,128)(2,1)S(1)} %convert_element_type.46), channel_id=1, source_target_pairs={{0,16},{8,24},{16,0},{24,8},{1,17},{9,25},{17,1},{25,9},{2,18},{10... | collective-permute-start | bytes 1179656 | tf_op jit(solution)/shard_map/ppermute | solution.py:30
  230.9 16.8 %collective-permute-start.38 = (f16[192,640]{1,0:T(8,128)(2,1)S(1)}, f16[192,640]{1,0:T(8,128)(2,1)S(1)}, u32[]{:S(2)}, u32[]{:S(2)}) collective-permute-start(f16[192,640]{1,0:T(8,128)(2,1)S(1)} %convert_element_type.36), channel_id=1, source_target_pairs={{0,8},{8,0},{16,24},{24,16},{1,9},{9,1},{17,25},{25,17},{2,10},{10... | collective-permute-start | bytes 737288 | tf_op jit(solution)/shard_map/ppermute | solution.py:30
  231.7 16.0 %collective-permute-start.39 = (f16[192,640]{1,0:T(8,128)(2,1)S(1)}, f16[192,640]{1,0:T(8,128)(2,1)S(1)}, u32[]{:S(2)}, u32[]{:S(2)}) collective-permute-start(f16[192,640]{1,0:T(8,128)(2,1)S(1)} %convert_element_type.38), channel_id=1, source_target_pairs={{0,16},{8,24},{16,0},{24,8},{1,17},{9,25},{17,1},{25,9},{2,18},{10... | collective-permute-start | bytes 737288 | tf_op jit(solution)/shard_map/ppermute | solution.py:30
  (15 other events, 142.9 us)

commit v2 on v1

--- a/solution.py
+++ b/solution.py
@@ -318,26 +318,26 @@
     def body(ids_ref, cents_ref, norm_ref, *refs):
         rows_out, score_out = refs[len(refs) - 2 :]
 
-        @pl.when(pl.program_id(0) == 0)
-        def _():
-            keep(refs[:n_in], pieces, rows_out)
-
-        score_out[...] = sharpness * (2.0 * product(cents_ref, rows_out) - norm_ref[...])
-
-    def block(i, ids):
-        mine = ids[1]
+        keep(refs[:n_in], pieces, rows_out)
+        mine = ids_ref[1]
         other = 2 * (mine ^ 2) + 1 if bit == 1 else 2 * (mine ^ 1)
-        return (jnp.where(i < 2, 2 * mine + i, other), 0)
+        for first, block, count in ((0, 2 * mine, 2 * half), (2 * half, other, half)):
+            span = pl.ds(pl.multiple_of(block * half, half), count)
+            score = sharpness * (2.0 * product(cents_ref.at[span], rows_out) - norm_ref[span, :])
+            score_out[first : first + count, :] = score
 
     grid_spec = pltpu.PrefetchScalarGridSpec(
         num_scalar_prefetch=1,
-        grid=(3,),
-        in_specs=[pl.BlockSpec((half, feat), block), pl.BlockSpec((half, 1), block)]
+        grid=(1,),
+        in_specs=[
+            pl.BlockSpec(centroids.shape, lambda i, ids: (0, 0)),
+            pl.BlockSpec(cent_norm.shape, lambda i, ids: (0, 0)),
+        ]
         + [pl.BlockSpec(r.shape, lambda i, ids: (0, 0)) for r in rows]
         + [ANY] * 2,
         out_specs=[
             pl.BlockSpec((n_rows, feat), lambda i, ids: (at, 0)),
-            pl.BlockSpec((half, n_rows), lambda i, ids: (i, at)),
+            pl.BlockSpec((3 * half, n_rows), lambda i, ids: (0, at)),
         ],
     )
     return pl.pallas_call(
@@ -346,7 +346,7 @@
         grid_spec=grid_spec,
         input_output_aliases={3 + n_in + i: i for i in range(2)},
         name="one_side_scores",
-        compiler_params=pltpu.CompilerParams(vmem_limit_bytes=12 << 20),
+        compiler_params=pltpu.CompilerParams(vmem_limit_bytes=20 << 20),
     )(ids, *vmem(centroids), cent_norm, *rows, *state)
 
 
@@ -440,74 +440,37 @@
     )(*vmem(*side_rows, *side_score), *norms)
 
 
-def own_sums(ids, rows, scores, norms, parts, centroids, width, tile, done):
+def own_sums(rows, scores, norms, width, tile):
     n_rows, feat = rows[0].shape
-    half = width // 2
-
-    def body(ids_ref, *refs):
-        row_refs, score_refs, norm_refs = refs[:3], refs[3:6], refs[6:9]
-        part_refs, tail_refs, old_ref = refs[9:11], refs[11:13], refs[13]
-        out_ref, count_ref, new_ref, sent_ref, square_ref, w_buf = refs[14:]
-
+
+    def body(a_ref, b_ref, c_ref, as_ref, bs_ref, cs_ref, an_ref, bn_ref, cn_ref, out_ref, count_ref, w_buf):
         @pl.when(pl.program_id(0) == 0)
         def _():
             total = None
-            for i in range(3):
-                total = weights_of(score_refs[i], norm_refs[i], w_buf, i * n_rows, total)
+            for i, (s_ref, n_ref) in enumerate(((as_ref, an_ref), (bs_ref, bn_ref), (cs_ref, cn_ref))):
+                total = weights_of(s_ref, n_ref, w_buf, i * n_rows, total)
             count_ref[...] = jnp.sum(total, axis=1, keepdims=True)
 
-        acc = jnp.dot(w_buf[:, :n_rows], row_refs[0][...], preferred_element_type=F32)
-        acc += jnp.dot(w_buf[:, n_rows : 2 * n_rows], row_refs[1][...], preferred_element_type=F32)
-        acc += jnp.dot(w_buf[:, 2 * n_rows :], row_refs[2][...], preferred_element_type=F32)
+        acc = jnp.dot(w_buf[:, :n_rows], a_ref[...], preferred_element_type=F32)
+        acc += jnp.dot(w_buf[:, n_rows : 2 * n_rows], b_ref[...], preferred_element_type=F32)
+        acc += jnp.dot(w_buf[:, 2 * n_rows :], c_ref[...], preferred_element_type=F32)
         out_ref[...] = acc
 
-        @pl.when(pl.program_id(0) == done)
-        def _():
-            for i in range(2):
-                span = slice(i * half, (i + 1) * half)
-                lane = lax.broadcasted_iota(jnp.int32, (half, LANES), 1)
-                sent = jnp.sum(jnp.where(lane < 3, tail_refs[i][...], 0.0), axis=1, keepdims=True)
-                back = part_refs[i][...] * (jnp.maximum(sent, 2.0**-20) * 2.0**-10)
-                before = old_ref[span, :].astype(F32)
-                after = (out_ref[span, :] + back + before) / (count_ref[span, :] + sent + 1.0)
-                new_ref[span, :] = after
-                sent_ref[span, :] = sent
-                square_ref[span, :] = jnp.sum(jnp.square(after - before), axis=1, keepdims=True)
-
-    def whole(shape):
-        return pl.BlockSpec(shape, lambda i, ids: (0,) * len(shape))
-
-    thin = jax.ShapeDtypeStruct((width, 1), F32)
-    return pl.pallas_call(
-        body,
-        out_shape=[
-            pltpu.VMEM((width, feat), F32),
-            thin,
-            jax.ShapeDtypeStruct((width, feat), F32),
-            thin,
-            thin,
+    return pl.pallas_call(
+        body,
+        out_shape=[pltpu.VMEM((width, feat), F32), jax.ShapeDtypeStruct((width, 1), F32)],
+        grid=(feat // tile,),
+        in_specs=[pl.BlockSpec((n_rows, tile), lambda i: (0, i))] * 3
+        + [pl.BlockSpec((width, n_rows), lambda i: (0, 0))] * 3
+        + [pl.BlockSpec(norms[0].shape, lambda i: (0, 0))] * 3,
+        out_specs=[
+            pl.BlockSpec((width, tile), lambda i: (0, i)),
+            pl.BlockSpec((width, 1), lambda i: (0, 0)),
         ],
-        grid_spec=pltpu.PrefetchScalarGridSpec(
-            num_scalar_prefetch=1,
-            grid=(feat // tile,),
-            in_specs=[pl.BlockSpec((n_rows, tile), lambda i, ids: (0, i))] * 3
-            + [whole((width, n_rows))] * 3
-            + [whole(norms[0].shape)] * 3
-            + [whole((half, tile))] * 2
-            + [pl.BlockSpec((half, LANES), lambda i, ids: (0, tile // LANES))] * 2
-            + [pl.BlockSpec((width, tile), lambda i, ids: (ids[1], done))],
-            out_specs=[
-                pl.BlockSpec((width, tile), lambda i, ids: (0, i)),
-                whole((width, 1)),
-                pl.BlockSpec((width, tile), lambda i, ids: (0, done)),
-                whole((width, 1)),
-                whole((width, 1)),
-            ],
-            scratch_shapes=[pltpu.VMEM((width, 3 * n_rows), BF16)],
-        ),
+        scratch_shapes=[pltpu.VMEM((width, 3 * n_rows), BF16)],
         name="own_sums",
         compiler_params=pltpu.CompilerParams(vmem_limit_bytes=24 << 20),
-    )(ids, *vmem(*rows, *scores), *norms, *parts, *parts, *vmem(centroids))
+    )(*vmem(*rows, *scores), *norms)
 
 
 def update(ids, own, counts, parts, centroids, first, columns, state, final, n_devices):
@@ -515,64 +478,64 @@
     half = width // 2
     at = first // columns
 
-    def body(ids_ref, own_ref, count_ref, a_ref, b_ref, old_ref, sent_in, square_in, _, new_ref, *refs):
-        i = pl.program_id(0)
-
-        def finish(part_ref):
-            sent = sent_in[...]
+    def body(ids_ref, own_ref, count_ref, a_ref, b_ref, old_ref, *refs):
+        tails = refs[:2]
+        new_ref, *refs = refs[3:] + refs[:2] if final else refs[2:]
+        tops = []
+        for i, part_ref in enumerate((a_ref, b_ref)):
+            span = slice(i * half, (i + 1) * half)
+            if final:
+                sent, before_square = refs[2][span, :], refs[3][span, :]
+            else:
+                tail = tails[i]
+                lane = lax.broadcasted_iota(jnp.int32, (half, LANES), 1)
+                sent = jnp.sum(jnp.where(lane < 3, tail[...], 0.0), axis=1, keepdims=True)
+                before_square = 0.0
+                refs[1][span, :] = sent
             back = part_ref[...] * (jnp.maximum(sent, 2.0**-20) * 2.0**-10)
-            before = old_ref[...].astype(F32)
-            after = (own_ref[...] + back + before) / (count_ref[...] + sent + 1.0)
-            new_ref[...] = after
-            total = square_in[...] + jnp.sum(jnp.square(after - before), axis=1, keepdims=True)
-            if not final:
-                refs[0][...] = total
-                return
-            move_ref, peak_ref = refs
-            move = jnp.sqrt(total + 1.0)
-            move_ref[...] = move
-            top = jnp.broadcast_to(jnp.max(move, axis=0, keepdims=True), peak_ref.shape)
-            peak_ref[...] = jnp.where(i == 0, top, jnp.maximum(top, peak_ref[...]))
-
-        @pl.when(i == 0)
-        def _():
-            finish(a_ref)
-
-        @pl.when(i == 1)
-        def _():
-            finish(b_ref)
-
-    column = pl.BlockSpec((half, 1), lambda i, ids: (i, 0))
-    block = pl.BlockSpec((half, columns), lambda i, ids: (i, at))
+            before = old_ref[span, :].astype(F32)
+            after = (own_ref[span, :] + back + before) / (count_ref[span, :] + sent + 1.0)
+            new_ref[span, :] = after
+            total = before_square + jnp.sum(jnp.square(after - before), axis=1, keepdims=True)
+            if final:
+                total = jnp.sqrt(total + 1.0)
+                tops.append(jnp.max(total, axis=0, keepdims=True))
+            refs[0][span, :] = total
+        if final:
+            refs[1][...] = jnp.broadcast_to(jnp.maximum(*tops), refs[1].shape)
+
+    def whole(shape):
+        return pl.BlockSpec(shape, lambda i, ids: (0, 0))
+
+    block = pl.BlockSpec((width, columns), lambda i, ids: (0, at))
     thin = jax.ShapeDtypeStruct((width, 1), F32)
-    new, sent, square = state
     out_shape = [jax.ShapeDtypeStruct((width, feat), F32), thin]
-    out_specs = [block, column]
+    out_specs = [block, whole((width, 1))]
     if final:
+        new, square, sent = state
+        extra, extra_specs = [sent, square, new], [whole((width, 1))] * 2 + [ANY]
         out_shape.append(jax.ShapeDtypeStruct((n_devices, LANES), F32))
-        out_specs.append(pl.BlockSpec((n_devices, LANES), lambda i, ids: (0, 0)))
+        out_specs.append(whole((n_devices, LANES)))
+    else:
+        extra, extra_specs = parts, [pl.BlockSpec((half, LANES), lambda i, ids: (0, columns // LANES))] * 2
+        out_shape.append(thin)
+        out_specs.append(whole((width, 1)))
     return pl.pallas_call(
         body,
         out_shape=out_shape,
         grid_spec=pltpu.PrefetchScalarGridSpec(
             num_scalar_prefetch=1,
-            grid=(2,),
-            in_specs=[
-                block,
-                column,
-                pl.BlockSpec((half, columns), lambda i, ids: (0, 0)),
-                pl.BlockSpec((half, columns), lambda i, ids: (0, 0)),
-                pl.BlockSpec((half, columns), lambda i, ids: (2 * ids[1] + i, at)),
-                column,
-                column,
-                ANY,
-            ],
+            grid=(1,),
+            in_specs=[block, whole((width, 1))]
+            + [whole((half, columns))] * 2
+            + [pl.BlockSpec((width, columns), lambda i, ids: (ids[1], at))]
+            + extra_specs,
             out_specs=out_specs,
         ),
-        input_output_aliases={8: 0},
+        input_output_aliases={8: 0} if final else {},
         name="update",
-        compiler_params=pltpu.CompilerParams(vmem_limit_bytes=10 << 20),
-    )(ids, *vmem(own), counts, *parts, *vmem(centroids), sent, square, new)
+        compiler_params=pltpu.CompilerParams(vmem_limit_bytes=16 << 20),
+    )(ids, *vmem(own), counts, *parts, *vmem(centroids), *extra)
 
 
 def sequence(n_mp):
@@ -663,7 +626,7 @@
         side_norm.append(swap(slot_norm, "dp", n_dp, bit))
 
     tile = feat // 4
-    spans = [(3 * tile, tile), (0, 2 * tile), (2 * tile, tile)]
+    spans = [(0, 2 * tile), (2 * tile, 2 * tile)]
     received = []
     for i, (first, columns) in enumerate(spans):
         sent = sent_sums(sides[:2], sides[2:], side_norm, half, first, columns, tile, i == 0)
@@ -672,22 +635,13 @@
         for bit, message in ((1, for_x), (2, for_y)):
             pair.append(swap(message, "dp", n_dp, bit).astype(F32))
         received.append(pair)
-    total, counts, updated, sent, square = own_sums(
-        ids,
-        [own[0], sides[0], sides[1]],
-        [own[1], sides[2], sides[3]],
-        [slot_norm] + side_norm,
-        received[0],
-        cents,
-        own_width,
-        tile,
-        spans[0][0] // tile,
-    )
-    for i, (first, columns) in list(enumerate(spans))[1:]:
-        updated, square, *peak = update(
-            ids, total, counts, received[i], cents, first, columns, [updated, sent, square], i == 2, n_dp * n_mp
-        )
-    movement, peak = square, peak[0]
+    total, counts = own_sums(
+        [own[0], sides[0], sides[1]], [own[1], sides[2], sides[3]], [slot_norm] + side_norm, own_width, tile
+    )
+    state = None
+    for i, (first, columns) in enumerate(spans):
+        state = update(ids, total, counts, received[i], cents, first, columns, state, i == len(spans) - 1, n_dp * n_mp)
+    updated, movement, peak = state
     shard_peaks = lax.all_to_all(peak, ("dp", "mp"), split_axis=0, concat_axis=0, tiled=True)
     shard_peak = jnp.max(shard_peaks.reshape(n_dp, n_mp, LANES), axis=(0, 2))
     new_lower = lower_bound - shard_peak[:, None]

time: 274 us -> 261 us (0.953)
  waiting for transfers between devices: 118 us -> 109 us
  Pallas kernels: 65.3 us -> 62.1 us
    ppermute x44 -> x42, waiting for transfers between devices: 112 us -> 103 us  [swap(): return lax.ppermute(value, axis, [(i, i ^ offset) for i in range(size)])]
    ppermute x44 -> x42, starting transfers between devices: 83.2 us -> 81.7 us  [swap(): return lax.ppermute(value, axis, [(i, i ^ offset) for i in range(size)])]
  transfers between devices with their start and end apart: 45 -> 43, of which waited for: 19 -> 20; matrix products, arithmetic and copies ran while one was open for 0% -> 0% of each run, Pallas kernels for 21% -> 20%
where the time goes in v2:
time: 261 us
  waiting for transfers between devices  109 us (42%)
  starting transfers between devices  85.6 us (33%)
  Pallas kernels  62.1 us (24%)
    ppermute x42, waiting for transfers between devices, swap(): return lax.ppermute(value, axis, [(i, i ^ offset) for i in range(size)])  103 us
    ppermute x42, starting transfers between devices, swap(): return lax.ppermute(value, axis, [(i, i ^ offset) for i in range(size)])  81.7 us
    pallas_call x4, Pallas kernels, own_scores(): pl.pallas_call(body, out_shape=[pltpu.VMEM(v.shape, v.dtype) for v in sta...  14.3 us
    pallas_call x3, Pallas kernels, side_scores(): pl.pallas_call(body, out_shape=[pltpu.VMEM(v.shape, v.dtype) for v in sta...  12 us
    pallas_call x1, Pallas kernels, own_sums(): pl.pallas_call(body, out_shape=[pltpu.VMEM((width, feat), F32), jax.Shape...  7.9 us
    all_to_all x1, waiting for transfers between devices, on_square(): lax.all_to_all(peak, ('dp', 'mp'), split_axis=0, concat_axis=0, tiled=True)  6.37 us
    pallas_call x1, Pallas kernels, load_centroids(): pl.pallas_call(body, out_shape=[pltpu.VMEM((width, feat), centroids.dtype...  5.97 us
    pallas_call x2, Pallas kernels, sent_sums(): pl.pallas_call(body, out_shape=[jax.ShapeDtypeStruct((half, width), F32)]...  5.29 us
  transfers between devices with their start and end apart: 43, of which 20 were waited for; matrix products, arithmetic and copies ran while one was open for 0% of the time, Pallas kernels for 20%

profile of v2, /device:TPU:0, one launch (start us, length us, event | category | flops | bytes accessed | tf_op | source)
XLA Modules:
  0.0 261.1 jit_solution(15482287054953701502)
XLA Ops:
  3.7 4.9 %collective-permute-start.5 = (bf16[128,1024]{1,0:T(8,128)(2,1)S(1)}, bf16[128,1024]{1,0:T(8,128)(2,1)S(1)}, u32[]{:S(2)}, u32[]{:S(2)}) collective-permute-start(bf16[128,1024]{1,0:T(8,128)(2,1)S(1)} %get-tuple-element.71), channel_id=1, source_target_pairs={{0,7},{1,6},{2,5},{3,4},{4,3},{5,2},{6,1},{7,0},{8,15},{9,14},{10,... | collective-permute-start | bytes 786440 | tf_op jit(solution)/shard_map/ppermute | solution.py:30
  12.0 3.3 %collective-permute-done.5.refs_1_ = bf16[128,1024]{1,0:T(8,128)(2,1)S(1)} collective-permute-done((bf16[128,1024]{1,0:T(8,128)(2,1)S(1)}, bf16[128,1024]{1,0:T(8,128)(2,1)S(1)}, u32[]{:S(2)}, u32[]{:S(2)}) %collective-permute-start.5) | collective-permute-done | bytes 262176 | tf_op jit(solution)/shard_map/ppermute | solution.py:30
  15.4 23.7 %collective-permute-start = (bf16[128,1024]{1,0:T(8,128)(2,1)S(1)}, bf16[128,1024]{1,0:T(8,128)(2,1)S(1)}, u32[]{:S(2)}, u32[]{:S(2)}) collective-permute-start(bf16[128,1024]{1,0:T(8,128)(2,1)S(1)} %get-tuple-element.65), channel_id=1, source_target_pairs={{0,5},{1,4},{2,7},{3,6},{4,1},{5,0},{6,3},{7,2},{8,13},{9,12},{10,... | collective-permute-start | bytes 786440 | tf_op jit(solution)/shard_map/ppermute | solution.py:30
  39.1 10.9 %collective-permute-start.1 = (bf16[128,1024]{1,0:T(8,128)(2,1)S(1)}, bf16[128,1024]{1,0:T(8,128)(2,1)S(1)}, u32[]{:S(2)}, u32[]{:S(2)}) collective-permute-start(bf16[128,1024]{1,0:T(8,128)(2,1)S(1)} %get-tuple-element.66), channel_id=1, source_target_pairs={{0,5},{1,4},{2,7},{3,6},{4,1},{5,0},{6,3},{7,2},{8,13},{9,12},{10,... | collective-permute-start | bytes 786440 | tf_op jit(solution)/shard_map/ppermute | solution.py:30
  52.2 8.2 %collective-permute-done.2.refs_0_ = bf16[128,1024]{1,0:T(8,128)(2,1)S(1)} collective-permute-done((bf16[128,1024]{1,0:T(8,128)(2,1)S(1)}, bf16[128,1024]{1,0:T(8,128)(2,1)S(1)}, u32[]{:S(2)}, u32[]{:S(2)}) %collective-permute-start.2) | collective-permute-done | bytes 262176 | tf_op jit(solution)/shard_map/ppermute | solution.py:30
  60.3 2.5 collective-permute-start.7
  62.8 14.4 %collective-permute-done.3.refs_1_ = bf16[128,1024]{1,0:T(8,128)(2,1)S(1)} collective-permute-done((bf16[128,1024]{1,0:T(8,128)(2,1)S(1)}, bf16[128,1024]{1,0:T(8,128)(2,1)S(1)}, u32[]{:S(2)}, u32[]{:S(2)}) %collective-permute-start.3) | collective-permute-done | bytes 262176 | tf_op jit(solution)/shard_map/ppermute | solution.py:30
  77.2 5.6 %collective-permute-done.rows_ref.a_ref = bf16[128,1024]{1,0:T(8,128)(2,1)S(1)} collective-permute-done((bf16[128,1024]{1,0:T(8,128)(2,1)S(1)}, bf16[128,1024]{1,0:T(8,128)(2,1)S(1)}, u32[]{:S(2)}, u32[]{:S(2)}) %collective-permute-start) | collective-permute-done | bytes 262176 | tf_op jit(solution)/shard_map/ppermute | solution.py:30
  82.8 5.6 %collective-permute-done.1.b_ref = bf16[128,1024]{1,0:T(8,128)(2,1)S(1)} collective-permute-done((bf16[128,1024]{1,0:T(8,128)(2,1)S(1)}, bf16[128,1024]{1,0:T(8,128)(2,1)S(1)}, u32[]{:S(2)}, u32[]{:S(2)}) %collective-permute-start.1) | collective-permute-done | bytes 262176 | tf_op jit(solution)/shard_map/ppermute | solution.py:30
  91.7 8.0 %collective-permute-done.8.refs_1_ = bf16[128,2048]{1,0:T(8,128)(2,1)S(1)} collective-permute-done((bf16[128,2048]{1,0:T(8,128)(2,1)S(1)}, bf16[128,2048]{1,0:T(8,128)(2,1)S(1)}, u32[]{:S(2)}, u32[]{:S(2)}) %collective-permute-start.8) | collective-permute-done | bytes 524320 | tf_op jit(solution)/shard_map/ppermute | solution.py:30
  101.0 9.8 %collective-permute-done.4.refs_0_ = bf16[128,2048]{1,0:T(8,128)(2,1)S(1)} collective-permute-done((bf16[128,2048]{1,0:T(8,128)(2,1)S(1)}, bf16[128,2048]{1,0:T(8,128)(2,1)S(1)}, u32[]{:S(2)}, u32[]{:S(2)}) %collective-permute-start.4) | collective-permute-done | bytes 524320 | tf_op jit(solution)/shard_map/ppermute | solution.py:30
  116.1 3.8 %collective-permute-done.18.refs_4_ = bf16[128,1024]{1,0:T(8,128)(2,1)S(1)} collective-permute-done((bf16[128,1024]{1,0:T(8,128)(2,1)S(1)}, bf16[128,1024]{1,0:T(8,128)(2,1)S(1)}, u32[]{:S(2)}, u32[]{:S(2)}) %collective-permute-start.18) | collective-permute-done | bytes 262176 | tf_op jit(solution)/shard_map/ppermute | solution.py:30
  121.2 4.3 %collective-permute-done.19.refs_5_ = bf16[128,1024]{1,0:T(8,128)(2,1)S(1)} collective-permute-done((bf16[128,1024]{1,0:T(8,128)(2,1)S(1)}, bf16[128,1024]{1,0:T(8,128)(2,1)S(1)}, u32[]{:S(2)}, u32[]{:S(2)}) %collective-permute-start.19) | collective-permute-done | bytes 262176 | tf_op jit(solution)/shard_map/ppermute | solution.py:30
  126.9 4.3 %collective-permute-done.30.refs_2_ = bf16[128,1024]{1,0:T(8,128)(2,1)S(1)} collective-permute-done((bf16[128,1024]{1,0:T(8,128)(2,1)S(1)}, bf16[128,1024]{1,0:T(8,128)(2,1)S(1)}, u32[]{:S(2)}, u32[]{:S(2)}) %collective-permute-start.30) | collective-permute-done | bytes 262176 | tf_op jit(solution)/shard_map/ppermute | solution.py:30
  132.5 6.0 %load_centroids.1 = (bf16[1536,2048]{1,0:T(8,128)(2,1)S(1)}, f32[1536,1]{1,0:T(8,128)S(1)}) custom-call(bf16[1536,2048]{1,0:T(8,128)(2,1)} %in_ref.1), custom_call_target="tpu_custom_call" | custom-call | tf_op jit(solution)/shard_map/load_centroids/pallas_call | solution.py:85
  140.1 3.7 %own_scores.4 = (bf16[1024,2048]{1,0:T(8,128)(2,1)S(1)}, f32[384,1024]{1,0:T(8,128)S(1)}, f32[8,1,128]{2,1,0:T(1,128)S(1)}) custom-call(s32[2]{0:T(128)S(1)} %pad_add_fusion.ids_ref, bf16[1536,2048]{1,0:T(8,128)(2,1)S(1)} %get-tuple-element.63.cents_ref.old_ref, f32[1536,1]{1,0:T(8,128)S(1)} %get-tuple-element.64.norm_ref, ...), custom_call_target="tpu_custom_call" | custom-call | tf_op jit(solution)/shard_map/own_scores/pallas_call | solution.py:156
  143.8 3.7 %own_scores.5 = (bf16[1024,2048]{1,0:T(8,128)(2,1)S(1)}, f32[384,1024]{1,0:T(8,128)S(1)}, f32[8,1,128]{2,1,0:T(1,128)S(1)}) custom-call(s32[2]{0:T(128)S(1)} %pad_add_fusion.ids_ref, bf16[1536,2048]{1,0:T(8,128)(2,1)S(1)} %get-tuple-element.63.cents_ref.old_ref, ...), custom_call_target="tpu_custom_call", output_to_operand_aliasing={{0}: (5, {}), {1}: (6, {}), {2}: (7, {})} | custom-call | tf_op jit(solution)/shard_map/own_scores/pallas_call | solution.py:156
  147.5 3.7 %own_scores.6 = (bf16[1024,2048]{1,0:T(8,128)(2,1)S(1)}, f32[384,1024]{1,0:T(8,128)S(1)}, f32[8,1,128]{2,1,0:T(1,128)S(1)}) custom-call(s32[2]{0:T(128)S(1)} %pad_add_fusion.ids_ref, bf16[1536,2048]{1,0:T(8,128)(2,1)S(1)} %get-tuple-element.63.cents_ref.old_ref, ...), custom_call_target="tpu_custom_call", output_to_operand_aliasing={{0}: (6, {}), {1}: (7, {}), {2}: (8, {})} | custom-call | tf_op jit(solution)/shard_map/own_scores/pallas_call | solution.py:156
  151.2 3.3 %own_scores.7 = (bf16[1024,2048]{1,0:T(8,128)(2,1)S(1)}, f32[384,1024]{1,0:T(8,128)S(1)}, f32[8,1,128]{2,1,0:T(1,128)S(1)}) custom-call(s32[2]{0:T(128)S(1)} %pad_add_fusion.ids_ref, bf16[1536,2048]{1,0:T(8,128)(2,1)S(1)} %get-tuple-element.63.cents_ref.old_ref, ...), custom_call_target="tpu_custom_call", output_to_operand_aliasing={{0}: (5, {}), {1}: (6, {}), {2}: (7, {})} | custom-call | tf_op jit(solution)/shard_map/own_scores/pallas_call | solution.py:156
  159.1 2.9 %collective-permute-start.34 = (f32[32,128]{1,0:T(8,128)S(1)}, f32[32,128]{1,0:T(8,128)S(1)}, u32[]{:S(2)}, u32[]{:S(2)}) collective-permute-start(f32[32,128]{1,0:T(8,128)S(1)} %constant_dynamic-update-slice_fusion.refs_0_), channel_id=1, source_target_pairs={{0,4},{1,5},{2,6},{3,7},{4,0},{5,1},{6,2},{7,3},{8,12},{9,13},{10,... | collective-permute-start | bytes 49160 | tf_op jit(solution)/shard_map/ppermute | solution.py:30
  174.3 10.2 %collective-permute-done.21.refs_1_ = bf16[128,2048]{1,0:T(8,128)(2,1)S(1)} collective-permute-done((bf16[128,2048]{1,0:T(8,128)(2,1)S(1)}, bf16[128,2048]{1,0:T(8,128)(2,1)S(1)}, u32[]{:S(2)}, u32[]{:S(2)}) %collective-permute-start.21) | collective-permute-done | bytes 524320 | tf_op jit(solution)/shard_map/ppermute | solution.py:30
  186.5 7.9 %collective-permute-done.23.refs_3_ = bf16[128,2048]{1,0:T(8,128)(2,1)S(1)} collective-permute-done((bf16[128,2048]{1,0:T(8,128)(2,1)S(1)}, bf16[128,2048]{1,0:T(8,128)(2,1)S(1)}, u32[]{:S(2)}, u32[]{:S(2)}) %collective-permute-start.23) | collective-permute-done | bytes 524320 | tf_op jit(solution)/shard_map/ppermute | solution.py:30
  197.1 7.9 %collective-permute-done.17.refs_3_ = bf16[128,2048]{1,0:T(8,128)(2,1)S(1)} collective-permute-done((bf16[128,2048]{1,0:T(8,128)(2,1)S(1)}, bf16[128,2048]{1,0:T(8,128)(2,1)S(1)}, u32[]{:S(2)}, u32[]{:S(2)}) %collective-permute-start.17) | collective-permute-done | bytes 524320 | tf_op jit(solution)/shard_map/ppermute | solution.py:30
  206.4 4.0 %side_scores.3 = (bf16[1024,2048]{1,0:T(8,128)(2,1)S(1)}, bf16[1024,2048]{1,0:T(8,128)(2,1)S(1)}, f32[576,1024]{1,0:T(8,128)S(1)}, f32[576,1024]{1,0:T(8,128)S(1)}) custom-call(s32[2]{0:T(128)S(1)} %pad_add_fusion.ids_ref, bf16[1536,2048]{1,0:T(8,128)(2,1)S(1)} %get-tuple-element.63.cents_ref.old_ref, f32[1536,1]{1,0:T(8,128)S(1)} %get-tuple-element.64.norm_ref, ...), custom_call_target="tpu_custom_call" | custom-call | tf_op jit(solution)/shard_map/side_scores/pallas_call | solution.py:303
  210.4 4.0 %side_scores.4 = (bf16[1024,2048]{1,0:T(8,128)(2,1)S(1)}, bf16[1024,2048]{1,0:T(8,128)(2,1)S(1)}, f32[576,1024]{1,0:T(8,128)S(1)}, f32[576,1024]{1,0:T(8,128)S(1)}) custom-call(s32[2]{0:T(128)S(1)} %pad_add_fusion.ids_ref, ...), custom_call_target="tpu_custom_call", output_to_operand_aliasing={{0}: (7, {}), {1}: (8, {}), {2}: (9, {}), {3}: (10, {})} | custom-call | tf_op jit(solution)/shard_map/side_scores/pallas_call | solution.py:303
  214.4 4.0 %side_scores.5 = (bf16[1024,2048]{1,0:T(8,128)(2,1)S(1)}, bf16[1024,2048]{1,0:T(8,128)(2,1)S(1)}, f32[576,1024]{1,0:T(8,128)S(1)}, f32[576,1024]{1,0:T(8,128)S(1)}) custom-call(s32[2]{0:T(128)S(1)} %pad_add_fusion.ids_ref, ...), custom_call_target="tpu_custom_call", output_to_operand_aliasing={{0}: (9, {}), {1}: (10, {}), {2}: (11, {}), {3}: (12, {})} | custom-call | tf_op jit(solution)/shard_map/side_scores/pallas_call | solution.py:303
  221.4 2.7 %sent_sums.3 = (f32[192,1152]{1,0:T(8,128)S(1)}, f32[192,1152]{1,0:T(8,128)S(1)}) custom-call(bf16[1024,2048]{1,0:T(8,128)(2,1)S(1)} %get-tuple-element.100.b_ref.x_ref, bf16[1024,2048]{1,0:T(8,128)(2,1)S(1)} %get-tuple-element.103.c_ref.y_ref, f32[576,1024]{1,0:T(8,128)S(1)} %get-tuple-element.105.bs_ref.xs_ref, ...), custom_call_target="tpu_custom_call" | custom-call | tf_op jit(solution)/shard_map/sent_sums/pallas_call | solution.py:431
  225.7 2.5 sent_sums.2
  231.3 7.9 %own_sums.1 = (f32[384,2048]{1,0:T(8,128)S(1)}, f32[384,1]{1,0:T(8,128)S(1)}) custom-call(bf16[1024,2048]{1,0:T(8,128)(2,1)S(1)} %get-tuple-element.89.a_ref, bf16[1024,2048]{1,0:T(8,128)(2,1)S(1)} %get-tuple-element.100.b_ref.x_ref, bf16[1024,2048]{1,0:T(8,128)(2,1)S(1)} %get-tuple-element.103.c_ref.y_ref, f32[384,1024]{1,0:T(8,128)S(1)} %get-tuple-element.104.as_ref, ...), custom_call_target="tpu_custom_call" | custom-call | tf_op jit(solution)/shard_map/own_sums/pallas_call | solution.py:459
  239.2 4.9 %collective-permute-done.38 = f16[192,1024]{1,0:T(8,128)(2,1)S(1)} collective-permute-done((f16[192,1024]{1,0:T(8,128)(2,1)S(1)}, f16[192,1024]{1,0:T(8,128)(2,1)S(1)}, u32[]{:S(2)}, u32[]{:S(2)}) %collective-permute-start.38) | collective-permute-done | bytes 393248 | tf_op jit(solution)/shard_map/ppermute | solution.py:30
  249.0 3.8 %all-to-all-start = ((f32[32,1,128]{2,1,0:T(1,128)}), f32[32,1,128]{2,1,0:T(1,128)S(1)}, u32[]{:S(2)}, u32[]{:S(2)}) async-start(f32[32,1,128]{2,1,0:T(1,128)} %bitcast.5), calls=%async_computation | async-start | bytes 32768 | tf_op jit(solution)/shard_map/all_to_all | solution.py:645
  253.6 6.4 %all-to-all-done = f32[32,1,128]{2,1,0:T(1,128)S(1)} async-done(((f32[32,1,128]{2,1,0:T(1,128)}), f32[32,1,128]{2,1,0:T(1,128)S(1)}, u32[]{:S(2)}, u32[]{:S(2)}) %all-to-all-start) | async-done | bytes 16416 | tf_op jit(solution)/shard_map/all_to_all | solution.py:645
  (94 shorter events, 61.4 us)
Async XLA Ops:
  8.6 30.5 %collective-permute-start.6 = (bf16[128,1024]{1,0:T(8,128)(2,1)S(1)}, bf16[128,1024]{1,0:T(8,128)(2,1)S(1)}, u32[]{:S(2)}, u32[]{:S(2)}) collective-permute-start(bf16[128,1024]{1,0:T(8,128)(2,1)S(1)} %get-tuple-element.72), channel_id=1, source_target_pairs={{0,7},{1,6},{2,5},{3,4},{4,3},{5,2},{6,1},{7,0},{8,15},{9,14},{10,... | collective-permute-start | bytes 786440 | tf_op jit(solution)/shard_map/ppermute | solution.py:30
  8.7 81.0 %collective-permute-start.9 = (bf16[128,2048]{1,0:T(8,128)(2,1)S(1)}, bf16[128,2048]{1,0:T(8,128)(2,1)S(1)}, u32[]{:S(2)}, u32[]{:S(2)}) collective-permute-start(bf16[128,2048]{1,0:T(8,128)(2,1)S(1)} %get-tuple-element.76), channel_id=1, source_target_pairs={{0,1},{1,0},{2,3},{3,2},{4,5},{5,4},{6,7},{7,6},{8,9},{9,8},{10,11... | collective-permute-start | bytes 1572872 | tf_op jit(solution)/shard_map/ppermute | solution.py:30
  9.1 51.2 %collective-permute-start.2 = (bf16[128,1024]{1,0:T(8,128)(2,1)S(1)}, bf16[128,1024]{1,0:T(8,128)(2,1)S(1)}, u32[]{:S(2)}, u32[]{:S(2)}) collective-permute-start(bf16[128,1024]{1,0:T(8,128)(2,1)S(1)} %get-tuple-element.68), channel_id=1, source_target_pairs={{0,4},{1,5},{2,6},{3,7},{4,0},{5,1},{6,2},{7,3},{8,12},{9,13},{10,... | collective-permute-start | bytes 786440 | tf_op jit(solution)/shard_map/ppermute | solution.py:30
  9.9 67.3 %collective-permute-start.3 = (bf16[128,1024]{1,0:T(8,128)(2,1)S(1)}, bf16[128,1024]{1,0:T(8,128)(2,1)S(1)}, u32[]{:S(2)}, u32[]{:S(2)}) collective-permute-start(bf16[128,1024]{1,0:T(8,128)(2,1)S(1)} %get-tuple-element.69), channel_id=1, source_target_pairs={{0,4},{1,5},{2,6},{3,7},{4,0},{5,1},{6,2},{7,3},{8,12},{9,13},{10,... | collective-permute-start | bytes 786440 | tf_op jit(solution)/shard_map/ppermute | solution.py:30
  15.4 67.4 %collective-permute-start = (bf16[128,1024]{1,0:T(8,128)(2,1)S(1)}, bf16[128,1024]{1,0:T(8,128)(2,1)S(1)}, u32[]{:S(2)}, u32[]{:S(2)}) collective-permute-start(bf16[128,1024]{1,0:T(8,128)(2,1)S(1)} %get-tuple-element.65), channel_id=1, source_target_pairs={{0,5},{1,4},{2,7},{3,6},{4,1},{5,0},{6,3},{7,2},{8,13},{9,12},{10,... | collective-permute-start | bytes 786440 | tf_op jit(solution)/shard_map/ppermute | solution.py:30
  39.1 49.3 %collective-permute-start.1 = (bf16[128,1024]{1,0:T(8,128)(2,1)S(1)}, bf16[128,1024]{1,0:T(8,128)(2,1)S(1)}, u32[]{:S(2)}, u32[]{:S(2)}) collective-permute-start(bf16[128,1024]{1,0:T(8,128)(2,1)S(1)} %get-tuple-element.66), channel_id=1, source_target_pairs={{0,5},{1,4},{2,7},{3,6},{4,1},{5,0},{6,3},{7,2},{8,13},{9,12},{10,... | collective-permute-start | bytes 786440 | tf_op jit(solution)/shard_map/ppermute | solution.py:30
  60.3 30.9 %collective-permute-start.7 = (bf16[128,2048]{1,0:T(8,128)(2,1)S(1)}, bf16[128,2048]{1,0:T(8,128)(2,1)S(1)}, u32[]{:S(2)}, u32[]{:S(2)}) collective-permute-start(bf16[128,2048]{1,0:T(8,128)(2,1)S(1)} %get-tuple-element.73), channel_id=1, source_target_pairs={{0,6},{1,7},{2,4},{3,5},{4,2},{5,3},{6,0},{7,1},{8,14},{9,15},{10,... | collective-permute-start | bytes 1572872 | tf_op jit(solution)/shard_map/ppermute | solution.py:30
  77.2 22.5 %collective-permute-start.8 = (bf16[128,2048]{1,0:T(8,128)(2,1)S(1)}, bf16[128,2048]{1,0:T(8,128)(2,1)S(1)}, u32[]{:S(2)}, u32[]{:S(2)}) collective-permute-start(bf16[128,2048]{1,0:T(8,128)(2,1)S(1)} %get-tuple-element.74), channel_id=1, source_target_pairs={{0,2},{1,3},{2,0},{3,1},{4,6},{5,7},{6,4},{7,5},{8,10},{9,11},{10,... | collective-permute-start | bytes 1572872 | tf_op jit(solution)/shard_map/ppermute | solution.py:30
  82.8 27.9 %collective-permute-start.4 = (bf16[128,2048]{1,0:T(8,128)(2,1)S(1)}, bf16[128,2048]{1,0:T(8,128)(2,1)S(1)}, u32[]{:S(2)}, u32[]{:S(2)}) collective-permute-start(bf16[128,2048]{1,0:T(8,128)(2,1)S(1)} %get-tuple-element.70), channel_id=1, source_target_pairs={{0,3},{1,2},{2,1},{3,0},{4,7},{5,6},{6,5},{7,4},{8,11},{9,10},{10,... | collective-permute-start | bytes 1572872 | tf_op jit(solution)/shard_map/ppermute | solution.py:30
  88.4 23.6 %collective-permute-start.24 = (bf16[128,2048]{1,0:T(8,128)(2,1)S(1)}, bf16[128,2048]{1,0:T(8,128)(2,1)S(1)}, u32[]{:S(2)}, u32[]{:S(2)}) collective-permute-start(bf16[128,2048]{1,0:T(8,128)(2,1)S(1)} %get-tuple-element.75.refs_0_), channel_id=1, source_target_pairs={{0,8},{8,0},{16,24},{24,16},{1,9},{9,1},{17,25},{25,17},{2,10},{10... | collective-permute-start | bytes 1572872 | tf_op jit(solution)/shard_map/ppermute | solution.py:30
  89.7 23.1 %collective-permute-start.26 = (bf16[128,2048]{1,0:T(8,128)(2,1)S(1)}, bf16[128,2048]{1,0:T(8,128)(2,1)S(1)}, u32[]{:S(2)}, u32[]{:S(2)}) collective-permute-start(bf16[128,2048]{1,0:T(8,128)(2,1)S(1)} %get-tuple-element.75.refs_0_), channel_id=1, source_target_pairs={{0,16},{8,24},{16,0},{24,8},{1,17},{9,25},{17,1},{25,9},{2,18},{10... | collective-permute-start | bytes 1572872 | tf_op jit(solution)/shard_map/ppermute | solution.py:30
  91.2 22.9 %collective-permute-start.15 = (bf16[128,1024]{1,0:T(8,128)(2,1)S(1)}, bf16[128,1024]{1,0:T(8,128)(2,1)S(1)}, u32[]{:S(2)}, u32[]{:S(2)}) collective-permute-start(bf16[128,1024]{1,0:T(8,128)(2,1)S(1)} %collective-permute-done.5.refs_1_), channel_id=1, source_target_pairs={{0,8},{8,0},{16,24},{24,16},{1,9},{9,1},{17,25},{25,17},{2,10},{10... | collective-permute-start | bytes 786440 | tf_op jit(solution)/shard_map/ppermute | solution.py:30
  99.7 15.1 %collective-permute-start.16 = (bf16[128,1024]{1,0:T(8,128)(2,1)S(1)}, bf16[128,1024]{1,0:T(8,128)(2,1)S(1)}, u32[]{:S(2)}, u32[]{:S(2)}) collective-permute-start(bf16[128,1024]{1,0:T(8,128)(2,1)S(1)} %collective-permute-done.6.refs_2_), channel_id=1, source_target_pairs={{0,8},{8,0},{16,24},{24,16},{1,9},{9,1},{17,25},{25,17},{2,10},{10... | collective-permute-start | bytes 786440 | tf_op jit(solution)/shard_map/ppermute | solution.py:30
  112.8 18.4 %collective-permute-start.30 = (bf16[128,1024]{1,0:T(8,128)(2,1)S(1)}, bf16[128,1024]{1,0:T(8,128)(2,1)S(1)}, u32[]{:S(2)}, u32[]{:S(2)}) collective-permute-start(bf16[128,1024]{1,0:T(8,128)(2,1)S(1)} %collective-permute-done.rows_ref.a_ref), channel_id=1, source_target_pairs={{0,16},{8,24},{16,0},{24,8},{1,17},{9,25},{17,1},{25,9},{2,18},{10... | collective-permute-start | bytes 786440 | tf_op jit(solution)/shard_map/ppermute | solution.py:30
  114.1 42.7 %collective-permute-start.28 = (bf16[128,1024]{1,0:T(8,128)(2,1)S(1)}, bf16[128,1024]{1,0:T(8,128)(2,1)S(1)}, u32[]{:S(2)}, u32[]{:S(2)}) collective-permute-start(bf16[128,1024]{1,0:T(8,128)(2,1)S(1)} %collective-permute-done.2.refs_0_), channel_id=1, source_target_pairs={{0,16},{8,24},{16,0},{24,8},{1,17},{9,25},{17,1},{25,9},{2,18},{10... | collective-permute-start | bytes 786440 | tf_op jit(solution)/shard_map/ppermute | solution.py:30
  114.8 42.1 %collective-permute-start.29 = (bf16[128,1024]{1,0:T(8,128)(2,1)S(1)}, bf16[128,1024]{1,0:T(8,128)(2,1)S(1)}, u32[]{:S(2)}, u32[]{:S(2)}) collective-permute-start(bf16[128,1024]{1,0:T(8,128)(2,1)S(1)} %collective-permute-done.3.refs_1_), channel_id=1, source_target_pairs={{0,16},{8,24},{16,0},{24,8},{1,17},{9,25},{17,1},{25,9},{2,18},{10... | collective-permute-start | bytes 786440 | tf_op jit(solution)/shard_map/ppermute | solution.py:30
  119.9 49.5 %collective-permute-start.25 = (bf16[128,2048]{1,0:T(8,128)(2,1)S(1)}, bf16[128,2048]{1,0:T(8,128)(2,1)S(1)}, u32[]{:S(2)}, u32[]{:S(2)}) collective-permute-start(bf16[128,2048]{1,0:T(8,128)(2,1)S(1)} %collective-permute-done.9.refs_1_), channel_id=1, source_target_pairs={{0,8},{8,0},{16,24},{24,16},{1,9},{9,1},{17,25},{25,17},{2,10},{10... | collective-permute-start | bytes 1572872 | tf_op jit(solution)/shard_map/ppermute | solution.py:30
  125.6 33.5 %collective-permute-start.31 = (bf16[128,1024]{1,0:T(8,128)(2,1)S(1)}, bf16[128,1024]{1,0:T(8,128)(2,1)S(1)}, u32[]{:S(2)}, u32[]{:S(2)}) collective-permute-start(bf16[128,1024]{1,0:T(8,128)(2,1)S(1)} %collective-permute-done.1.b_ref), channel_id=1, source_target_pairs={{0,16},{8,24},{16,0},{24,8},{1,17},{9,25},{17,1},{25,9},{2,18},{10... | collective-permute-start | bytes 786440 | tf_op jit(solution)/shard_map/ppermute | solution.py:30
  131.2 27.9 %collective-permute-start.12 = (bf16[128,1024]{1,0:T(8,128)(2,1)S(1)}, bf16[128,1024]{1,0:T(8,128)(2,1)S(1)}, u32[]{:S(2)}, u32[]{:S(2)}) collective-permute-start(bf16[128,1024]{1,0:T(8,128)(2,1)S(1)} %collective-permute-done.rows_ref.a_ref), channel_id=1, source_target_pairs={{0,8},{8,0},{16,24},{24,16},{1,9},{9,1},{17,25},{25,17},{2,10},{10... | collective-permute-start | bytes 786440 | tf_op jit(solution)/shard_map/ppermute | solution.py:30
  165.2 19.3 %collective-permute-start.21 = (bf16[128,2048]{1,0:T(8,128)(2,1)S(1)}, bf16[128,2048]{1,0:T(8,128)(2,1)S(1)}, u32[]{:S(2)}, u32[]{:S(2)}) collective-permute-start(bf16[128,2048]{1,0:T(8,128)(2,1)S(1)} %collective-permute-done.8.refs_1_), channel_id=1, source_target_pairs={{0,8},{8,0},{16,24},{24,16},{1,9},{9,1},{17,25},{25,17},{2,10},{10... | collective-permute-start | bytes 1572872 | tf_op jit(solution)/shard_map/ppermute | solution.py:30
  168.4 16.7 %collective-permute-start.22 = (bf16[128,2048]{1,0:T(8,128)(2,1)S(1)}, bf16[128,2048]{1,0:T(8,128)(2,1)S(1)}, u32[]{:S(2)}, u32[]{:S(2)}) collective-permute-start(bf16[128,2048]{1,0:T(8,128)(2,1)S(1)} %collective-permute-done.7.refs_0_), channel_id=1, source_target_pairs={{0,16},{8,24},{16,0},{24,8},{1,17},{9,25},{17,1},{25,9},{2,18},{10... | collective-permute-start | bytes 1572872 | tf_op jit(solution)/shard_map/ppermute | solution.py:30
  169.5 24.9 %collective-permute-start.23 = (bf16[128,2048]{1,0:T(8,128)(2,1)S(1)}, bf16[128,2048]{1,0:T(8,128)(2,1)S(1)}, u32[]{:S(2)}, u32[]{:S(2)}) collective-permute-start(bf16[128,2048]{1,0:T(8,128)(2,1)S(1)} %collective-permute-done.8.refs_1_), channel_id=1, source_target_pairs={{0,16},{8,24},{16,0},{24,8},{1,17},{9,25},{17,1},{25,9},{2,18},{10... | collective-permute-start | bytes 1572872 | tf_op jit(solution)/shard_map/ppermute | solution.py:30
  171.8 24.7 %collective-permute-start.14 = (bf16[128,2048]{1,0:T(8,128)(2,1)S(1)}, bf16[128,2048]{1,0:T(8,128)(2,1)S(1)}, u32[]{:S(2)}, u32[]{:S(2)}) collective-permute-start(bf16[128,2048]{1,0:T(8,128)(2,1)S(1)} %collective-permute-done.4.refs_0_), channel_id=1, source_target_pairs={{0,8},{8,0},{16,24},{24,16},{1,9},{9,1},{17,25},{25,17},{2,10},{10... | collective-permute-start | bytes 1572872 | tf_op jit(solution)/shard_map/ppermute | solution.py:30
  173.2 31.7 %collective-permute-start.17 = (bf16[128,2048]{1,0:T(8,128)(2,1)S(1)}, bf16[128,2048]{1,0:T(8,128)(2,1)S(1)}, u32[]{:S(2)}, u32[]{:S(2)}) collective-permute-start(bf16[128,2048]{1,0:T(8,128)(2,1)S(1)} %collective-permute-done.4.refs_0_), channel_id=1, source_target_pairs={{0,16},{8,24},{16,0},{24,8},{1,17},{9,25},{17,1},{25,9},{2,18},{10... | collective-permute-start | bytes 1572872 | tf_op jit(solution)/shard_map/ppermute | solution.py:30
  184.5 35.4 %collective-permute-start.10 = (bf16[128,1024]{1,0:T(8,128)(2,1)S(1)}, bf16[128,1024]{1,0:T(8,128)(2,1)S(1)}, u32[]{:S(2)}, u32[]{:S(2)}) collective-permute-start(bf16[128,1024]{1,0:T(8,128)(2,1)S(1)} %collective-permute-done.2.refs_0_), channel_id=1, source_target_pairs={{0,8},{8,0},{16,24},{24,16},{1,9},{9,1},{17,25},{25,17},{2,10},{10... | collective-permute-start | bytes 786440 | tf_op jit(solution)/shard_map/ppermute | solution.py:30
  185.1 34.8 %collective-permute-start.11 = (bf16[128,1024]{1,0:T(8,128)(2,1)S(1)}, bf16[128,1024]{1,0:T(8,128)(2,1)S(1)}, u32[]{:S(2)}, u32[]{:S(2)}) collective-permute-start(bf16[128,1024]{1,0:T(8,128)(2,1)S(1)} %collective-permute-done.3.refs_1_), channel_id=1, source_target_pairs={{0,8},{8,0},{16,24},{24,16},{1,9},{9,1},{17,25},{25,17},{2,10},{10... | collective-permute-start | bytes 786440 | tf_op jit(solution)/shard_map/ppermute | solution.py:30
  194.4 25.5 %collective-permute-start.13 = (bf16[128,1024]{1,0:T(8,128)(2,1)S(1)}, bf16[128,1024]{1,0:T(8,128)(2,1)S(1)}, u32[]{:S(2)}, u32[]{:S(2)}) collective-permute-start(bf16[128,1024]{1,0:T(8,128)(2,1)S(1)} %collective-permute-done.1.b_ref), channel_id=1, source_target_pairs={{0,8},{8,0},{16,24},{24,16},{1,9},{9,1},{17,25},{25,17},{2,10},{10... | collective-permute-start | bytes 786440 | tf_op jit(solution)/shard_map/ppermute | solution.py:30
  196.5 24.9 %collective-permute-start.36 = (f32[8,128]{1,0:T(8,128)S(1)}, f32[8,128]{1,0:T(8,128)S(1)}, u32[]{:S(2)}, u32[]{:S(2)}) collective-permute-start(f32[8,128]{1,0:T(8,128)S(1)} %get-tuple-element.108.an_ref), channel_id=1, source_target_pairs={{0,8},{8,0},{16,24},{24,16},{1,9},{9,1},{17,25},{25,17},{2,10},{10... | collective-permute-start | bytes 12296 | tf_op jit(solution)/shard_map/ppermute | solution.py:30
  204.9 16.4 %collective-permute-start.37 = (f32[8,128]{1,0:T(8,128)S(1)}, f32[8,128]{1,0:T(8,128)S(1)}, u32[]{:S(2)}, u32[]{:S(2)}) collective-permute-start(f32[8,128]{1,0:T(8,128)S(1)} %get-tuple-element.108.an_ref), channel_id=1, source_target_pairs={{0,16},{8,24},{16,0},{24,8},{1,17},{9,25},{17,1},{25,9},{2,18},{10... | collective-permute-start | bytes 12296 | tf_op jit(solution)/shard_map/ppermute | solution.py:30
  224.2 20.1 %collective-permute-start.40 = (f16[192,1152]{1,0:T(8,128)(2,1)S(1)}, f16[192,1152]{1,0:T(8,128)(2,1)S(1)}, u32[]{:S(2)}, u32[]{:S(2)}) collective-permute-start(f16[192,1152]{1,0:T(8,128)(2,1)S(1)} %convert_element_type.28), channel_id=1, source_target_pairs={{0,8},{8,0},{16,24},{24,16},{1,9},{9,1},{17,25},{25,17},{2,10},{10... | collective-permute-start | bytes 1327112 | tf_op jit(solution)/shard_map/ppermute | solution.py:30
  224.9 19.4 %collective-permute-start.41 = (f16[192,1152]{1,0:T(8,128)(2,1)S(1)}, f16[192,1152]{1,0:T(8,128)(2,1)S(1)}, u32[]{:S(2)}, u32[]{:S(2)}) collective-permute-start(f16[192,1152]{1,0:T(8,128)(2,1)S(1)} %convert_element_type.30), channel_id=1, source_target_pairs={{0,16},{8,24},{16,0},{24,8},{1,17},{9,25},{17,1},{25,9},{2,18},{10... | collective-permute-start | bytes 1327112 | tf_op jit(solution)/shard_map/ppermute | solution.py:30
  228.3 15.7 %collective-permute-start.38 = (f16[192,1024]{1,0:T(8,128)(2,1)S(1)}, f16[192,1024]{1,0:T(8,128)(2,1)S(1)}, u32[]{:S(2)}, u32[]{:S(2)}) collective-permute-start(f16[192,1024]{1,0:T(8,128)(2,1)S(1)} %convert_element_type.24), channel_id=1, source_target_pairs={{0,8},{8,0},{16,24},{24,16},{1,9},{9,1},{17,25},{25,17},{2,10},{10... | collective-permute-start | bytes 1179656 | tf_op jit(solution)/shard_map/ppermute | solution.py:30
  (13 other events, 120.9 us)

commit v3 on v2

--- a/solution.py
+++ b/solution.py
@@ -113,36 +113,22 @@
 
     def body(ids_ref, cents_ref, norm_ref, *refs):
         row_refs = refs[:n_in]
-        rows_out, score_out, lse_out, top_ref, mass_ref = refs[len(refs) - 5 :]
-        step = pl.program_id(0)
-
-        @pl.when(step == 0)
-        def _():
-            keep(row_refs, pieces, rows_out)
-            top_ref[...] = jnp.full(top_ref.shape, -NEVER, F32)
-            mass_ref[...] = jnp.zeros(mass_ref.shape, F32)
-
-        score = sharpness * (2.0 * product(cents_ref, rows_out) - norm_ref[...])
-
-        @pl.when(step == ids_ref[1])
-        def _():
-            score_out[...] = score
-
-        old_top = top_ref[...]
-        top = jnp.maximum(old_top, jnp.max(score, axis=0, keepdims=True))
-        mass = mass_ref[...] * jnp.exp(old_top - top) + jnp.sum(jnp.exp(score - top), axis=0, keepdims=True)
-        top_ref[...] = top
-        mass_ref[...] = mass
-        lse = top + jnp.log(mass)
+        rows_out, score_out, lse_out, score_buf = refs[len(refs) - 4 :]
+
+        keep(row_refs, pieces, rows_out)
+        score_buf[...] = sharpness * (2.0 * product(cents_ref, rows_out) - norm_ref[...])
+        score_out[...] = score_buf[pl.ds(pl.multiple_of(ids_ref[1] * part, part), part), :]
+        top = jnp.max(score_buf[...], axis=0, keepdims=True)
+        lse = top + jnp.log(jnp.sum(jnp.exp(score_buf[...] - top), axis=0, keepdims=True))
         for i in range(n_slots):
             lse_out[i] = lse[:, i * BLOCK : (i + 1) * BLOCK]
 
     grid_spec = pltpu.PrefetchScalarGridSpec(
         num_scalar_prefetch=1,
-        grid=(n_parts,),
+        grid=(1,),
         in_specs=[
-            pl.BlockSpec((part, feat), lambda i, ids: (i, 0)),
-            pl.BlockSpec((part, 1), lambda i, ids: (i, 0)),
+            pl.BlockSpec((width, feat), lambda i, ids: (0, 0)),
+            pl.BlockSpec((width, 1), lambda i, ids: (0, 0)),
         ]
         + [pl.BlockSpec(r.shape, lambda i, ids: (0, 0)) for r in rows]
         + ([] if fresh else [ANY] * 3),
@@ -151,7 +137,7 @@
             pl.BlockSpec((part, n_rows), lambda i, ids: (0, at)),
             pl.BlockSpec((n_slots, 1, BLOCK), lambda i, ids: (at, 0, 0)),
         ],
-        scratch_shapes=[pltpu.VMEM((1, n_rows), F32)] * 2,
+        scratch_shapes=[pltpu.VMEM((width, n_rows), F32)],
     )
     return pl.pallas_call(
         body,
@@ -159,7 +145,7 @@
         grid_spec=grid_spec,
         input_output_aliases={} if fresh else {3 + n_in + i: i for i in range(3)},
         name="own_scores",
-        compiler_params=pltpu.CompilerParams(vmem_limit_bytes=10 << 20),
+        compiler_params=pltpu.CompilerParams(vmem_limit_bytes=20 << 20),
     )(ids, *vmem(centroids), cent_norm, *rows, *([] if fresh else state))
 
 
@@ -188,36 +174,21 @@
 def last_scores(ids, centroids, cent_norm, rows, ahead, codes, state, n_parts, sharpness):
     width, feat = centroids.shape
     part = width // n_parts
-    wide = 2 * part
     mid = feat // 2
     n_mp = codes.shape[0]
     last = n_mp - 1
 
     def body(ids_ref, cents_ref, norm_ref, a_ref, b_ref, ahead_ref, code_ref, lse_ref, *refs):
-        rows_out, score_out, note_ref, top_ref, mass_ref = refs[len(refs) - 5 :]
-        step = pl.program_id(0)
-
-        @pl.when(step == 0)
-        def _():
-            rows_out[:, :mid] = a_ref[...]
-            rows_out[:, mid:] = b_ref[...]
-            top_ref[...] = jnp.full(top_ref.shape, -NEVER, F32)
-            mass_ref[...] = jnp.zeros(mass_ref.shape, F32)
-            for k in range(last):
-                note_ref[k : k + 1, :] = lse_ref[k]
-            note_ref[n_mp:, :] = code_ref[...]
-
-        score = sharpness * (2.0 * (ahead_ref[...] + product(cents_ref, b_ref)) - norm_ref[...])
-
-        @pl.when(step == ids_ref[1] // 2)
-        def _():
-            score_out[...] = jnp.where(ids_ref[1] % 2 == 0, score[:part], score[part:])
-
-        old_top = top_ref[...]
-        top = jnp.maximum(old_top, jnp.max(score, axis=0, keepdims=True))
-        mass = mass_ref[...] * jnp.exp(old_top - top) + jnp.sum(jnp.exp(score - top), axis=0, keepdims=True)
-        top_ref[...] = top
-        mass_ref[...] = mass
+        rows_out, score_out, note_ref, score_buf = refs[len(refs) - 4 :]
+        rows_out[:, :mid] = a_ref[...]
+        rows_out[:, mid:] = b_ref[...]
+        for k in range(last):
+            note_ref[k : k + 1, :] = lse_ref[k]
+        note_ref[n_mp:, :] = code_ref[...]
+        score_buf[...] = sharpness * (2.0 * (ahead_ref[...] + product(cents_ref, b_ref)) - norm_ref[...])
+        score_out[...] = score_buf[pl.ds(pl.multiple_of(ids_ref[1] * part, part), part), :]
+        top = jnp.max(score_buf[...], axis=0, keepdims=True)
+        mass = jnp.sum(jnp.exp(score_buf[...] - top), axis=0, keepdims=True)
         note_ref[last : last + 1, :] = top + jnp.log(mass)
 
     def whole(shape):
@@ -225,13 +196,13 @@
 
     grid_spec = pltpu.PrefetchScalarGridSpec(
         num_scalar_prefetch=1,
-        grid=(n_parts // 2,),
+        grid=(1,),
         in_specs=[
-            pl.BlockSpec((wide, mid), lambda i, ids: (i, 1)),
-            pl.BlockSpec((wide, 1), lambda i, ids: (i, 0)),
+            pl.BlockSpec((width, mid), lambda i, ids: (0, 1)),
+            pl.BlockSpec((width, 1), lambda i, ids: (0, 0)),
             whole((BLOCK, mid)),
             whole((BLOCK, mid)),
-            pl.BlockSpec((wide, BLOCK), lambda i, ids: (i, 0)),
+            pl.BlockSpec((width, BLOCK), lambda i, ids: (0, 0)),
             whole(codes.shape),
             whole(state[2].shape),
             ANY,
@@ -242,7 +213,7 @@
             pl.BlockSpec((part, BLOCK), lambda i, ids: (0, last)),
             whole((2 * n_mp, LANES)),
         ],
-        scratch_shapes=[pltpu.VMEM((1, BLOCK), F32)] * 2,
+        scratch_shapes=[pltpu.VMEM((width, BLOCK), F32)],
     )
     return pl.pallas_call(
         body,
@@ -251,67 +222,13 @@
         grid_spec=grid_spec,
         input_output_aliases={8: 0, 9: 1},
         name="last_scores",
-        compiler_params=pltpu.CompilerParams(vmem_limit_bytes=10 << 20),
+        compiler_params=pltpu.CompilerParams(vmem_limit_bytes=16 << 20),
     )(ids, *vmem(centroids), cent_norm, *rows, ahead, codes, state[2], *state[:2])
-
-
-def side_scores(ids, centroids, cent_norm, sides, pieces, state, at, n_slots, half, sharpness):
-    feat = centroids.shape[1]
-    n_rows = n_slots * BLOCK
-    fresh = isinstance(state[0], jax.ShapeDtypeStruct)
-    n_in = len(sides[0])
-
-    def body(ids_ref, cents_ref, norm_ref, *refs):
-        x_refs, y_refs = refs[:n_in], refs[n_in : 2 * n_in]
-        x_rows, y_rows, x_out, y_out = refs[len(refs) - 4 :]
-        step = pl.program_id(0)
-
-        def score(rows_ref):
-            return sharpness * (2.0 * product(cents_ref, rows_ref) - norm_ref[...])
-
-        @pl.when(step == 0)
-        def _():
-            keep(x_refs, pieces, x_rows)
-            keep(y_refs, pieces, y_rows)
-
-        @pl.when(step != 3)
-        def _():
-            x_out[...] = score(x_rows)
-
-        @pl.when(step != 2)
-        def _():
-            y_out[...] = score(y_rows)
-
-    def block(i, ids):
-        mine = ids[1]
-        other = jnp.where(i == 2, 2 * (mine ^ 2) + 1, 2 * (mine ^ 1))
-        return (jnp.where(i < 2, 2 * mine + i, other), 0)
-
-    grid_spec = pltpu.PrefetchScalarGridSpec(
-        num_scalar_prefetch=1,
-        grid=(4,),
-        in_specs=[pl.BlockSpec((half, feat), block), pl.BlockSpec((half, 1), block)]
-        + [pl.BlockSpec(r.shape, lambda i, ids: (0, 0)) for r in sides[0] + sides[1]]
-        + ([] if fresh else [ANY] * 4),
-        out_specs=[
-            pl.BlockSpec((n_rows, feat), lambda i, ids: (at, 0)),
-            pl.BlockSpec((n_rows, feat), lambda i, ids: (at, 0)),
-            pl.BlockSpec((half, n_rows), lambda i, ids: (jnp.minimum(i, 2), at)),
-            pl.BlockSpec((half, n_rows), lambda i, ids: (jnp.where(i == 3, 2, jnp.minimum(i, 1)), at)),
-        ],
-    )
-    return pl.pallas_call(
-        body,
-        out_shape=[pltpu.VMEM(v.shape, v.dtype) for v in state],
-        grid_spec=grid_spec,
-        input_output_aliases={} if fresh else {3 + 2 * n_in + i: i for i in range(4)},
-        name="side_scores",
-        compiler_params=pltpu.CompilerParams(vmem_limit_bytes=12 << 20),
-    )(ids, *vmem(centroids), cent_norm, *sides[0], *sides[1], *([] if fresh else state))
 
 
 def one_side_scores(ids, centroids, cent_norm, rows, pieces, state, at, n_slots, half, sharpness, bit):
     feat = centroids.shape[1]
+    fresh = isinstance(state[0], jax.ShapeDtypeStruct)
     n_rows = n_slots * BLOCK
     n_in = len(rows)
 
@@ -334,7 +251,7 @@
             pl.BlockSpec(cent_norm.shape, lambda i, ids: (0, 0)),
         ]
         + [pl.BlockSpec(r.shape, lambda i, ids: (0, 0)) for r in rows]
-        + [ANY] * 2,
+        + ([] if fresh else [ANY] * 2),
         out_specs=[
             pl.BlockSpec((n_rows, feat), lambda i, ids: (at, 0)),
             pl.BlockSpec((3 * half, n_rows), lambda i, ids: (0, at)),
@@ -344,10 +261,10 @@
         body,
         out_shape=[pltpu.VMEM(v.shape, v.dtype) for v in state],
         grid_spec=grid_spec,
-        input_output_aliases={3 + n_in + i: i for i in range(2)},
+        input_output_aliases={} if fresh else {3 + n_in + i: i for i in range(2)},
         name="one_side_scores",
         compiler_params=pltpu.CompilerParams(vmem_limit_bytes=20 << 20),
-    )(ids, *vmem(centroids), cent_norm, *rows, *state)
+    )(ids, *vmem(centroids), cent_norm, *rows, *([] if fresh else state))
 
 
 def log_total(kept):
@@ -593,7 +510,7 @@
     ]
     sides = [jax.ShapeDtypeStruct((n_rows, feat), BF16)] * 2
     sides += [jax.ShapeDtypeStruct((3 * half, n_rows), F32)] * 2
-    ahead = first_product(cents, got[cuts[last][0]], n_dp)
+    ahead = first_product(cents, got[cuts[last][0]], 1)
     for group in own_groups(n_mp):
         held = [p for at in group for p in cuts[seq[at]]]
         placed = [(seq.index(p[0]) - group[0], p[1], p[2]) for p in held]
@@ -605,9 +522,6 @@
         held = cuts[seq[2 * i]] + cuts[seq[2 * i + 1]]
         placed = [(seq.index(p[0]) - 2 * i, p[1], p[2]) for p in held]
         pair = [[side[bit, p] for p in held] for bit in (1, 2)]
-        if i < n_mp // 2 - 1:
-            sides = list(side_scores(ids, cents, cent_norm, pair, placed, sides, i, 2, half, sharpness))
-            continue
         for bit in (1, 2):
             sides[bit - 1 :: 2] = one_side_scores(
                 ids, cents, cent_norm, pair[bit - 1], placed, sides[bit - 1 :: 2], i, 2, half, sharpness, bit

time: 261 us -> 283 us (1.084)
  waiting for transfers between devices: 109 us -> 154 us
  starting transfers between devices: 85.6 us -> 70.3 us
  Pallas kernels: 62.1 us -> 54.8 us
    ppermute x42, waiting for transfers between devices: 103 us -> 147 us  [swap(): return lax.ppermute(value, axis, [(i, i ^ offset) for i in range(size)])]
    ppermute x42, starting transfers between devices: 81.7 us -> 67 us  [swap(): return lax.ppermute(value, axis, [(i, i ^ offset) for i in range(size)])]
    pallas_call x3 -> x0, Pallas kernels: 12 us -> none  [side_scores(): pl.pallas_call(body, out_shape=[pltpu.VMEM(v.shape, v.dtype) for v in sta...]
    pallas_call x2 -> x8, Pallas kernels: 2.94 us -> 12 us  [one_side_scores(): pl.pallas_call(body, out_shape=[pltpu.VMEM(v.shape, v.dtype) for v in sta...]
    pallas_call x4, Pallas kernels: 14.3 us -> 11.3 us  [own_scores(): pl.pallas_call(body, out_shape=[pltpu.VMEM(v.shape, v.dtype) for v in sta...]
  transfers between devices with their start and end apart: 43 -> 43, of which waited for: 20 -> 22; matrix products, arithmetic and copies ran while one was open for 0% -> 0% of each run, Pallas kernels for 20% -> 16%
where the time goes in v3:
time: 283 us
  waiting for transfers between devices  154 us (54%)
  starting transfers between devices  70.3 us (25%)
  Pallas kernels  54.8 us (19%)
    ppermute x42, waiting for transfers between devices, swap(): return lax.ppermute(value, axis, [(i, i ^ offset) for i in range(size)])  147 us
    ppermute x42, starting transfers between devices, swap(): return lax.ppermute(value, axis, [(i, i ^ offset) for i in range(size)])  67 us
    pallas_call x8, Pallas kernels, one_side_scores(): pl.pallas_call(body, out_shape=[pltpu.VMEM(v.shape, v.dtype) for v in sta...  12 us
    pallas_call x4, Pallas kernels, own_scores(): pl.pallas_call(body, out_shape=[pltpu.VMEM(v.shape, v.dtype) for v in sta...  11.3 us
    pallas_call x1, Pallas kernels, own_sums(): pl.pallas_call(body, out_shape=[pltpu.VMEM((width, feat), F32), jax.Shape...  7.93 us
    all_to_all x1, waiting for transfers between devices, on_square(): lax.all_to_all(peak, ('dp', 'mp'), split_axis=0, concat_axis=0, tiled=True)  6.37 us
    pallas_call x1, Pallas kernels, load_centroids(): pl.pallas_call(body, out_shape=[pltpu.VMEM((width, feat), centroids.dtype...  5.97 us
  transfers between devices with their start and end apart: 43, of which 22 were waited for; matrix products, arithmetic and copies ran while one was open for 0% of the time, Pallas kernels for 16%

profile of v3, /device:TPU:0, one launch (start us, length us, event | category | flops | bytes accessed | tf_op | source)
XLA Modules:
  0.0 282.8 jit_solution(3685435206774892581)
XLA Ops:
  3.7 4.0 %collective-permute-start = (bf16[128,1024]{1,0:T(8,128)(2,1)S(1)}, bf16[128,1024]{1,0:T(8,128)(2,1)S(1)}, u32[]{:S(2)}, u32[]{:S(2)}) collective-permute-start(bf16[128,1024]{1,0:T(8,128)(2,1)S(1)} %get-tuple-element.65), channel_id=1, source_target_pairs={{0,5},{1,4},{2,7},{3,6},{4,1},{5,0},{6,3},{7,2},{8,13},{9,12},{10,... | collective-permute-start | bytes 786440 | tf_op jit(solution)/shard_map/ppermute | solution.py:30
  7.8 2.8 collective-permute-start.2
  10.8 2.9 %collective-permute-start.5 = (bf16[128,1024]{1,0:T(8,128)(2,1)S(1)}, bf16[128,1024]{1,0:T(8,128)(2,1)S(1)}, u32[]{:S(2)}, u32[]{:S(2)}) collective-permute-start(bf16[128,1024]{1,0:T(8,128)(2,1)S(1)} %get-tuple-element.71), channel_id=1, source_target_pairs={{0,7},{1,6},{2,5},{3,4},{4,3},{5,2},{6,1},{7,0},{8,15},{9,14},{10,... | collective-permute-start | bytes 786440 | tf_op jit(solution)/shard_map/ppermute | solution.py:30
  15.7 26.4 %collective-permute-done.rows_ref.a_ref = bf16[128,1024]{1,0:T(8,128)(2,1)S(1)} collective-permute-done((bf16[128,1024]{1,0:T(8,128)(2,1)S(1)}, bf16[128,1024]{1,0:T(8,128)(2,1)S(1)}, u32[]{:S(2)}, u32[]{:S(2)}) %collective-permute-start) | collective-permute-done | bytes 262176 | tf_op jit(solution)/shard_map/ppermute | solution.py:30
  43.4 4.6 %collective-permute-done.1.b_ref = bf16[128,1024]{1,0:T(8,128)(2,1)S(1)} collective-permute-done((bf16[128,1024]{1,0:T(8,128)(2,1)S(1)}, bf16[128,1024]{1,0:T(8,128)(2,1)S(1)}, u32[]{:S(2)}, u32[]{:S(2)}) %collective-permute-start.1) | collective-permute-done | bytes 262176 | tf_op jit(solution)/shard_map/ppermute | solution.py:30
  47.9 4.3 %collective-permute-start.7 = (bf16[128,2048]{1,0:T(8,128)(2,1)S(1)}, bf16[128,2048]{1,0:T(8,128)(2,1)S(1)}, u32[]{:S(2)}, u32[]{:S(2)}) collective-permute-start(bf16[128,2048]{1,0:T(8,128)(2,1)S(1)} %get-tuple-element.73), channel_id=1, source_target_pairs={{0,6},{1,7},{2,4},{3,5},{4,2},{5,3},{6,0},{7,1},{8,14},{9,15},{10,... | collective-permute-start | bytes 1572872 | tf_op jit(solution)/shard_map/ppermute | solution.py:30
  52.2 2.4 collective-permute-done.2.refs_0_
  55.0 16.4 %collective-permute-done.3.refs_1_ = bf16[128,1024]{1,0:T(8,128)(2,1)S(1)} collective-permute-done((bf16[128,1024]{1,0:T(8,128)(2,1)S(1)}, bf16[128,1024]{1,0:T(8,128)(2,1)S(1)}, u32[]{:S(2)}, u32[]{:S(2)}) %collective-permute-start.3) | collective-permute-done | bytes 262176 | tf_op jit(solution)/shard_map/ppermute | solution.py:30
  71.4 3.4 %collective-permute-start.6 = (bf16[128,1024]{1,0:T(8,128)(2,1)S(1)}, bf16[128,1024]{1,0:T(8,128)(2,1)S(1)}, u32[]{:S(2)}, u32[]{:S(2)}) collective-permute-start(bf16[128,1024]{1,0:T(8,128)(2,1)S(1)} %get-tuple-element.72), channel_id=1, source_target_pairs={{0,7},{1,6},{2,5},{3,4},{4,3},{5,2},{6,1},{7,0},{8,15},{9,14},{10,... | collective-permute-start | bytes 786440 | tf_op jit(solution)/shard_map/ppermute | solution.py:30
  74.8 11.6 %collective-permute-done.6.refs_2_ = bf16[128,1024]{1,0:T(8,128)(2,1)S(1)} collective-permute-done((bf16[128,1024]{1,0:T(8,128)(2,1)S(1)}, bf16[128,1024]{1,0:T(8,128)(2,1)S(1)}, u32[]{:S(2)}, u32[]{:S(2)}) %collective-permute-start.6) | collective-permute-done | bytes 262176 | tf_op jit(solution)/shard_map/ppermute | solution.py:30
  89.9 9.0 %collective-permute-done.8.refs_1_ = bf16[128,2048]{1,0:T(8,128)(2,1)S(1)} collective-permute-done((bf16[128,2048]{1,0:T(8,128)(2,1)S(1)}, bf16[128,2048]{1,0:T(8,128)(2,1)S(1)}, u32[]{:S(2)}, u32[]{:S(2)}) %collective-permute-start.8) | collective-permute-done | bytes 524320 | tf_op jit(solution)/shard_map/ppermute | solution.py:30
  103.0 15.1 %collective-permute-done.12.refs_2_ = bf16[128,1024]{1,0:T(8,128)(2,1)S(1)} collective-permute-done((bf16[128,1024]{1,0:T(8,128)(2,1)S(1)}, bf16[128,1024]{1,0:T(8,128)(2,1)S(1)}, u32[]{:S(2)}, u32[]{:S(2)}) %collective-permute-start.12) | collective-permute-done | bytes 262176 | tf_op jit(solution)/shard_map/ppermute | solution.py:30
  119.5 4.2 %collective-permute-done.13.refs_3_ = bf16[128,1024]{1,0:T(8,128)(2,1)S(1)} collective-permute-done((bf16[128,1024]{1,0:T(8,128)(2,1)S(1)}, bf16[128,1024]{1,0:T(8,128)(2,1)S(1)}, u32[]{:S(2)}, u32[]{:S(2)}) %collective-permute-start.13) | collective-permute-done | bytes 262176 | tf_op jit(solution)/shard_map/ppermute | solution.py:30
  125.1 4.2 %collective-permute-done.15.refs_1_ = bf16[128,1024]{1,0:T(8,128)(2,1)S(1)} collective-permute-done((bf16[128,1024]{1,0:T(8,128)(2,1)S(1)}, bf16[128,1024]{1,0:T(8,128)(2,1)S(1)}, u32[]{:S(2)}, u32[]{:S(2)}) %collective-permute-start.15) | collective-permute-done | bytes 262176 | tf_op jit(solution)/shard_map/ppermute | solution.py:30
  130.7 3.6 %collective-permute-done.16.refs_2_ = bf16[128,1024]{1,0:T(8,128)(2,1)S(1)} collective-permute-done((bf16[128,1024]{1,0:T(8,128)(2,1)S(1)}, bf16[128,1024]{1,0:T(8,128)(2,1)S(1)}, u32[]{:S(2)}, u32[]{:S(2)}) %collective-permute-start.16) | collective-permute-done | bytes 262176 | tf_op jit(solution)/shard_map/ppermute | solution.py:30
  137.2 6.0 %load_centroids.1 = (bf16[1536,2048]{1,0:T(8,128)(2,1)S(1)}, f32[1536,1]{1,0:T(8,128)S(1)}) custom-call(bf16[1536,2048]{1,0:T(8,128)(2,1)} %in_ref.1), custom_call_target="tpu_custom_call" | custom-call | tf_op jit(solution)/shard_map/load_centroids/pallas_call | solution.py:85
  144.1 2.9 %own_scores.4 = (bf16[1024,2048]{1,0:T(8,128)(2,1)S(1)}, f32[384,1024]{1,0:T(8,128)S(1)}, f32[8,1,128]{2,1,0:T(1,128)S(1)}) custom-call(s32[2]{0:T(128)S(1)} %pad_add_fusion.ids_ref, bf16[1536,2048]{1,0:T(8,128)(2,1)S(1)} %get-tuple-element.63.cents_ref.old_ref, f32[1536,1]{1,0:T(8,128)S(1)} %get-tuple-element.64.norm_ref, ...), custom_call_target="tpu_custom_call" | custom-call | tf_op jit(solution)/shard_map/own_scores/pallas_call | solution.py:142
  147.0 2.9 %own_scores.5 = (bf16[1024,2048]{1,0:T(8,128)(2,1)S(1)}, f32[384,1024]{1,0:T(8,128)S(1)}, f32[8,1,128]{2,1,0:T(1,128)S(1)}) custom-call(s32[2]{0:T(128)S(1)} %pad_add_fusion.ids_ref, bf16[1536,2048]{1,0:T(8,128)(2,1)S(1)} %get-tuple-element.63.cents_ref.old_ref, ...), custom_call_target="tpu_custom_call", output_to_operand_aliasing={{0}: (5, {}), {1}: (6, {}), {2}: (7, {})} | custom-call | tf_op jit(solution)/shard_map/own_scores/pallas_call | solution.py:142
  149.9 2.9 %own_scores.6 = (bf16[1024,2048]{1,0:T(8,128)(2,1)S(1)}, f32[384,1024]{1,0:T(8,128)S(1)}, f32[8,1,128]{2,1,0:T(1,128)S(1)}) custom-call(s32[2]{0:T(128)S(1)} %pad_add_fusion.ids_ref, bf16[1536,2048]{1,0:T(8,128)(2,1)S(1)} %get-tuple-element.63.cents_ref.old_ref, ...), custom_call_target="tpu_custom_call", output_to_operand_aliasing={{0}: (6, {}), {1}: (7, {}), {2}: (8, {})} | custom-call | tf_op jit(solution)/shard_map/own_scores/pallas_call | solution.py:142
  152.8 2.6 own_scores.7
  159.4 13.3 %collective-permute-start.33 = (f32[32,128]{1,0:T(8,128)S(1)}, f32[32,128]{1,0:T(8,128)S(1)}, u32[]{:S(2)}, u32[]{:S(2)}) collective-permute-start(f32[32,128]{1,0:T(8,128)S(1)} %constant_dynamic-update-slice_fusion.refs_0_), channel_id=1, source_target_pairs={{0,2},{1,3},{2,0},{3,1},{4,6},{5,7},{6,4},{7,5},{8,10},{9,11},{10,... | collective-permute-start | bytes 49160 | tf_op jit(solution)/shard_map/ppermute | solution.py:30
  174.7 3.1 %collective-permute-start.35 = (f32[32,128]{1,0:T(8,128)S(1)}, f32[32,128]{1,0:T(8,128)S(1)}, u32[]{:S(2)}, u32[]{:S(2)}) collective-permute-start(f32[32,128]{1,0:T(8,128)S(1)} %constant_dynamic-update-slice_fusion.refs_0_), channel_id=1, source_target_pairs={{0,6},{1,7},{2,4},{3,5},{4,2},{5,3},{6,0},{7,1},{8,14},{9,15},{10,... | collective-permute-start | bytes 49160 | tf_op jit(solution)/shard_map/ppermute | solution.py:30
  184.3 9.8 %collective-permute-done.20.refs_1_ = bf16[128,2048]{1,0:T(8,128)(2,1)S(1)} collective-permute-done((bf16[128,2048]{1,0:T(8,128)(2,1)S(1)}, bf16[128,2048]{1,0:T(8,128)(2,1)S(1)}, u32[]{:S(2)}, u32[]{:S(2)}) %collective-permute-start.20) | collective-permute-done | bytes 524320 | tf_op jit(solution)/shard_map/ppermute | solution.py:30
  196.2 10.1 %collective-permute-done.28.refs_0_ = bf16[128,2048]{1,0:T(8,128)(2,1)S(1)} collective-permute-done((bf16[128,2048]{1,0:T(8,128)(2,1)S(1)}, bf16[128,2048]{1,0:T(8,128)(2,1)S(1)}, u32[]{:S(2)}, u32[]{:S(2)}) %collective-permute-start.28) | collective-permute-done | bytes 524320 | tf_op jit(solution)/shard_map/ppermute | solution.py:30
  207.5 10.0 %collective-permute-done.29.refs_1_ = bf16[128,2048]{1,0:T(8,128)(2,1)S(1)} collective-permute-done((bf16[128,2048]{1,0:T(8,128)(2,1)S(1)}, bf16[128,2048]{1,0:T(8,128)(2,1)S(1)}, u32[]{:S(2)}, u32[]{:S(2)}) %collective-permute-start.29) | collective-permute-done | bytes 524320 | tf_op jit(solution)/shard_map/ppermute | solution.py:30
  218.6 10.2 %collective-permute-done.31.refs_1_ = bf16[128,2048]{1,0:T(8,128)(2,1)S(1)} collective-permute-done((bf16[128,2048]{1,0:T(8,128)(2,1)S(1)}, bf16[128,2048]{1,0:T(8,128)(2,1)S(1)}, u32[]{:S(2)}, u32[]{:S(2)}) %collective-permute-start.31) | collective-permute-done | bytes 524320 | tf_op jit(solution)/shard_map/ppermute | solution.py:30
  240.0 3.1 %collective-permute-done.24.refs_3_ = bf16[128,1024]{1,0:T(8,128)(2,1)S(1)} collective-permute-done((bf16[128,1024]{1,0:T(8,128)(2,1)S(1)}, bf16[128,1024]{1,0:T(8,128)(2,1)S(1)}, u32[]{:S(2)}, u32[]{:S(2)}) %collective-permute-start.24) | collective-permute-done | bytes 262176 | tf_op jit(solution)/shard_map/ppermute | solution.py:30
  244.6 2.8 sent_sums.3
  254.3 7.9 %own_sums.1 = (f32[384,2048]{1,0:T(8,128)S(1)}, f32[384,1]{1,0:T(8,128)S(1)}) custom-call(bf16[1024,2048]{1,0:T(8,128)(2,1)S(1)} %get-tuple-element.89.a_ref, bf16[1024,2048]{1,0:T(8,128)(2,1)S(1)} %get-tuple-element.96.b_ref.x_ref, bf16[1024,2048]{1,0:T(8,128)(2,1)S(1)} %get-tuple-element.103.c_ref.y_ref, f32[384,1024]{1,0:T(8,128)S(1)} %get-tuple-element.104.as_ref, ...), custom_call_target="tpu_custom_call" | custom-call | tf_op jit(solution)/shard_map/own_sums/pallas_call | solution.py:376
  262.2 3.3 %collective-permute-done.38 = f16[192,1024]{1,0:T(8,128)(2,1)S(1)} collective-permute-done((f16[192,1024]{1,0:T(8,128)(2,1)S(1)}, f16[192,1024]{1,0:T(8,128)(2,1)S(1)}, u32[]{:S(2)}, u32[]{:S(2)}) %collective-permute-start.38) | collective-permute-done | bytes 393248 | tf_op jit(solution)/shard_map/ppermute | solution.py:30
  271.3 3.3 %all-to-all-start = ((f32[32,1,128]{2,1,0:T(1,128)}), f32[32,1,128]{2,1,0:T(1,128)S(1)}, u32[]{:S(2)}, u32[]{:S(2)}) async-start(f32[32,1,128]{2,1,0:T(1,128)} %bitcast.5), calls=%async_computation | async-start | bytes 32768 | tf_op jit(solution)/shard_map/all_to_all | solution.py:559
  275.3 6.4 %all-to-all-done = f32[32,1,128]{2,1,0:T(1,128)S(1)} async-done(((f32[32,1,128]{2,1,0:T(1,128)}), f32[32,1,128]{2,1,0:T(1,128)S(1)}, u32[]{:S(2)}, u32[]{:S(2)}) %all-to-all-start) | async-done | bytes 16416 | tf_op jit(solution)/shard_map/all_to_all | solution.py:559
  (97 shorter events, 66.7 us)
Async XLA Ops:
  3.7 38.5 %collective-permute-start = (bf16[128,1024]{1,0:T(8,128)(2,1)S(1)}, bf16[128,1024]{1,0:T(8,128)(2,1)S(1)}, u32[]{:S(2)}, u32[]{:S(2)}) collective-permute-start(bf16[128,1024]{1,0:T(8,128)(2,1)S(1)} %get-tuple-element.65), channel_id=1, source_target_pairs={{0,5},{1,4},{2,7},{3,6},{4,1},{5,0},{6,3},{7,2},{8,13},{9,12},{10,... | collective-permute-start | bytes 786440 | tf_op jit(solution)/shard_map/ppermute | solution.py:30
  7.8 40.1 %collective-permute-start.1 = (bf16[128,1024]{1,0:T(8,128)(2,1)S(1)}, bf16[128,1024]{1,0:T(8,128)(2,1)S(1)}, u32[]{:S(2)}, u32[]{:S(2)}) collective-permute-start(bf16[128,1024]{1,0:T(8,128)(2,1)S(1)} %get-tuple-element.66), channel_id=1, source_target_pairs={{0,5},{1,4},{2,7},{3,6},{4,1},{5,0},{6,3},{7,2},{8,13},{9,12},{10,... | collective-permute-start | bytes 786440 | tf_op jit(solution)/shard_map/ppermute | solution.py:30
  7.8 46.7 %collective-permute-start.2 = (bf16[128,1024]{1,0:T(8,128)(2,1)S(1)}, bf16[128,1024]{1,0:T(8,128)(2,1)S(1)}, u32[]{:S(2)}, u32[]{:S(2)}) collective-permute-start(bf16[128,1024]{1,0:T(8,128)(2,1)S(1)} %get-tuple-element.68), channel_id=1, source_target_pairs={{0,4},{1,5},{2,6},{3,7},{4,0},{5,1},{6,2},{7,3},{8,12},{9,13},{10,... | collective-permute-start | bytes 786440 | tf_op jit(solution)/shard_map/ppermute | solution.py:30
  10.6 60.7 %collective-permute-start.3 = (bf16[128,1024]{1,0:T(8,128)(2,1)S(1)}, bf16[128,1024]{1,0:T(8,128)(2,1)S(1)}, u32[]{:S(2)}, u32[]{:S(2)}) collective-permute-start(bf16[128,1024]{1,0:T(8,128)(2,1)S(1)} %get-tuple-element.69), channel_id=1, source_target_pairs={{0,4},{1,5},{2,6},{3,7},{4,0},{5,1},{6,2},{7,3},{8,12},{9,13},{10,... | collective-permute-start | bytes 786440 | tf_op jit(solution)/shard_map/ppermute | solution.py:30
  10.8 60.6 %collective-permute-start.5 = (bf16[128,1024]{1,0:T(8,128)(2,1)S(1)}, bf16[128,1024]{1,0:T(8,128)(2,1)S(1)}, u32[]{:S(2)}, u32[]{:S(2)}) collective-permute-start(bf16[128,1024]{1,0:T(8,128)(2,1)S(1)} %get-tuple-element.71), channel_id=1, source_target_pairs={{0,7},{1,6},{2,5},{3,4},{4,3},{5,2},{6,1},{7,0},{8,15},{9,14},{10,... | collective-permute-start | bytes 786440 | tf_op jit(solution)/shard_map/ppermute | solution.py:30
  42.2 45.7 %collective-permute-start.4 = (bf16[128,2048]{1,0:T(8,128)(2,1)S(1)}, bf16[128,2048]{1,0:T(8,128)(2,1)S(1)}, u32[]{:S(2)}, u32[]{:S(2)}) collective-permute-start(bf16[128,2048]{1,0:T(8,128)(2,1)S(1)} %get-tuple-element.70), channel_id=1, source_target_pairs={{0,3},{1,2},{2,1},{3,0},{4,7},{5,6},{6,5},{7,4},{8,11},{9,10},{10,... | collective-permute-start | bytes 1572872 | tf_op jit(solution)/shard_map/ppermute | solution.py:30
  47.9 41.3 %collective-permute-start.7 = (bf16[128,2048]{1,0:T(8,128)(2,1)S(1)}, bf16[128,2048]{1,0:T(8,128)(2,1)S(1)}, u32[]{:S(2)}, u32[]{:S(2)}) collective-permute-start(bf16[128,2048]{1,0:T(8,128)(2,1)S(1)} %get-tuple-element.73), channel_id=1, source_target_pairs={{0,6},{1,7},{2,4},{3,5},{4,2},{5,3},{6,0},{7,1},{8,14},{9,15},{10,... | collective-permute-start | bytes 1572872 | tf_op jit(solution)/shard_map/ppermute | solution.py:30
  54.6 44.3 %collective-permute-start.8 = (bf16[128,2048]{1,0:T(8,128)(2,1)S(1)}, bf16[128,2048]{1,0:T(8,128)(2,1)S(1)}, u32[]{:S(2)}, u32[]{:S(2)}) collective-permute-start(bf16[128,2048]{1,0:T(8,128)(2,1)S(1)} %get-tuple-element.74), channel_id=1, source_target_pairs={{0,2},{1,3},{2,0},{3,1},{4,6},{5,7},{6,4},{7,5},{8,10},{9,11},{10,... | collective-permute-start | bytes 1572872 | tf_op jit(solution)/shard_map/ppermute | solution.py:30
  71.4 29.2 %collective-permute-start.9 = (bf16[128,2048]{1,0:T(8,128)(2,1)S(1)}, bf16[128,2048]{1,0:T(8,128)(2,1)S(1)}, u32[]{:S(2)}, u32[]{:S(2)}) collective-permute-start(bf16[128,2048]{1,0:T(8,128)(2,1)S(1)} %get-tuple-element.76), channel_id=1, source_target_pairs={{0,1},{1,0},{2,3},{3,2},{4,5},{5,4},{6,7},{7,6},{8,9},{9,8},{10,11... | collective-permute-start | bytes 1572872 | tf_op jit(solution)/shard_map/ppermute | solution.py:30
  89.2 46.6 %collective-permute-start.19 = (bf16[128,2048]{1,0:T(8,128)(2,1)S(1)}, bf16[128,2048]{1,0:T(8,128)(2,1)S(1)}, u32[]{:S(2)}, u32[]{:S(2)}) collective-permute-start(bf16[128,2048]{1,0:T(8,128)(2,1)S(1)} %get-tuple-element.75.refs_0_), channel_id=1, source_target_pairs={{0,8},{8,0},{16,24},{24,16},{1,9},{9,1},{17,25},{25,17},{2,10},{10... | collective-permute-start | bytes 1572872 | tf_op jit(solution)/shard_map/ppermute | solution.py:30
  98.9 19.2 %collective-permute-start.12 = (bf16[128,1024]{1,0:T(8,128)(2,1)S(1)}, bf16[128,1024]{1,0:T(8,128)(2,1)S(1)}, u32[]{:S(2)}, u32[]{:S(2)}) collective-permute-start(bf16[128,1024]{1,0:T(8,128)(2,1)S(1)} %collective-permute-done.rows_ref.a_ref), channel_id=1, source_target_pairs={{0,8},{8,0},{16,24},{24,16},{1,9},{9,1},{17,25},{25,17},{2,10},{10... | collective-permute-start | bytes 786440 | tf_op jit(solution)/shard_map/ppermute | solution.py:30
  100.6 23.1 %collective-permute-start.13 = (bf16[128,1024]{1,0:T(8,128)(2,1)S(1)}, bf16[128,1024]{1,0:T(8,128)(2,1)S(1)}, u32[]{:S(2)}, u32[]{:S(2)}) collective-permute-start(bf16[128,1024]{1,0:T(8,128)(2,1)S(1)} %collective-permute-done.1.b_ref), channel_id=1, source_target_pairs={{0,8},{8,0},{16,24},{24,16},{1,9},{9,1},{17,25},{25,17},{2,10},{10... | collective-permute-start | bytes 786440 | tf_op jit(solution)/shard_map/ppermute | solution.py:30
  100.9 28.4 %collective-permute-start.15 = (bf16[128,1024]{1,0:T(8,128)(2,1)S(1)}, bf16[128,1024]{1,0:T(8,128)(2,1)S(1)}, u32[]{:S(2)}, u32[]{:S(2)}) collective-permute-start(bf16[128,1024]{1,0:T(8,128)(2,1)S(1)} %collective-permute-done.5.refs_1_), channel_id=1, source_target_pairs={{0,8},{8,0},{16,24},{24,16},{1,9},{9,1},{17,25},{25,17},{2,10},{10... | collective-permute-start | bytes 786440 | tf_op jit(solution)/shard_map/ppermute | solution.py:30
  102.6 31.7 %collective-permute-start.16 = (bf16[128,1024]{1,0:T(8,128)(2,1)S(1)}, bf16[128,1024]{1,0:T(8,128)(2,1)S(1)}, u32[]{:S(2)}, u32[]{:S(2)}) collective-permute-start(bf16[128,1024]{1,0:T(8,128)(2,1)S(1)} %collective-permute-done.6.refs_2_), channel_id=1, source_target_pairs={{0,8},{8,0},{16,24},{24,16},{1,9},{9,1},{17,25},{25,17},{2,10},{10... | collective-permute-start | bytes 786440 | tf_op jit(solution)/shard_map/ppermute | solution.py:30
  118.1 54.7 %collective-permute-start.30 = (bf16[128,2048]{1,0:T(8,128)(2,1)S(1)}, bf16[128,2048]{1,0:T(8,128)(2,1)S(1)}, u32[]{:S(2)}, u32[]{:S(2)}) collective-permute-start(bf16[128,2048]{1,0:T(8,128)(2,1)S(1)} %get-tuple-element.75.refs_0_), channel_id=1, source_target_pairs={{0,16},{8,24},{16,0},{24,8},{1,17},{9,25},{17,1},{25,9},{2,18},{10... | collective-permute-start | bytes 1572872 | tf_op jit(solution)/shard_map/ppermute | solution.py:30
  123.7 33.6 %collective-permute-start.21 = (bf16[128,1024]{1,0:T(8,128)(2,1)S(1)}, bf16[128,1024]{1,0:T(8,128)(2,1)S(1)}, u32[]{:S(2)}, u32[]{:S(2)}) collective-permute-start(bf16[128,1024]{1,0:T(8,128)(2,1)S(1)} %collective-permute-done.2.refs_0_), channel_id=1, source_target_pairs={{0,16},{8,24},{16,0},{24,8},{1,17},{9,25},{17,1},{25,9},{2,18},{10... | collective-permute-start | bytes 786440 | tf_op jit(solution)/shard_map/ppermute | solution.py:30
  129.3 28.0 %collective-permute-start.26 = (bf16[128,1024]{1,0:T(8,128)(2,1)S(1)}, bf16[128,1024]{1,0:T(8,128)(2,1)S(1)}, u32[]{:S(2)}, u32[]{:S(2)}) collective-permute-start(bf16[128,1024]{1,0:T(8,128)(2,1)S(1)} %collective-permute-done.5.refs_1_), channel_id=1, source_target_pairs={{0,16},{8,24},{16,0},{24,8},{1,17},{9,25},{17,1},{25,9},{2,18},{10... | collective-permute-start | bytes 786440 | tf_op jit(solution)/shard_map/ppermute | solution.py:30
  134.3 46.6 %collective-permute-start.14 = (bf16[128,2048]{1,0:T(8,128)(2,1)S(1)}, bf16[128,2048]{1,0:T(8,128)(2,1)S(1)}, u32[]{:S(2)}, u32[]{:S(2)}) collective-permute-start(bf16[128,2048]{1,0:T(8,128)(2,1)S(1)} %collective-permute-done.4.refs_0_), channel_id=1, source_target_pairs={{0,8},{8,0},{16,24},{24,16},{1,9},{9,1},{17,25},{25,17},{2,10},{10... | collective-permute-start | bytes 1572872 | tf_op jit(solution)/shard_map/ppermute | solution.py:30
  135.8 23.6 %collective-permute-start.27 = (bf16[128,1024]{1,0:T(8,128)(2,1)S(1)}, bf16[128,1024]{1,0:T(8,128)(2,1)S(1)}, u32[]{:S(2)}, u32[]{:S(2)}) collective-permute-start(bf16[128,1024]{1,0:T(8,128)(2,1)S(1)} %collective-permute-done.6.refs_2_), channel_id=1, source_target_pairs={{0,16},{8,24},{16,0},{24,8},{1,17},{9,25},{17,1},{25,9},{2,18},{10... | collective-permute-start | bytes 786440 | tf_op jit(solution)/shard_map/ppermute | solution.py:30
  157.3 24.9 %collective-permute-start.17 = (bf16[128,2048]{1,0:T(8,128)(2,1)S(1)}, bf16[128,2048]{1,0:T(8,128)(2,1)S(1)}, u32[]{:S(2)}, u32[]{:S(2)}) collective-permute-start(bf16[128,2048]{1,0:T(8,128)(2,1)S(1)} %collective-permute-done.7.refs_0_), channel_id=1, source_target_pairs={{0,8},{8,0},{16,24},{24,16},{1,9},{9,1},{17,25},{25,17},{2,10},{10... | collective-permute-start | bytes 1572872 | tf_op jit(solution)/shard_map/ppermute | solution.py:30
  158.5 24.9 %collective-permute-start.18 = (bf16[128,2048]{1,0:T(8,128)(2,1)S(1)}, bf16[128,2048]{1,0:T(8,128)(2,1)S(1)}, u32[]{:S(2)}, u32[]{:S(2)}) collective-permute-start(bf16[128,2048]{1,0:T(8,128)(2,1)S(1)} %collective-permute-done.8.refs_1_), channel_id=1, source_target_pairs={{0,8},{8,0},{16,24},{24,16},{1,9},{9,1},{17,25},{25,17},{2,10},{10... | collective-permute-start | bytes 1572872 | tf_op jit(solution)/shard_map/ppermute | solution.py:30
  177.8 16.3 %collective-permute-start.20 = (bf16[128,2048]{1,0:T(8,128)(2,1)S(1)}, bf16[128,2048]{1,0:T(8,128)(2,1)S(1)}, u32[]{:S(2)}, u32[]{:S(2)}) collective-permute-start(bf16[128,2048]{1,0:T(8,128)(2,1)S(1)} %collective-permute-done.9.refs_1_), channel_id=1, source_target_pairs={{0,8},{8,0},{16,24},{24,16},{1,9},{9,1},{17,25},{25,17},{2,10},{10... | collective-permute-start | bytes 1572872 | tf_op jit(solution)/shard_map/ppermute | solution.py:30
  180.9 25.4 %collective-permute-start.28 = (bf16[128,2048]{1,0:T(8,128)(2,1)S(1)}, bf16[128,2048]{1,0:T(8,128)(2,1)S(1)}, u32[]{:S(2)}, u32[]{:S(2)}) collective-permute-start(bf16[128,2048]{1,0:T(8,128)(2,1)S(1)} %collective-permute-done.7.refs_0_), channel_id=1, source_target_pairs={{0,16},{8,24},{16,0},{24,8},{1,17},{9,25},{17,1},{25,9},{2,18},{10... | collective-permute-start | bytes 1572872 | tf_op jit(solution)/shard_map/ppermute | solution.py:30
  182.3 35.2 %collective-permute-start.29 = (bf16[128,2048]{1,0:T(8,128)(2,1)S(1)}, bf16[128,2048]{1,0:T(8,128)(2,1)S(1)}, u32[]{:S(2)}, u32[]{:S(2)}) collective-permute-start(bf16[128,2048]{1,0:T(8,128)(2,1)S(1)} %collective-permute-done.8.refs_1_), channel_id=1, source_target_pairs={{0,16},{8,24},{16,0},{24,8},{1,17},{9,25},{17,1},{25,9},{2,18},{10... | collective-permute-start | bytes 1572872 | tf_op jit(solution)/shard_map/ppermute | solution.py:30
  183.4 45.3 %collective-permute-start.31 = (bf16[128,2048]{1,0:T(8,128)(2,1)S(1)}, bf16[128,2048]{1,0:T(8,128)(2,1)S(1)}, u32[]{:S(2)}, u32[]{:S(2)}) collective-permute-start(bf16[128,2048]{1,0:T(8,128)(2,1)S(1)} %collective-permute-done.9.refs_1_), channel_id=1, source_target_pairs={{0,16},{8,24},{16,0},{24,8},{1,17},{9,25},{17,1},{25,9},{2,18},{10... | collective-permute-start | bytes 1572872 | tf_op jit(solution)/shard_map/ppermute | solution.py:30
  194.1 45.9 %collective-permute-start.22 = (bf16[128,1024]{1,0:T(8,128)(2,1)S(1)}, bf16[128,1024]{1,0:T(8,128)(2,1)S(1)}, u32[]{:S(2)}, u32[]{:S(2)}) collective-permute-start(bf16[128,1024]{1,0:T(8,128)(2,1)S(1)} %collective-permute-done.3.refs_1_), channel_id=1, source_target_pairs={{0,16},{8,24},{16,0},{24,8},{1,17},{9,25},{17,1},{25,9},{2,18},{10... | collective-permute-start | bytes 786440 | tf_op jit(solution)/shard_map/ppermute | solution.py:30
  195.0 45.0 %collective-permute-start.23 = (bf16[128,1024]{1,0:T(8,128)(2,1)S(1)}, bf16[128,1024]{1,0:T(8,128)(2,1)S(1)}, u32[]{:S(2)}, u32[]{:S(2)}) collective-permute-start(bf16[128,1024]{1,0:T(8,128)(2,1)S(1)} %collective-permute-done.rows_ref.a_ref), channel_id=1, source_target_pairs={{0,16},{8,24},{16,0},{24,8},{1,17},{9,25},{17,1},{25,9},{2,18},{10... | collective-permute-start | bytes 786440 | tf_op jit(solution)/shard_map/ppermute | solution.py:30
  206.3 36.8 %collective-permute-start.24 = (bf16[128,1024]{1,0:T(8,128)(2,1)S(1)}, bf16[128,1024]{1,0:T(8,128)(2,1)S(1)}, u32[]{:S(2)}, u32[]{:S(2)}) collective-permute-start(bf16[128,1024]{1,0:T(8,128)(2,1)S(1)} %collective-permute-done.1.b_ref), channel_id=1, source_target_pairs={{0,16},{8,24},{16,0},{24,8},{1,17},{9,25},{17,1},{25,9},{2,18},{10... | collective-permute-start | bytes 786440 | tf_op jit(solution)/shard_map/ppermute | solution.py:30
  217.5 27.1 %collective-permute-start.36 = (f32[8,128]{1,0:T(8,128)S(1)}, f32[8,128]{1,0:T(8,128)S(1)}, u32[]{:S(2)}, u32[]{:S(2)}) collective-permute-start(f32[8,128]{1,0:T(8,128)S(1)} %get-tuple-element.108.an_ref), channel_id=1, source_target_pairs={{0,8},{8,0},{16,24},{24,16},{1,9},{9,1},{17,25},{25,17},{2,10},{10... | collective-permute-start | bytes 12296 | tf_op jit(solution)/shard_map/ppermute | solution.py:30
  228.8 15.8 %collective-permute-start.37 = (f32[8,128]{1,0:T(8,128)S(1)}, f32[8,128]{1,0:T(8,128)S(1)}, u32[]{:S(2)}, u32[]{:S(2)}) collective-permute-start(f32[8,128]{1,0:T(8,128)S(1)} %get-tuple-element.108.an_ref), channel_id=1, source_target_pairs={{0,16},{8,24},{16,0},{24,8},{1,17},{9,25},{17,1},{25,9},{2,18},{10... | collective-permute-start | bytes 12296 | tf_op jit(solution)/shard_map/ppermute | solution.py:30
  247.4 19.1 %collective-permute-start.40 = (f16[192,1152]{1,0:T(8,128)(2,1)S(1)}, f16[192,1152]{1,0:T(8,128)(2,1)S(1)}, u32[]{:S(2)}, u32[]{:S(2)}) collective-permute-start(f16[192,1152]{1,0:T(8,128)(2,1)S(1)} %convert_element_type.28), channel_id=1, source_target_pairs={{0,8},{8,0},{16,24},{24,16},{1,9},{9,1},{17,25},{25,17},{2,10},{10... | collective-permute-start | bytes 1327112 | tf_op jit(solution)/shard_map/ppermute | solution.py:30
  248.6 18.0 %collective-permute-start.41 = (f16[192,1152]{1,0:T(8,128)(2,1)S(1)}, f16[192,1152]{1,0:T(8,128)(2,1)S(1)}, u32[]{:S(2)}, u32[]{:S(2)}) collective-permute-start(f16[192,1152]{1,0:T(8,128)(2,1)S(1)} %convert_element_type.30), channel_id=1, source_target_pairs={{0,16},{8,24},{16,0},{24,8},{1,17},{9,25},{17,1},{25,9},{2,18},{10... | collective-permute-start | bytes 1327112 | tf_op jit(solution)/shard_map/ppermute | solution.py:30
  (13 other events, 137.8 us)
